TPU v7x, 16 devices: a whole 2x2x2 slice. The times are simulated.
16 devices in a mesh: fsdp: 16 (over z, y, x, core).
Axes of the slice: x: 2, y: 2, z: 2, core: 2. Of those that a mesh axis runs over, the one named last changes fastest.
Arguments:
- hidden: bfloat16 [5, 16384, 576], P(None, 'fsdp')
- w_gate: bfloat16 [5, 576, 1536], P(None, 'fsdp')
- w_up: bfloat16 [5, 576, 1536], P(None, 'fsdp')
- w_down: bfloat16 [5, 1536, 576], P(None, 'fsdp')
- w_out: bfloat16 [576, 49152], P('fsdp')
- targets: int32 [16384], P('fsdp')
- loss_mask: int32 [16384], P('fsdp')
Outputs:
- output 1: float32 [5, 576, 1536], P(None, 'fsdp')
- output 2: float32 [5, 576, 1536], P(None, 'fsdp')
- output 3: float32 [5, 1536, 576], P(None, 'fsdp')
- output 4: float32 [576, 49152], P('fsdp')
- output 5: bfloat16 [16384, 576], P('fsdp')
- output 6: float32 [], replicated
All inputs are finite; a program needn't handle non-finite values.
Results may differ from a plain program's by a relative error of at most 0.0137025.
Values are sent between devices in bfloat16 or wider.
A program may use at most 1 GiB of HBM per device.

v0:
```python
import jax
import jax.numpy as jnp
from jax import lax
from jax.sharding import PartitionSpec as P

NORM_EPS = 1e-5
AXIS_NAME = 'fsdp'


def contract_rows(left, right):
    return lax.dot_general(left, right, (((0,), (0,)), ((), ())), preferred_element_type=jnp.float32)


def contract_cols(left, right):
    return lax.dot_general(left, right, (((1,), (1,)), ((), ())), preferred_element_type=jnp.float32)


def norm_apply(x_in):
    x_f32 = x_in.astype(jnp.float32)
    inv_rms = lax.rsqrt(jnp.mean(x_f32 * x_f32, axis=-1, keepdims=True) + NORM_EPS)
    return (x_f32 * inv_rms).astype(jnp.bfloat16)


def norm_grad(x_in, grad_y):
    x_f32 = x_in.astype(jnp.float32)
    inv_rms = lax.rsqrt(jnp.mean(x_f32 * x_f32, axis=-1, keepdims=True) + NORM_EPS)
    x_dot_grad = jnp.mean(x_f32 * grad_y, axis=-1, keepdims=True)
    return inv_rms * grad_y - x_f32 * (inv_rms * inv_rms * inv_rms) * x_dot_grad


def block_forward(h_in, gate_w, up_w):
    normed = norm_apply(h_in)
    gate_pre = jnp.dot(normed, gate_w, preferred_element_type=jnp.float32)
    up_pre = jnp.dot(normed, up_w, preferred_element_type=jnp.float32)
    gate_sig = jax.nn.sigmoid(gate_pre)
    gated_act = (gate_pre * gate_sig * up_pre).astype(jnp.bfloat16)
    return normed, gate_pre, up_pre, gate_sig, gated_act


def block_backward(h_in, grad_in, gate_w, up_w, down_w, saved_fwd):
    normed, gate_pre, up_pre, gate_sig, gated_act = saved_fwd
    grad_bf16 = grad_in.astype(jnp.bfloat16)
    grad_act = contract_cols(grad_bf16, down_w)
    grad_gate_pre = (grad_act * up_pre * gate_sig * (1.0 + gate_pre * (1.0 - gate_sig))).astype(jnp.bfloat16)
    grad_up_pre = (grad_act * gate_pre * gate_sig).astype(jnp.bfloat16)
    grad_down_w = contract_rows(gated_act, grad_bf16)
    grad_gate_w = contract_rows(normed, grad_gate_pre)
    grad_up_w = contract_rows(normed, grad_up_pre)
    grad_norm = contract_cols(grad_gate_pre, gate_w) + contract_cols(grad_up_pre, up_w)
    return grad_in + norm_grad(h_in, grad_norm), grad_gate_w, grad_up_w, grad_down_w


def head_grads(h_top, out_w, tgt_ids, mask_ids, mask_count):
    normed_top = norm_apply(h_top)
    logits = jnp.dot(normed_top, out_w, preferred_element_type=jnp.float32)
    shifted = logits - jnp.max(logits, axis=-1, keepdims=True)
    exp_shift = jnp.exp(shifted)
    exp_sum = jnp.sum(exp_shift, axis=-1, keepdims=True)
    is_target = lax.broadcasted_iota(jnp.int32, (1, logits.shape[1]), 1) == tgt_ids[:, None]
    tok_loss = jnp.log(exp_sum[:, 0]) - jnp.sum(jnp.where(is_target, shifted, 0.0), axis=-1)
    weight = mask_ids.astype(jnp.float32) / mask_count
    loss_part = jnp.sum(weight * tok_loss)
    grad_logits = (weight[:, None] * (exp_shift / exp_sum - is_target.astype(jnp.float32))).astype(jnp.bfloat16)
    grad_wout = contract_rows(normed_top, grad_logits)
    grad_top = norm_grad(h_top, contract_cols(grad_logits, out_w))
    return loss_part, grad_wout, grad_top


def gather_rows(local_piece):
    return lax.all_gather(local_piece, AXIS_NAME, axis=0, tiled=True)


def scatter_rows(full_array):
    return lax.psum_scatter(full_array, AXIS_NAME, scatter_dimension=0, tiled=True)


def solution(mesh):
    def device_step(hidden, w_gate, w_up, w_down, w_out, targets, loss_mask):
        layers = hidden.shape[0]
        top_layer = layers - 1
        mask_count = lax.psum(jnp.sum(loss_mask).astype(jnp.float32), AXIS_NAME)
        gate_full = gather_rows(w_gate[top_layer])
        up_full = gather_rows(w_up[top_layer])
        down_full = gather_rows(w_down[top_layer])
        saved_fwd = block_forward(hidden[top_layer], gate_full, up_full)
        h_top = (hidden[top_layer].astype(jnp.float32) + jnp.dot(saved_fwd[4], down_full, preferred_element_type=jnp.float32)).astype(jnp.bfloat16)
        out_full = gather_rows(w_out)
        loss_part, grad_wout, grad_run = head_grads(h_top, out_full, targets, loss_mask, mask_count)
        mean_loss = lax.psum(loss_part, AXIS_NAME)
        grad_out = scatter_rows(grad_wout)
        gate_grads, up_grads, down_grads = [], [], []
        for layer_idx in range(top_layer, -1, -1):
            if layer_idx != top_layer:
                gate_full = gather_rows(w_gate[layer_idx])
                up_full = gather_rows(w_up[layer_idx])
                down_full = gather_rows(w_down[layer_idx])
                saved_fwd = block_forward(hidden[layer_idx], gate_full, up_full)
            grad_run, grad_gate_w, grad_up_w, grad_down_w = block_backward(hidden[layer_idx], grad_run, gate_full, up_full, down_full, saved_fwd)
            gate_grads.insert(0, scatter_rows(grad_gate_w))
            up_grads.insert(0, scatter_rows(grad_up_w))
            down_grads.insert(0, scatter_rows(grad_down_w))
        return (jnp.stack(gate_grads), jnp.stack(up_grads), jnp.stack(down_grads), grad_out, grad_run.astype(jnp.bfloat16), mean_loss)

    stacked_spec = P(None, AXIS_NAME, None)
    row_spec = P(AXIS_NAME, None)
    return jax.shard_map(device_step, mesh=mesh, in_specs=(stacked_spec, stacked_spec, stacked_spec, stacked_spec, row_spec, P(AXIS_NAME), P(AXIS_NAME)), out_specs=(stacked_spec, stacked_spec, stacked_spec, row_spec, row_spec, P()), check_vma=False)
```

profile of v0, /device:TPU:0, one launch (start us, length us, event | category | flops | bytes accessed | tf_op | source)
XLA Modules:
  0.0 3915.7 jit_solution(495620546501964954)
XLA Ops:
  26.6 35.1 psum.14
  61.7 7.7 fusion.102
  69.4 13.3 all-gather.35.cloned.1.call-done
  82.7 10.4 multiply_convert_fusion.15
  93.1 19.7 all-gather.37.cloned.1.call-done
  118.5 223.8 %all-gather.63.cloned.1.call-done = bf16[16,36,49152]{2,1,0:T(8,128)(2,1)} async-done(((bf16[1,36,49152]{2,1,0:T(8,128)(2,1)}), bf16[16,36,49152]{2,1,0:T(8,128)(2,1)}) %all-gather.63.cloned.1.call-update) | async-done | bytes 56623120 | tf_op jit(solution)/shard_map/all_gather | solution.py:70
  342.3 62.2 %reshape.155 = bf16[576,49152]{1,0:T(8,128)(2,1)} reshape(bf16[16,36,49152]{2,1,0:T(8,128)(2,1)} %all-gather.63.cloned.1.call-done) | data formatting | bytes 113246208
  404.4 96.1 %fusion.206 = (f32[1024]{0:T(1024)S(1)}, f32[1024,49152]{1,0:T(8,128)}) fusion(bf16[576,49152]{1,0:T(8,128)(2,1)} %reshape.155, bf16[1024,576]{0,1:T(8,128)(2,1)S(1)} %fusion.125.clone.4), kind=kOutput, calls=%fused_computation.245 | convolution fusion | flops 58032390144 | bytes 259133440 | tf_op jit(solution)/shard_map/dot_general | solution.py:55
  500.6 70.9 %select_reduce_fusion = (f32[1024]{0:T(1024)S(1)}, f32[1024]{0:T(1024)S(1)}) fusion(f32[1024,49152]{1,0:T(8,128)} %get-tuple-element.78, s32[1024]{0:T(1024)S(1)} %copy-done.44, f32[1024]{0:T(1024)S(1)} %get-tuple-element.77), kind=kLoop, calls=%fused_computation | loop fusion | flops 251656192 | bytes 201342976 | tf_op jit(solution)/shard_map/reduce_sum | solution.py:60
  572.8 96.3 %multiply_convert_fusion = bf16[1024,49152]{1,0:T(8,128)(2,1)} fusion(f32[1024,49152]{1,0:T(8,128)} %get-tuple-element.78, s32[1024]{0:T(1024)S(1)} %copy-done.44, f32[1024]{0:T(1024)S(1)} %get-tuple-element.7, f32[1024]{0:T(1024)S(1)} %get-tuple-element.77, f32[1024]{0:T(1024)S(1)} %get-tuple-element.35), kind=kLoop, calls=%fused_computation.1 | loop fusion | flops 352321536 | bytes 302006272 | tf_op jit(solution)/shard_map/convert_element_type | solution.py:63
  669.1 67.0 %fusion.19 = (f32[1024]{0:T(1024)S(1)}, f32[1024,576]{0,1:T(8,128)S(1)}) fusion(bf16[1024,576]{0,1:T(8,128)(2,1)S(1)} %copy-done.1, bf16[1024,49152]{1,0:T(8,128)(2,1)} %multiply_convert_fusion, bf16[576,49152]{1,0:T(8,128)(2,1)} %reshape.155), kind=kOutput, calls=%fused_computation.57 | convolution fusion | flops 57983827968 | bytes 160829440 | tf_op jit(solution)/shard_map/dot_general | solution.py:15
  737.6 7.8 multiply_convert_fusion.14
  756.0 8.5 fusion.90
  772.1 8.3 multiply_convert_fusion.11
  792.1 7.6 fusion.82
  799.7 7.9 fusion.86
  807.6 8.7 multiply_convert_fusion.9
  827.9 7.6 fusion.78
  835.5 7.9 fusion.74
  843.4 8.3 multiply_convert_fusion.7
  862.6 8.5 fusion.70
  885.2 85.3 %fusion.122 = f32[576,49152]{1,0:T(8,128)} fusion(bf16[1024,49152]{1,0:T(8,128)(2,1)} %multiply_convert_fusion, bf16[1024,576]{0,1:T(8,128)(2,1)S(1)} %copy-done.1, f32[1024]{0:T(1024)S(1)} %copy-done.40), kind=kOutput, calls=%fused_computation.148 | convolution fusion | flops 57983827968 | bytes 215093248 | tf_op jit(solution)/shard_map/dot_general | solution.py:11
  970.5 10.1 fusion.12
  980.7 1561.6 %fusion.10 = f32[48,49152]{1,0:T(8,128)} fusion(f32[576,49152]{1,0:T(8,128)} %fusion.122), kind=kCustom, calls=%all-reduce-scatter.10 | all-reduce-scatter fusion | flops 37748736 | bytes 122683392
  2562.1 10.1 fusion.13
  2612.4 8.0 multiply_convert_fusion.5
  2631.4 727.9 %fusion.202 = (f32[40,1536]{1,0:T(8,128)S(1)}, f32[40,1536]{1,0:T(8,128)S(1)}, f32[40,1536]{1,0:T(8,128)S(1)}, f32[40,1536]{1,0:T(8,128)S(1)}, f32[40,1536]{1,0:...) fusion(f32[576,1536]{1,0:T(8,128)} %fusion.180, ...), kind=kCustom, calls=%all-reduce-scatter.11 | all-reduce-scatter fusion | flops 9830401 | bytes 37847040
  3360.2 15.9 collective-permute-start.19
  3377.1 7.7 collective-permute-start.17
  3435.9 10.5 collective-permute-start.23
  3507.6 167.0 %psum.15 = f32[]{:T(128)} all-reduce(f32[]{:T(128)} %get-tuple-element.34), channel_id=1, replica_groups=mesh['fsdp'=16] {'fsdp'}, use_global_device_ids=true, to_apply=%region_34.35 | all-reduce | flops 1 | bytes 8 | tf_op jit(solution)/shard_map/psum | solution.py:89
  3735.0 166.1 %concatenate.10 = f32[228,49152]{1,0:T(8,128)} concatenate(f32[36,49152]{1,0:T(8,128)} %collective-permute-done.23, f32[48,49152]{1,0:T(8,128)} %collective-permute-done.22, f32[48,49152]{1,0:T(8,128)} %collective-permute-done.21, f32[48,49152]{1,0:T(8,128)} %collective-permute-done.20, f32[48,49152]{1,0:T(8,128)} %fusion.10), dimensions={0} | concatenate | bytes 89653248
  (410 shorter events, 345.3 us)
Async XLA Ops:
  7.2 54.5 %all-gather.33.cloned.1.call-start = ((), (), s32[]{:S(2)}) async-start(), calls=%async_computation.10 | async-start | bytes 3760128 | tf_op jit(solution)/shard_map/all_gather | solution.py:70
  9.3 73.4 %all-gather.35.cloned.1.call-start = ((), (), s32[]{:S(2)}) async-start(), calls=%async_computation.11 | async-start | bytes 3760128 | tf_op jit(solution)/shard_map/all_gather | solution.py:70
  11.5 101.4 %all-gather.37.cloned.1.call-start = ((), (), s32[]{:S(2)}) async-start(), calls=%async_computation.12 | async-start | bytes 2088960 | tf_op jit(solution)/shard_map/all_gather | solution.py:70
  12.4 329.9 %all-gather.63.cloned.1.call-start = ((), (), s32[]{:S(2)}) async-start(), calls=%async_computation.25 | async-start | bytes 66846720 | tf_op jit(solution)/shard_map/all_gather | solution.py:70
  13.0 743.0 %all-gather.43.cloned.1.call-start = ((), (), s32[]{:S(2)}) async-start(), calls=%async_computation.15 | async-start | bytes 3760128 | tf_op jit(solution)/shard_map/all_gather | solution.py:70
  13.9 750.6 %all-gather.41.cloned.1.call-start = ((), (), s32[]{:S(2)}) async-start(), calls=%async_computation.14 | async-start | bytes 3760128 | tf_op jit(solution)/shard_map/all_gather | solution.py:70
  14.8 757.2 %all-gather.39.cloned.1.call-start = ((), (), s32[]{:S(2)}) async-start(), calls=%async_computation.13 | async-start | bytes 2088960 | tf_op jit(solution)/shard_map/all_gather | solution.py:70
  15.6 776.5 %all-gather.49.cloned.1.call-start = ((), (), s32[]{:S(2)}) async-start(), calls=%async_computation.18 | async-start | bytes 3760128 | tf_op jit(solution)/shard_map/all_gather | solution.py:70
  16.5 783.2 %all-gather.47.cloned.1.call-start = ((), (), s32[]{:S(2)}) async-start(), calls=%async_computation.17 | async-start | bytes 3760128 | tf_op jit(solution)/shard_map/all_gather | solution.py:70
  17.5 790.1 %all-gather.45.cloned.1.call-start = ((), (), s32[]{:S(2)}) async-start(), calls=%async_computation.16 | async-start | bytes 2088960 | tf_op jit(solution)/shard_map/all_gather | solution.py:70
  18.0 809.8 %all-gather.53.cloned.1.call-start = ((), (), s32[]{:S(2)}) async-start(), calls=%async_computation.20 | async-start | bytes 3760128 | tf_op jit(solution)/shard_map/all_gather | solution.py:70
  19.0 816.5 %all-gather.55.cloned.1.call-start = ((), (), s32[]{:S(2)}) async-start(), calls=%async_computation.21 | async-start | bytes 3760128 | tf_op jit(solution)/shard_map/all_gather | solution.py:70
  19.9 823.4 %all-gather.51.cloned.1.call-start = ((), (), s32[]{:S(2)}) async-start(), calls=%async_computation.19 | async-start | bytes 2088960 | tf_op jit(solution)/shard_map/all_gather | solution.py:70
  20.7 841.9 %all-gather.59.cloned.1.call-start = ((), (), s32[]{:S(2)}) async-start(), calls=%async_computation.23 | async-start | bytes 3760128 | tf_op jit(solution)/shard_map/all_gather | solution.py:70
  21.6 849.5 %all-gather.61.cloned.1.call-start = ((), (), s32[]{:S(2)}) async-start(), calls=%async_computation.24 | async-start | bytes 3760128 | tf_op jit(solution)/shard_map/all_gather | solution.py:70
  22.6 2588.3 %all-gather.57.cloned.1.call-start = ((), (), s32[]{:S(2)}) async-start(), calls=%async_computation.22 | async-start | bytes 2088960 | tf_op jit(solution)/shard_map/all_gather | solution.py:70
  23.1 3706.8 %reduce-scatter.28.cloned.1.call-start = ((), (), s32[]{:S(2)}) async-start(), calls=%async_computation.5 | async-start | bytes 4177920 | tf_op jit(solution)/shard_map/reduce_scatter | solution.py:74
  885.1 2845.8 %reduce-scatter.30.cloned.1.call-start = ((), (), s32[]{:S(2)}) async-start(), calls=%async_computation.6 | async-start | bytes 4177920 | tf_op jit(solution)/shard_map/reduce_scatter | solution.py:74
  980.6 2751.3 %reduce-scatter.32.cloned.1.call-start = ((), (), s32[]{:S(2)}) async-start(), calls=%async_computation.7 | async-start | bytes 4177920 | tf_op jit(solution)/shard_map/reduce_scatter | solution.py:74
  2542.3 1192.6 %collective-permute-start.20 = (f32[48,49152]{1,0:T(8,128)}, f32[48,49152]{1,0:T(8,128)}, u32[]{:S(2)}, u32[]{:S(2)}) collective-permute-start(f32[48,49152]{1,0:T(8,128)} %fusion.10), channel_id=1, source_target_pairs={{0,1},{1,2},{2,3},{3,4},{4,5},{5,6},{6,7},{7,8},{8,9},{9,10},{10,1... | collective-permute-start | bytes 28311560
  2547.3 1187.6 %collective-permute-start.21 = (f32[48,49152]{1,0:T(8,128)}, f32[48,49152]{1,0:T(8,128)}, u32[]{:S(2)}, u32[]{:S(2)}) collective-permute-start(f32[48,49152]{1,0:T(8,128)} %fusion.10), channel_id=1, source_target_pairs={{0,2},{1,3},{2,4},{3,5},{4,6},{5,7},{6,8},{7,9},{8,10},{9,11},{10,... | collective-permute-start | bytes 28311560
  2552.2 1182.8 %collective-permute-start.22 = (f32[48,49152]{1,0:T(8,128)}, f32[48,49152]{1,0:T(8,128)}, u32[]{:S(2)}, u32[]{:S(2)}) collective-permute-start(f32[48,49152]{1,0:T(8,128)} %fusion.10), channel_id=1, source_target_pairs={{0,3},{1,4},{2,5},{3,6},{4,7},{5,8},{6,9},{7,10},{8,11},{9,12},{10... | collective-permute-start | bytes 28311560
  2572.2 1160.7 %reduce-scatter.34.cloned.1.call-start = ((), (), s32[]{:S(2)}) async-start(), calls=%async_computation.8 | async-start | bytes 4177920 | tf_op jit(solution)/shard_map/reduce_scatter | solution.py:74
  2610.8 1123.2 %reduce-scatter.36.cloned.1.call-start = ((), (), s32[]{:S(2)}) async-start(), calls=%async_computation.9 | async-start | bytes 4177920 | tf_op jit(solution)/shard_map/reduce_scatter | solution.py:74
  3360.2 25.4 collective-permute-start.19
  3377.1 11.5 collective-permute-start.17
  3414.0 21.9 collective-permute-start.18
  3425.8 20.6 collective-permute-start.16
  3435.9 299.0 %collective-permute-start.23 = (f32[36,49152]{1,0:T(8,128)}, f32[36,49152]{1,0:T(8,128)}, u32[]{:S(2)}, u32[]{:S(2)}) collective-permute-start(f32[36,49152]{1,0:T(8,128)} %slice.96), channel_id=1, source_target_pairs={{0,4},{1,5},{2,6},{3,7},{4,8},{5,9},{6,10},{7,11},{8,12},{9,13},{1... | collective-permute-start | bytes 21233672
  3472.0 13.9 collective-permute-start.6
  3495.9 178.7 %collective-permute-start.2 = (f32[40,1536]{1,0:T(8,128)S(1)}, f32[40,1536]{1,0:T(8,128)}, u32[]{:S(2)}, u32[]{:S(2)}) collective-permute-start(f32[40,1536]{1,0:T(8,128)S(1)} %get-tuple-element.25), channel_id=1, source_target_pairs={{0,1},{1,2},{2,3},{3,4},{4,5},{5,6},{6,7},{7,8},{8,9},{9,10},{10,1... | collective-permute-start | bytes 737288
  3674.6 40.5 %collective-permute-start = (f32[40,1536]{1,0:T(8,128)S(1)}, f32[40,1536]{1,0:T(8,128)}, u32[]{:S(2)}, u32[]{:S(2)}) collective-permute-start(f32[40,1536]{1,0:T(8,128)S(1)} %get-tuple-element.24), channel_id=1, source_target_pairs={{0,1},{1,2},{2,3},{3,4},{4,5},{5,6},{6,7},{7,8},{8,9},{9,10},{10,1... | collective-permute-start | bytes 737288
  (115 other events, 5120.0 us)
Sparse Core Ops, SparseCore 0:
  10.8 35.8 all-gather.32
  49.5 33.2 all-gather.34
  84.9 27.8 all-gather.36
  114.9 227.2 all-gather.62
  344.3 32.7 all-gather.42
  379.2 32.7 all-gather.40
  414.3 27.8 all-gather.38
  444.4 32.7 all-gather.48
  479.5 32.7 all-gather.46
  514.4 27.8 all-gather.44
  544.5 32.7 all-gather.52
  580.0 32.7 all-gather.54
  615.0 27.8 all-gather.50
  645.0 32.8 all-gather.58
  680.5 32.7 all-gather.60
  715.4 27.8 all-gather.56
  885.3 57.6 reduce-scatter.27
  980.7 70.5 reduce-scatter.29
  2572.4 474.8 reduce-scatter.31
  3051.4 70.6 reduce-scatter.33
  3486.0 158.9 reduce-scatter.35
where the time goes:
time: 3930 us; the launch traced here: 3920 us
  blocking collectives  2490 us (63%)
  matrix products  489 us (12%)
  local copies, waits for them, and re-layouts  335 us (9%)
  waiting for transfers between devices  268 us (7%)
  other arithmetic  188 us (5%)
  starting transfers between devices  127 us (3%)
    unnamed x2, blocking collectives  2290 us
    unnamed x250, local copies, waits for them, and re-layouts  329 us
    all_gather x16, waiting for transfers between devices, gather_rows(): return lax.all_gather(local_piece, AXIS_NAME, axis=0, tiled=True)  257 us
    dot_general x16, matrix products, contract_rows(): lax.dot_general(left, right, (((0,), (0,)), ((), ())), preferred_element_...  170 us
    psum x1, blocking collectives, device_step(): mean_loss = lax.psum(loss_part, AXIS_NAME)  167 us
    dot_general x16, matrix products, contract_cols(): lax.dot_general(left, right, (((1,), (1,)), ((), ())), preferred_element_...  140 us
    unnamed x24, starting transfers between devices  126 us
    convert_element_type x1, other arithmetic, head_grads(): (weight[:, None] * (exp_shift / exp_sum - is_target.astype(jnp.float32)))...  96.3 us
  transfers between devices with their start and end apart: 45, of which 9 were waited for; matrix products, arithmetic and copies ran while one was open for 79% of the time, Pallas kernels for 0%

commit v1 on v0

v1 whole, which is shorter than its diff:
```python
import functools

import jax
import jax.numpy as jnp
from jax import lax
from jax.experimental import pallas as pl
from jax.experimental.pallas import tpu as pltpu
from jax.sharding import PartitionSpec as P

EPS = 1e-5
AXIS = 'fsdp'
N_DEV = 16
LAYERS = 5
TOK = 1024
DIM = 576
FFN = 1536
VOCAB = 49152
VLOC = VOCAB // N_DEV
TOKENS = TOK * N_DEV
CHUNKS = 2
TB = TOK // CHUNKS
CHUNK_TOK = TB * N_DEV
ZROWS = TB * 9 // 2
STRIPS = 4
SW = VLOC // STRIPS
PROWS = 1296
BF = jnp.bfloat16
F32 = jnp.float32
VMEM_LIMIT = 62 * 1024 * 1024


def dot_nn(a, b):
    return lax.dot_general(a, b, (((1,), (0,)), ((), ())), preferred_element_type=F32)


def dot_nt(a, b):
    return lax.dot_general(a, b, (((1,), (1,)), ((), ())), preferred_element_type=F32)


def dot_tn(a, b):
    return lax.dot_general(a, b, (((0,), (0,)), ((), ())), preferred_element_type=F32)


def inv_rms_of(x):
    return lax.rsqrt(jnp.mean(x * x, axis=-1, keepdims=True) + EPS)


def norm_grad(x, e):
    r = inv_rms_of(x)
    return r * e - x * (r * r * r) * jnp.mean(x * e, axis=-1, keepdims=True)


def store_packed(ref, val, rows):
    half = rows // 2
    for c in range(4):
        ref[0, c * rows:(c + 1) * rows, :] = val[:, c * 128:(c + 1) * 128]
    ref[0, 4 * rows:4 * rows + half, :] = jnp.concatenate([val[:half, 512:], val[half:, 512:]], axis=1)


def load_packed(dst, ref, rows):
    half = rows // 2
    for c in range(4):
        dst[:, c * 128:(c + 1) * 128] = ref[0, c * rows:(c + 1) * rows, :]
    tail = ref[0, 4 * rows:4 * rows + half, :]
    dst[0:half, 512:576] = tail[:, :64]
    dst[half:rows, 512:576] = tail[:, 64:]


def unpack_rows(p, rows):
    half = rows // 2
    tail = p[4 * rows:]
    tail = jnp.concatenate([tail[:, :64], tail[:, 64:]], axis=0)
    return jnp.concatenate([p[c * rows:(c + 1) * rows] for c in range(4)] + [tail], axis=1)


def fwd_body(h_ref, wg_ref, wu_ref, wd_ref, t_ref, z_ref):
    h = h_ref[...].astype(F32)
    n = (h * inv_rms_of(h)).astype(BF)
    u = dot_nn(n, wg_ref[...])
    v = dot_nn(n, wu_ref[...])
    a = (u * jax.nn.sigmoid(u) * v).astype(BF)
    t = (h + dot_nn(a, wd_ref[...])).astype(BF)
    t_ref[...] = t
    t = t.astype(F32)
    store_packed(z_ref, (t * inv_rms_of(t)).astype(BF), TB)


def top_forward(h, wg, wu, wd):
    full = lambda shape: pl.BlockSpec(shape, lambda i: (0,) * len(shape))
    return pl.pallas_call(
        fwd_body,
        grid=(CHUNKS,),
        in_specs=[pl.BlockSpec((TB, DIM), lambda i: (i, 0)), full((DIM, FFN)), full((DIM, FFN)), full((FFN, DIM))],
        out_specs=[pl.BlockSpec((TB, DIM), lambda i: (i, 0)), pl.BlockSpec((1, ZROWS, 128), lambda i: (i, 0, 0))],
        out_shape=[jax.ShapeDtypeStruct((TOK, DIM), BF), jax.ShapeDtypeStruct((CHUNKS, ZROWS, 128), BF)],
        compiler_params=pltpu.CompilerParams(vmem_limit_bytes=VMEM_LIMIT),
        cost_estimate=pl.CostEstimate(flops=6 * TOK * DIM * FFN, bytes_accessed=10 * 2**20, transcendentals=TOK * FFN),
        name='top_forward',
    )(h, wg, wu, wd)


def pass1_body(z_ref, w_ref, tok_ref, e_ref, ms_ref, st_ref, z_s):
    load_packed(z_s, z_ref, TB)
    z = z_s[...]
    tokc = jnp.concatenate([tok_ref[...], jnp.zeros((120, TB), F32)], axis=0).T
    tgt = tokc[:, 0:1]
    lane = lax.broadcasted_iota(jnp.int32, (TB, 128), 1)
    ids = lax.broadcasted_iota(jnp.int32, (1, SW), 1).astype(F32)
    ms = jnp.zeros((TB, 128), F32)
    tl = jnp.zeros((TB, 1), F32)
    m_list, s_list = [], []
    for s in range(STRIPS):
        l = dot_nn(z, w_ref[:, s * SW:(s + 1) * SW])
        m = jnp.max(l, axis=1, keepdims=True)
        e = jnp.exp(l - m)
        e_ref[:, s * SW:(s + 1) * SW] = e
        s_list.append(jnp.sum(e, axis=1, keepdims=True))
        m_list.append(m)
        tl = tl + jnp.sum(jnp.where(ids == tgt - float(s * SW), l, 0.0), axis=1, keepdims=True)
        ms = jnp.where(lane == s, m, ms)
    m_all = functools.reduce(jnp.maximum, m_list)
    s_all = sum(sv * jnp.exp(mv - m_all) for sv, mv in zip(s_list, m_list))
    ms_ref[...] = ms
    st = jnp.where(lane == 0, m_all, jnp.where(lane == 1, s_all, jnp.where(lane == 2, tl, 0.0)))
    st_ref[...] = st.T[0:8, :]


def head_pass1(z_all, w, tok):
    return pl.pallas_call(
        pass1_body,
        grid=(N_DEV,),
        in_specs=[
            pl.BlockSpec((1, ZROWS, 128), lambda i: (i, 0, 0)),
            pl.BlockSpec((DIM, VLOC), lambda i: (0, 0)),
            pl.BlockSpec((8, TB), lambda i: (0, i)),
        ],
        out_specs=[
            pl.BlockSpec((TB, VLOC), lambda i: (i, 0)),
            pl.BlockSpec((TB, 128), lambda i: (i, 0)),
            pl.BlockSpec((8, TB), lambda i: (0, i)),
        ],
        out_shape=[
            jax.ShapeDtypeStruct((CHUNK_TOK, VLOC), F32),
            jax.ShapeDtypeStruct((CHUNK_TOK, 128), F32),
            jax.ShapeDtypeStruct((8, CHUNK_TOK), F32),
        ],
        scratch_shapes=[pltpu.VMEM((TB, DIM), BF)],
        compiler_params=pltpu.CompilerParams(vmem_limit_bytes=VMEM_LIMIT),
        cost_estimate=pl.CostEstimate(flops=2 * CHUNK_TOK * DIM * VLOC, bytes_accessed=4 * CHUNK_TOK * VLOC, transcendentals=CHUNK_TOK * VLOC),
        name='head_pass1',
    )(z_all, w, tok)


def pass2_body(has_acc, *refs):
    if has_acc:
        z_ref, w_ref, tok_ref, e_ref, ms_ref, acc_ref, dz_ref, gw_ref, z_s, q_s = refs
    else:
        z_ref, w_ref, tok_ref, e_ref, ms_ref, dz_ref, gw_ref, z_s, q_s = refs
        acc_ref = None

    @pl.when(pl.program_id(0) == 0)
    def _():
        if has_acc:
            gw_ref[...] = acc_ref[...]
        else:
            gw_ref[...] = jnp.zeros_like(gw_ref)

    load_packed(z_s, z_ref, TB)
    z = z_s[...]
    tokc = jnp.concatenate([tok_ref[...], jnp.zeros((120, TB), F32)], axis=0).T
    tgt, w_tok, m_glob, s_inv = (tokc[:, i:i + 1] for i in range(4))
    ids = lax.broadcasted_iota(jnp.int32, (1, SW), 1).astype(F32)
    for s in range(STRIPS):
        cols = slice(s * SW, (s + 1) * SW)
        scale = jnp.exp(ms_ref[:, s:s + 1] - m_glob) * s_inv
        p = e_ref[:, cols] * scale
        p = jnp.where(ids == tgt - float(s * SW), p - 1.0, p)
        q = (w_tok * p).astype(BF)
        q_s[:, cols] = q
        gw_ref[:, cols] += dot_tn(z, q)
    dz = dot_nt(q_s[...], w_ref[...])
    store_packed(dz_ref, dz, TB)


def head_pass2(z_all, w, tok, e, ms, acc):
    in_specs = [
        pl.BlockSpec((1, ZROWS, 128), lambda i: (i, 0, 0)),
        pl.BlockSpec((DIM, VLOC), lambda i: (0, 0)),
        pl.BlockSpec((8, TB), lambda i: (0, i)),
        pl.BlockSpec((TB, VLOC), lambda i: (i, 0)),
        pl.BlockSpec((TB, 128), lambda i: (i, 0)),
    ]
    args = [z_all, w, tok, e, ms]
    if acc is not None:
        in_specs.append(pl.BlockSpec((DIM, VLOC), lambda i: (0, 0), pipeline_mode=pl.Buffered(1)))
        args.append(acc)
    return pl.pallas_call(
        functools.partial(pass2_body, acc is not None),
        grid=(N_DEV,),
        in_specs=in_specs,
        out_specs=[
            pl.BlockSpec((1, ZROWS, 128), lambda i: (i, 0, 0)),
            pl.BlockSpec((DIM, VLOC), lambda i: (0, 0), pipeline_mode=pl.Buffered(1)),
        ],
        out_shape=[
            jax.ShapeDtypeStruct((N_DEV, ZROWS, 128), F32),
            jax.ShapeDtypeStruct((DIM, VLOC), F32),
        ],
        scratch_shapes=[pltpu.VMEM((TB, DIM), BF), pltpu.VMEM((TB, VLOC), BF)],
        compiler_params=pltpu.CompilerParams(vmem_limit_bytes=VMEM_LIMIT),
        cost_estimate=pl.CostEstimate(flops=4 * CHUNK_TOK * DIM * VLOC, bytes_accessed=4 * CHUNK_TOK * VLOC, transcendentals=0),
        name='head_pass2',
    )(*args)


BT = 256


def bwd_body(off, has_buf, *refs):
    if has_buf:
        h_ref, g_ref, wg_ref, wu_ref, wd_ref, _, go_ref, buf_ref, n_s, k_s, a_s, du_s, dv_s, pk_s, sem = refs
    else:
        h_ref, g_ref, wg_ref, wu_ref, wd_ref, go_ref, buf_ref, n_s, k_s, a_s, du_s, dv_s, pk_s, sem = refs

    def step(i, carry):
        rows = pl.ds(pl.multiple_of(i * BT, BT), BT)
        h = h_ref[rows, :].astype(F32)
        r = inv_rms_of(h)
        n = (h * r).astype(BF)
        g = g_ref[rows, :]
        k = g.astype(BF)
        u = dot_nn(n, wg_ref[...])
        v = dot_nn(n, wu_ref[...])
        e = dot_nt(k, wd_ref[...])
        sg = jax.nn.sigmoid(u)
        us = u * sg
        a = (us * v).astype(BF)
        du = (e * v * sg * (1.0 + u * (1.0 - sg))).astype(BF)
        dv = (e * us).astype(BF)
        n_s[rows, :] = n
        k_s[rows, :] = k
        a_s[rows, :] = a
        du_s[rows, :] = du
        dv_s[rows, :] = dv
        dn = dot_nt(du, wg_ref[...]) + dot_nt(dv, wu_ref[...])
        go_ref[rows, :] = (g + r * dn - h * (r * r * r) * jnp.mean(h * dn, axis=-1, keepdims=True)).astype(go_ref.dtype)
        return carry

    lax.fori_loop(0, TOK // BT, step, 0)
    n = n_s[...]
    k = k_s[...]
    for c in range(6):
        gg = dot_tn(n, du_s[:, c * 256:(c + 1) * 256])
        gu = dot_tn(n, dv_s[:, c * 256:(c + 1) * 256])
        for j in range(2):
            base = (2 * c + j) * 72
            for d in range(N_DEV):
                pk_s[d, base:base + 36, :] = gg[36 * d:36 * d + 36, j * 128:(j + 1) * 128]
                pk_s[d, base + 36:base + 72, :] = gu[36 * d:36 * d + 36, j * 128:(j + 1) * 128]
    for c in range(4):
        gd = dot_tn(a_s[:, c * 384:(c + 1) * 384], k)
        for j in range(4):
            d = c * 4 + j
            x = gd[96 * j:96 * j + 96, :]
            for b in range(4):
                pk_s[d, 864 + 96 * b:864 + 96 * b + 96, :] = x[:, 128 * b:128 * b + 128]
            pk_s[d, 1248:1296, :] = jnp.concatenate([x[:48, 512:], x[48:, 512:]], axis=1)
    copy = pltpu.make_async_copy(pk_s, buf_ref.at[:, pl.ds(off, PROWS), :], sem)
    copy.start()
    copy.wait()


def block_backward(h, g, wg, wu, wd, buf, slot, slots, out_dtype):
    vm = pl.BlockSpec(memory_space=pltpu.VMEM)
    hb = pl.BlockSpec(memory_space=pl.ANY)
    args = [h, g, wg, wu, wd]
    in_specs = [vm] * 5
    aliases = {}
    if buf is not None:
        args.append(buf)
        in_specs.append(hb)
        aliases = {5: 1}
    return pl.pallas_call(
        functools.partial(bwd_body, slot * PROWS, buf is not None),
        in_specs=in_specs,
        out_specs=[vm, hb],
        out_shape=[jax.ShapeDtypeStruct((TOK, DIM), out_dtype), jax.ShapeDtypeStruct((N_DEV, slots * PROWS, 128), F32)],
        scratch_shapes=[
            pltpu.VMEM((TOK, DIM), BF), pltpu.VMEM((TOK, DIM), BF), pltpu.VMEM((TOK, FFN), BF),
            pltpu.VMEM((TOK, FFN), BF), pltpu.VMEM((TOK, FFN), BF), pltpu.VMEM((N_DEV, PROWS, 128), F32),
            pltpu.SemaphoreType.DMA,
        ],
        input_output_aliases=aliases,
        compiler_params=pltpu.CompilerParams(vmem_limit_bytes=VMEM_LIMIT),
        cost_estimate=pl.CostEstimate(flops=16 * TOK * DIM * FFN, bytes_accessed=24 * 2**20, transcendentals=TOK * FFN),
        name='block_backward',
    )(*args)


def unpack_body(p_ref, gg_ref, gu_ref, gd_ref):
    for c in range(12):
        gg_ref[0, :, c * 128:(c + 1) * 128] = p_ref[c * 72:c * 72 + 36, :]
        gu_ref[0, :, c * 128:(c + 1) * 128] = p_ref[c * 72 + 36:c * 72 + 72, :]
    for b in range(4):
        gd_ref[0, :, b * 128:(b + 1) * 128] = p_ref[864 + 96 * b:864 + 96 * b + 96, :]
    tail = p_ref[1248:1296, :]
    gd_ref[0, 0:48, 512:576] = tail[:, :64]
    gd_ref[0, 48:96, 512:576] = tail[:, 64:]


def unpack_grads(packed):
    return pl.pallas_call(
        unpack_body,
        grid=(LAYERS,),
        in_specs=[pl.BlockSpec((PROWS, 128), lambda i: (i, 0))],
        out_specs=[
            pl.BlockSpec((1, 36, FFN), lambda i: (i, 0, 0)),
            pl.BlockSpec((1, 36, FFN), lambda i: (i, 0, 0)),
            pl.BlockSpec((1, 96, DIM), lambda i: (i, 0, 0)),
        ],
        out_shape=[
            jax.ShapeDtypeStruct((LAYERS, 36, FFN), F32),
            jax.ShapeDtypeStruct((LAYERS, 36, FFN), F32),
            jax.ShapeDtypeStruct((LAYERS, 96, DIM), F32),
        ],
        name='unpack_grads',
    )(packed)


def pack_weights(wg, wu, wd):
    tail = jnp.concatenate([wd[:48, 512:], wd[48:, 512:]], axis=1)
    return jnp.concatenate(
        [wg.reshape(432, 128), wu.reshape(432, 128)] + [wd[:, c * 128:(c + 1) * 128] for c in range(4)] + [tail], axis=0)


def unpack_weights(p):
    wg = p[:, :432].reshape(DIM, FFN)
    wu = p[:, 432:864].reshape(DIM, FFN)
    tail = p[:, 1248:]
    tail = jnp.concatenate([tail[:, :, :64], tail[:, :, 64:]], axis=1)
    wd = jnp.concatenate([p[:, 864 + 96 * c:864 + 96 * c + 96] for c in range(4)] + [tail], axis=2)
    return wg, wu, wd.reshape(FFN, DIM)


GROUPS = ((4, 3), (2, 1, 0))


def solution(mesh):
    def device_step(hidden, w_gate, w_up, w_down, w_out, targets, loss_mask):
        me = lax.axis_index(AXIS)
        gather = functools.partial(lax.all_gather, axis_name=AXIS)
        packs = [pack_weights(w_gate[l], w_up[l], w_down[l]) for l in range(LAYERS)]
        weights = [None] * LAYERS
        weights[4] = unpack_weights(gather(packs[4]))
        lab = gather(jnp.stack([targets, loss_mask]))
        w_vocab = lax.all_to_all(w_out.reshape(36, N_DEV, VLOC), AXIS, 1, 0).reshape(DIM, VLOC)
        t, z_packed = top_forward(hidden[4], *weights[4])

        mask = lab[:, 1, :].astype(F32)
        w_tok = mask / jnp.sum(mask)
        tgt = (lab[:, 0, :] - me * VLOC).astype(F32)

        z_all, rest = [], None
        for c in range(CHUNKS):
            z_all.append(gather(z_packed[c]))
        rest = gather(jnp.stack(packs[:4]))
        acc, loss, g_rows = None, jnp.zeros((), F32), []
        for c in range(CHUNKS):
            sl = slice(c * TB, (c + 1) * TB)
            tg = tgt[:, sl].reshape(1, CHUNK_TOK)
            wt = w_tok[:, sl].reshape(1, CHUNK_TOK)
            zero = jnp.zeros((1, CHUNK_TOK), F32)
            e, ms, st = head_pass1(z_all[c], w_vocab, jnp.concatenate([tg] + [zero] * 7, axis=0))
            m_glob = lax.pmax(st[0:1], AXIS)
            sums = lax.psum(jnp.concatenate([st[1:2] * jnp.exp(st[0:1] - m_glob), st[2:3]], axis=0), AXIS)
            loss = loss + jnp.sum(wt * (m_glob + jnp.log(sums[0:1]) - sums[1:2]))
            tok = jnp.concatenate([tg, wt, m_glob, 1.0 / sums[0:1]] + [zero] * 4, axis=0)
            dz, acc = head_pass2(z_all[c], w_vocab, tok, e, ms, acc)
            dz = lax.psum_scatter(dz, AXIS, scatter_dimension=0, tiled=False)
            g_rows.append(norm_grad(t[sl].astype(F32), unpack_rows(dz, TB)))
        grad_out = lax.all_to_all(acc.reshape(N_DEV, 36, VLOC), AXIS, 0, 1)
        grad_out = grad_out.reshape(36, VOCAB)
        for l in range(4):
            weights[l] = unpack_weights(rest[:, l])

        g = jnp.concatenate(g_rows, axis=0)
        packed = [None] * LAYERS
        for group in GROUPS:
            buf = None
            for i, l in enumerate(group):
                g, buf = block_backward(hidden[l], g, *weights[l], buf, i, len(group), BF if l == 0 else F32)
            red = lax.psum_scatter(buf, AXIS, scatter_dimension=0, tiled=False)
            for i, l in enumerate(group):
                packed[l] = red[i * PROWS:(i + 1) * PROWS]
        grad_gate, grad_up, grad_down = unpack_grads(jnp.concatenate(packed, axis=0))
        return grad_gate, grad_up, grad_down, grad_out, g, loss

    stacked = P(None, AXIS, None)
    row = P(AXIS, None)
    return jax.shard_map(device_step, mesh=mesh, in_specs=(stacked, stacked, stacked, stacked, row, P(AXIS), P(AXIS)), out_specs=(stacked, stacked, stacked, row, row, P()), check_vma=False)
```

time: 3930 us -> 1310 us (0.33)
  blocking collectives: 2490 us -> 66.6 us
  Pallas kernels: 0 us -> 494 us
  matrix products: 489 us -> 0 us
  waiting for transfers between devices: 268 us -> 520 us
  other arithmetic: 188 us -> 13.7 us
  local copies, waits for them, and re-layouts: 335 us -> 175 us
  starting transfers between devices: 127 us -> 8.33 us
    unnamed x2 -> x0, blocking collectives: 2290 us -> none
    pallas_call x0 -> x11, Pallas kernels: none -> 494 us  [the longest x2 193 us: head_pass2(): pl.pallas_call(functools.partial(pass2_body, acc is not None), grid=(N_DE...]
    dot_general x44 -> x0, matrix products: 489 us -> none  [the longest x16 170 us: contract_rows(): lax.dot_general(left, right, (((0,), (0,)), ((), ())), preferred_element_...]
    unnamed x250 -> x147, local copies, waits for them, and re-layouts: 329 us -> 63.2 us
    reduce_scatter x5 -> x4, waiting for transfers between devices: 0.09 us -> 242 us  [the longest x2 194 us: device_step(): red = lax.psum_scatter(buf, AXIS, scatter_dimension=0, tiled=False)]
    all_gather x16 -> x4, waiting for transfers between devices: 257 us -> 36.3 us  [the longest x1 35 us: device_step(): weights[4] = unpack_weights(gather(packs[4]))]
    psum x2 -> x0, blocking collectives: 202 us -> none  [the longest x1 167 us: device_step(): mean_loss = lax.psum(loss_part, AXIS_NAME)]
    unnamed x24 -> x0, starting transfers between devices: 126 us -> none
  transfers between devices with their start and end apart: 45 -> 12, of which waited for: 9 -> 8; matrix products, arithmetic and copies ran while one was open for 79% -> 11% of each run, Pallas kernels for 0% -> 20%
where the time goes in v1:
time: 1310 us; the launch traced here: 1300 us
  waiting for transfers between devices  520 us (40%)
  Pallas kernels  494 us (38%)
  local copies, waits for them, and re-layouts  175 us (13%)
  blocking collectives  66.6 us (5%)
  between operations  18 us (1%)
  other arithmetic  13.7 us (1%)
    reduce_scatter x2, waiting for transfers between devices, device_step(): red = lax.psum_scatter(buf, AXIS, scatter_dimension=0, tiled=False)  194 us
    pallas_call x2, Pallas kernels, head_pass2(): pl.pallas_call(functools.partial(pass2_body, acc is not None), grid=(N_DE...  193 us
    pallas_call x5, Pallas kernels, block_backward(): pl.pallas_call(functools.partial(bwd_body, slot * PROWS, buf is not None)...  160 us
    pallas_call x2, Pallas kernels, head_pass1(): pl.pallas_call(pass1_body, grid=(N_DEV,), in_specs=[pl.BlockSpec((1, ZROW...  123 us
    all_to_all x1, waiting for transfers between devices, device_step(): grad_out = lax.all_to_all(acc.reshape(N_DEV, 36, VLOC), AXIS, 0, 1)  114 us
    all_gather x1, blocking collectives, device_step(): lab = gather(jnp.stack([targets, loss_mask]))  66.6 us
    pmax x1, waiting for transfers between devices, device_step(): m_glob = lax.pmax(st[0:1], AXIS)  65.3 us
    unnamed x147, local copies, waits for them, and re-layouts  63.2 us
  transfers between devices with their start and end apart: 12, of which 8 were waited for; matrix products, arithmetic and copies ran while one was open for 11% of the time, Pallas kernels for 20%

profile of v1, /device:TPU:0, one launch (start us, length us, event | category | flops | bytes accessed | tf_op | source)
XLA Modules:
  0.0 1296.4 jit_solution(3111997585306651439)
XLA Ops:
  12.2 5.1 fusion.28
  18.8 35.0 %all-gather.13.cloned.1.call-done = bf16[20736,128]{1,0:T(8,128)(2,1)} async-done(((bf16[1296,128]{1,0:T(8,128)(2,1)}), bf16[20736,128]{1,0:T(8,128)(2,1)}) %all-gather.13.cloned.1.call-update) | async-done | bytes 5308432 | tf_op jit(solution)/shard_map/all_gather | solution.py:354
  59.6 3.0 reshape.128.wg_ref.refs_2_
  62.6 3.0 reshape.129.wu_ref.refs_3_
  72.1 11.9 top_forward.1
  87.1 4.3 copy.63
  91.8 3.9 copy.52
  95.7 3.4 all-to-all-start
  99.5 66.6 %all-gather.3 = s32[16,2,1024]{2,1,0:T(2,128)S(1)} all-gather(s32[1,2,1024]{2,1,0:T(2,128)S(1)} %add_bitcast_fusion), channel_id=3, replica_groups=mesh['fsdp'=16] {'fsdp'}, dimensions={0}, use_global_device_ids=true | all-gather | bytes 139264 | tf_op jit(solution)/shard_map/all_gather | solution.py:355
  169.9 4.7 reshape_squeeze.38.w_ref.refs_1_
  175.9 61.7 %head_pass1.3 = (f32[8192,3072]{1,0:T(8,128)}, f32[8192,128]{1,0:T(8,128)}, f32[8,8192]{1,0:T(8,128)}) custom-call(bf16[16,2304,128]{2,1,0:T(8,128)(2,1)} %all-gather.11.cloned.1.call-done.z_ref.refs_0_, bf16[576,3072]{1,0:T(8,128)(2,1)} %reshape_squeeze.38.w_ref.refs_1_, f32[8,8192]{1,0:T(8,128)} %concatenate.105.tok_ref), custom_call_target="tpu_custom_call" | custom-call | flops 28991029248 | bytes 100663296 | tf_op jit(solution)/shard_map/head_pass1/pallas_call | solution.py:129
  239.2 61.6 %head_pass1.2 = (f32[8192,3072]{1,0:T(8,128)}, f32[8192,128]{1,0:T(8,128)}, f32[8,8192]{1,0:T(8,128)}) custom-call(bf16[16,2304,128]{2,1,0:T(8,128)(2,1)} %all-gather.9.cloned.1.call-done.z_ref.refs_0_, bf16[576,3072]{1,0:T(8,128)(2,1)} %reshape_squeeze.38.w_ref.refs_1_, f32[8,8192]{1,0:T(8,128)} %concatenate.100.tok_ref), custom_call_target="tpu_custom_call" | custom-call | flops 28991029248 | bytes 100663296 | tf_op jit(solution)/shard_map/head_pass1/pallas_call | solution.py:129
  302.5 65.3 %all-reduce.9.cloned.1.call-done = (f32[1,8192]{1,0:T(1,128)}, f32[1,8192]{1,0:T(1,128)}) async-done(((f32[1,8192]{1,0:T(1,128)}, f32[1,8192]{1,0:T(1,128)}), (f32[1,8192]{1,0:T(1,128)}, f32[1,8192]{1,0:T(1,128)})) %all-reduce.9.cloned.1.call-update) | async-done | bytes 65552 | tf_op jit(solution)/shard_map/pmax | solution.py:374
  374.3 62.4 %all-reduce.7.cloned.1.call-done = (f32[2,8192]{1,0:T(2,128)}, f32[2,8192]{1,0:T(2,128)}) async-done(((f32[2,8192]{1,0:T(2,128)}, f32[2,8192]{1,0:T(2,128)}), (f32[2,8192]{1,0:T(2,128)}, f32[2,8192]{1,0:T(2,128)})) %all-reduce.7.cloned.1.call-update) | async-done | bytes 131088 | tf_op jit(solution)/shard_map/psum | solution.py:375
  439.2 95.5 %head_pass2.2 = (f32[16,2304,128]{2,1,0:T(8,128)}, f32[576,3072]{1,0:T(8,128)}) custom-call(bf16[16,2304,128]{2,1,0:T(8,128)(2,1)} %all-gather.9.cloned.1.call-done.z_ref.refs_0_, bf16[576,3072]{1,0:T(8,128)(2,1)} %reshape_squeeze.38.w_ref.refs_1_, f32[8,8192]{1,0:T(8,128)} %concatenate.102.refs_2_, f32[8192,3072]{1,0:T(8,128)} %get-tuple-element.34.refs_3_, ...), custom_call_target="tpu_custom_call" | custom-call | flops 57982058496 | bytes 100663296 | tf_op jit(solution)/shard_map/head_pass2/pallas_call | solution.py:197
  537.2 97.4 %head_pass2.3 = (f32[16,2304,128]{2,1,0:T(8,128)}, f32[576,3072]{1,0:T(8,128)}) custom-call(bf16[16,2304,128]{2,1,0:T(8,128)(2,1)} %all-gather.11.cloned.1.call-done.z_ref.refs_0_, bf16[576,3072]{1,0:T(8,128)(2,1)} %reshape_squeeze.38.w_ref.refs_1_, f32[8,8192]{1,0:T(8,128)} %concatenate.107.refs_2_, f32[8192,3072]{1,0:T(8,128)} %get-tuple-element.38.refs_3_, ...), custom_call_target="tpu_custom_call" | custom-call | flops 57982058496 | bytes 100663296 | tf_op jit(solution)/shard_map/head_pass2/pallas_call | solution.py:197
  641.8 14.8 %slice_bitcast_fusion = (bf16[16,1296,128]{2,1,0:T(8,128)(2,1)}, bf16[16,1296,128]{2,1,0:T(8,128)(2,1)}, bf16[16,1296,128]{2,1,0:T(8,128)(2,1)}, bf16[16,1296,128]{2,1,0:T(8,128)(2,1)S(1)}) fusion(bf16[16,4,1296,128]{3,2,1,0:T(8,128)(2,1)} %bitcast.138), kind=kLoop, calls=%fused_computation.1 | loop fusion | bytes 42467328 | tf_op jit(solution)/shard_map/squeeze | solution.py:384
  686.6 3.2 reshape.145.refs_3_
  718.7 47.8 %reduce-scatter.7.cloned.1.call-done = f32[1,2304,128]{2,1,0:T(8,128)} async-done(((f32[16,2304,128]{2,1,0:T(8,128)}), f32[1,2304,128]{2,1,0:T(8,128)}) %reduce-scatter.7.cloned.1.call-update) | async-done | bytes 1179664 | tf_op jit(solution)/shard_map/reduce_scatter | solution.py:379
  772.9 32.1 %block_backward.5 = (f32[1024,576]{1,0:T(8,128)}, f32[16,2592,128]{2,1,0:T(8,128)}) custom-call(bf16[1024,576]{1,0:T(8,128)(2,1)} %bitcast.149, f32[1024,576]{1,0:T(8,128)} %pad_maximum_fusion.refs_1_, bf16[576,1536]{1,0:T(8,128)(2,1)} %reshape.128.wg_ref.refs_2_, bf16[576,1536]{1,0:T(8,128)(2,1)} %reshape.129.wu_ref.refs_3_, bf16[1536,576]{1,0:T(8,128)(2,1)} %bitcast.169), custom_call_target="tpu_custom_call" | custom-call | flops 14495514624 | bytes 25165824 | tf_op jit(solution)/shard_map/block_backward/pallas_call | solution.py:283
  805.0 32.5 %block_backward.6 = (f32[1024,576]{1,0:T(8,128)}, f32[16,2592,128]{2,1,0:T(8,128)}) custom-call(bf16[1024,576]{1,0:T(8,128)(2,1)} %bitcast.153, f32[1024,576]{1,0:T(8,128)} %get-tuple-element.42.refs_1_, bf16[576,1536]{1,0:T(8,128)(2,1)} %reshape.135.refs_2_, bf16[576,1536]{1,0:T(8,128)(2,1)} %reshape.136.refs_3_, ...), custom_call_target="tpu_custom_call", output_to_operand_aliasing={{1}: (5, {})} | custom-call | flops 14495514624 | bytes 25165824 | tf_op jit(solution)/shard_map/block_backward/pallas_call | solution.py:283
  837.6 32.2 %block_backward.7 = (f32[1024,576]{1,0:T(8,128)}, f32[16,3888,128]{2,1,0:T(8,128)}) custom-call(bf16[1024,576]{1,0:T(8,128)(2,1)} %bitcast.152, f32[1024,576]{1,0:T(8,128)} %get-tuple-element.44.refs_1_, bf16[576,1536]{1,0:T(8,128)(2,1)} %reshape.138.refs_2_, bf16[576,1536]{1,0:T(8,128)(2,1)} %reshape.139.refs_3_, bf16[1536,576]{1,0:T(8,128)(2,1)} %bitcast.171), custom_call_target="tpu_custom_call" | custom-call | flops 14495514624 | bytes 25165824 | tf_op jit(solution)/shard_map/block_backward/pallas_call | solution.py:283
  869.8 32.0 %block_backward.8 = (f32[1024,576]{1,0:T(8,128)}, f32[16,3888,128]{2,1,0:T(8,128)}) custom-call(bf16[1024,576]{1,0:T(8,128)(2,1)} %bitcast.151, f32[1024,576]{1,0:T(8,128)} %get-tuple-element.45.refs_1_, bf16[576,1536]{1,0:T(8,128)(2,1)} %reshape.141.refs_2_, bf16[576,1536]{1,0:T(8,128)(2,1)} %reshape.142.refs_3_, ...), custom_call_target="tpu_custom_call", output_to_operand_aliasing={{1}: (5, {})} | custom-call | flops 14495514624 | bytes 25165824 | tf_op jit(solution)/shard_map/block_backward/pallas_call | solution.py:283
  901.7 31.7 %block_backward.9 = (bf16[1024,576]{1,0:T(8,128)(2,1)}, f32[16,3888,128]{2,1,0:T(8,128)}) custom-call(bf16[1024,576]{1,0:T(8,128)(2,1)} %bitcast.150, f32[1024,576]{1,0:T(8,128)} %get-tuple-element.47.refs_1_, bf16[576,1536]{1,0:T(8,128)(2,1)} %reshape.144.refs_2_, bf16[576,1536]{1,0:T(8,128)(2,1)} %reshape.145.refs_3_, ...), custom_call_target="tpu_custom_call", output_to_operand_aliasing={{1}: (5, {})} | custom-call | flops 14495514624 | bytes 25165824 | tf_op jit(solution)/shard_map/block_backward/pallas_call | solution.py:283
  934.1 11.5 broadcast_in_dim_reshape.8
  945.6 3.7 all-to-all-start.1
  950.5 113.5 %all-to-all-done.1 = f32[16,36,1,3072]{3,2,1,0:T(1,128)} async-done(((f32[16,36,1,3072]{3,2,1,0:T(1,128)}), f32[16,36,1,3072]{3,2,1,0:T(1,128)}, u32[]{:S(2)}, u32[]{:S(2)}) %all-to-all-start.1) | async-done | bytes 7077920 | tf_op jit(solution)/shard_map/all_to_all | solution.py:381
  1064.1 7.1 copy.72
  1072.4 7.7 copy.68
  1081.5 68.9 %reduce-scatter.9.cloned.1.call-done = f32[1,3888,128]{2,1,0:T(8,128)} async-done(((f32[16,3888,128]{2,1,0:T(8,128)}), f32[1,3888,128]{2,1,0:T(8,128)}) %reduce-scatter.9.cloned.1.call-update) | async-done | bytes 1990672 | tf_op jit(solution)/shard_map/reduce_scatter | solution.py:392
  1153.8 124.8 %reduce-scatter.11.cloned.1.call-done = f32[1,2592,128]{2,1,0:T(8,128)} async-done(((f32[16,2592,128]{2,1,0:T(8,128)}), f32[1,2592,128]{2,1,0:T(8,128)}) %reduce-scatter.11.cloned.1.call-update) | async-done | bytes 1327120 | tf_op jit(solution)/shard_map/reduce_scatter | solution.py:392
  1282.6 5.4 unpack_grads.1
  (246 shorter events, 124.6 us)
Async XLA Ops:
  7.2 3.2 copy-start.13
  7.2 46.5 %all-gather.13.cloned.1.call-start = ((), (), s32[]{:S(2)}) async-start(), calls=%async_computation.12 | async-start | bytes 5640192 | tf_op jit(solution)/shard_map/all_gather | solution.py:354
  12.2 163.8 %all-gather.11.cloned.1.call-start = ((), (), s32[]{:S(2)}) async-start(), calls=%async_computation.8 | async-start | bytes 10027008 | tf_op jit(solution)/shard_map/all_gather | solution.py:365
  65.7 5.5 copy-start.10
  65.7 5.5 copy-start.11
  86.4 152.8 %all-gather.9.cloned.1.call-start = ((), (), s32[]{:S(2)}) async-start(), calls=%async_computation.6 | async-start | bytes 10027008 | tf_op jit(solution)/shard_map/all_gather | solution.py:365
  95.7 3.8 copy-start.33
  95.7 3.8 copy-start.34
  95.7 70.5 %copy-start.24 = (bf16[1,36,1536]{2,1,0:T(8,128)(2,1)S(1)}, bf16[1,36,1536]{2,1,0:T(8,128)(2,1)}, u32[]{:S(2)}) copy-start(bf16[1,36,1536]{2,1,0:T(8,128)(2,1)} %get-tuple-element.141) | copy-start | bytes 331780
  95.7 70.7 %copy-start.26 = (bf16[1,36,1536]{2,1,0:T(8,128)(2,1)S(1)}, bf16[1,36,1536]{2,1,0:T(8,128)(2,1)}, u32[]{:S(2)}) copy-start(bf16[1,36,1536]{2,1,0:T(8,128)(2,1)} %get-tuple-element.136) | copy-start | bytes 331780
  95.7 70.9 %copy-start.23 = (bf16[1,36,1536]{2,1,0:T(8,128)(2,1)S(1)}, bf16[1,36,1536]{2,1,0:T(8,128)(2,1)}, u32[]{:S(2)}) copy-start(bf16[1,36,1536]{2,1,0:T(8,128)(2,1)} %get-tuple-element.140) | copy-start | bytes 331780
  95.7 71.0 %copy-start.25 = (bf16[1,36,1536]{2,1,0:T(8,128)(2,1)S(1)}, bf16[1,36,1536]{2,1,0:T(8,128)(2,1)}, u32[]{:S(2)}) copy-start(bf16[1,36,1536]{2,1,0:T(8,128)(2,1)} %get-tuple-element.135) | copy-start | bytes 331780
  95.7 74.2 %all-to-all-start = ((bf16[1,36,16,3072]{3,1,0,2:T(8,128)(2,1)}), bf16[1,36,16,3072]{3,1,0,2:T(8,128)(2,1)}, u32[]{:S(2)}, u32[]{:S(2)}) async-start(bf16[1,36,16,3072]{3,1,0,2:T(8,128)(2,1)} %copy.52), calls=%async_computation | async-start | bytes 7864320 | tf_op jit(solution)/shard_map/all_to_all | solution.py:356
  99.2 67.8 %copy-start.19 = (bf16[96,576]{1,0:T(8,128)(2,1)S(1)}, bf16[96,576]{1,0:T(8,128)(2,1)}, u32[]{:S(2)}) copy-start(bf16[96,576]{1,0:T(8,128)(2,1)} %get-tuple-element.131) | copy-start | bytes 331780
  99.2 67.9 %copy-start.18 = (bf16[96,576]{1,0:T(8,128)(2,1)S(1)}, bf16[96,576]{1,0:T(8,128)(2,1)}, u32[]{:S(2)}) copy-start(bf16[96,576]{1,0:T(8,128)(2,1)} %get-tuple-element.130) | copy-start | bytes 331780
  99.2 69.5 %copy-start.20 = (bf16[1,36,1536]{2,1,0:T(8,128)(2,1)S(1)}, bf16[1,36,1536]{2,1,0:T(8,128)(2,1)}, u32[]{:S(2)}) copy-start(bf16[1,36,1536]{2,1,0:T(8,128)(2,1)} %get-tuple-element.137) | copy-start | bytes 331780
  99.2 69.7 %copy-start.22 = (bf16[1,36,1536]{2,1,0:T(8,128)(2,1)S(1)}, bf16[1,36,1536]{2,1,0:T(8,128)(2,1)}, u32[]{:S(2)}) copy-start(bf16[1,36,1536]{2,1,0:T(8,128)(2,1)} %get-tuple-element.132) | copy-start | bytes 331780
  99.2 69.8 %copy-start.17 = (bf16[1,36,1536]{2,1,0:T(8,128)(2,1)S(1)}, bf16[1,36,1536]{2,1,0:T(8,128)(2,1)}, u32[]{:S(2)}) copy-start(bf16[1,36,1536]{2,1,0:T(8,128)(2,1)} %get-tuple-element.138) | copy-start | bytes 331780
  99.2 268.6 %all-reduce.9.cloned.1.call-start = ((), (), s32[]{:S(2)}) async-start(), calls=%async_computation.15 | async-start | bytes 131072 | tf_op jit(solution)/shard_map/pmax | solution.py:374
  302.4 134.3 %all-reduce.7.cloned.1.call-start = ((), (), s32[]{:S(2)}) async-start(), calls=%async_computation.14 | async-start | bytes 262144 | tf_op jit(solution)/shard_map/psum | solution.py:375
  371.0 270.8 %all-gather.15.cloned.1.call-start = ((), (), s32[]{:S(2)}) async-start(), calls=%async_computation.13 | async-start | bytes 22560768 | tf_op jit(solution)/shard_map/all_gather | solution.py:366
  371.0 65.7 %copy-start.28 = (f32[1,8192]{1,0:T(1,128)S(1)}, f32[1,8192]{1,0:T(1,128)}, u32[]{:S(2)}) copy-start(f32[1,8192]{1,0:T(1,128)} %get-tuple-element.93) | copy-start | bytes 98308
  372.3 345.4 %reduce-scatter.5.cloned.1.call-start = ((), (), s32[]{:S(2)}) async-start(), calls=%async_computation.7 | async-start | bytes 20054016 | tf_op jit(solution)/shard_map/reduce_scatter | solution.py:379
  534.7 231.8 %reduce-scatter.7.cloned.1.call-start = ((), (), s32[]{:S(2)}) async-start(), calls=%async_computation.9 | async-start | bytes 20054016 | tf_op jit(solution)/shard_map/reduce_scatter | solution.py:379
  634.7 515.7 %reduce-scatter.9.cloned.1.call-start = ((), (), s32[]{:S(2)}) async-start(), calls=%async_computation.10 | async-start | bytes 33841152 | tf_op jit(solution)/shard_map/reduce_scatter | solution.py:392
  695.5 6.0 copy-start.29
  701.7 6.0 copy-start.30
  707.8 8.9 copy-start.31
  717.6 51.0 %copy-start.8 = (f32[1,2304,128]{2,1,0:T(8,128)S(1)}, f32[1,2304,128]{2,1,0:T(8,128)}, u32[]{:S(2)}) copy-start(f32[1,2304,128]{2,1,0:T(8,128)} %reduce-scatter.5.cloned.1.call-done) | copy-start | bytes 3538948
  933.5 345.2 %reduce-scatter.11.cloned.1.call-start = ((), (), s32[]{:S(2)}) async-start(), calls=%async_computation.11 | async-start | bytes 22560768 | tf_op jit(solution)/shard_map/reduce_scatter | solution.py:392
  945.6 118.5 %all-to-all-start.1 = ((f32[16,36,1,3072]{3,2,1,0:T(1,128)}), f32[16,36,1,3072]{3,2,1,0:T(1,128)}, u32[]{:S(2)}, u32[]{:S(2)}) async-start(f32[16,36,1,3072]{3,2,1,0:T(1,128)} %broadcast_in_dim_reshape.8), calls=%async_computation.5 | async-start | bytes 14155776 | tf_op jit(solution)/shard_map/all_to_all | solution.py:381
  1072.4 7.7 copy-start.7
  (15 other events, 30.6 us)
Sparse Core Ops, SparseCore 0:
  12.3 41.3 all-gather.12
  86.5 89.3 all-gather.10
  178.1 51.8 all-gather.8
  302.5 65.3 all-reduce.8
  372.7 63.9 all-reduce.6
  438.8 88.9 all-gather.14
  534.9 112.5 reduce-scatter.4
  652.4 114.1 reduce-scatter.6
  933.6 216.7 reduce-scatter.8
  1155.4 123.2 reduce-scatter.10

commit v2 on v1

v2 whole, which is shorter than its diff:
```python
import functools

import jax
import jax.numpy as jnp
from jax import lax
from jax.experimental import pallas as pl
from jax.experimental.pallas import tpu as pltpu
from jax.sharding import PartitionSpec as P

EPS = 1e-5
AXIS = 'fsdp'
N_DEV = 16
LAYERS = 5
TOK = 1024
DIM = 576
FFN = 1536
VOCAB = 49152
VLOC = VOCAB // N_DEV
TOKENS = TOK * N_DEV
CHUNKS = 2
TB = TOK // CHUNKS
CHUNK_TOK = TB * N_DEV
ZROWS = TB * 9 // 2
STRIPS = 4
SW = VLOC // STRIPS
PROWS = 1296
BF = jnp.bfloat16
F32 = jnp.float32
MESH = pl.DeviceIdType.MESH
VMEM_LIMIT = 62 * 1024 * 1024


def whole(*shape):
    return pl.BlockSpec(shape, lambda i: tuple(0 * d for d in shape))


def rows_spec(*shape):
    rest = shape[1:]
    return pl.BlockSpec(shape, lambda i: (i, *(0 * d for d in rest)))


def lanes_spec(*shape):
    return pl.BlockSpec(shape, lambda i: (0, i))


VM = pl.BlockSpec(memory_space=pltpu.VMEM)
HB = pl.BlockSpec(memory_space=pl.ANY)


def dot_nn(a, b):
    return lax.dot_general(a, b, (((1,), (0,)), ((), ())), preferred_element_type=F32)


def dot_nt(a, b):
    return lax.dot_general(a, b, (((1,), (1,)), ((), ())), preferred_element_type=F32)


def dot_tn(a, b):
    return lax.dot_general(a, b, (((0,), (0,)), ((), ())), preferred_element_type=F32)


def inv_rms_of(x):
    return lax.rsqrt(jnp.mean(x * x, axis=-1, keepdims=True) + EPS)


def norm_grad(x, e):
    r = inv_rms_of(x)
    return r * e - x * (r * r * r) * jnp.mean(x * e, axis=-1, keepdims=True)


def store_packed(ref, val, rows):
    half = rows // 2
    for c in range(4):
        ref[0, c * rows:(c + 1) * rows, :] = val[:, c * 128:(c + 1) * 128]
    ref[0, 4 * rows:4 * rows + half, :] = jnp.concatenate([val[:half, 512:], val[half:, 512:]], axis=1)


def load_packed(dst, ref, rows):
    half = rows // 2
    for c in range(4):
        dst[:, c * 128:(c + 1) * 128] = ref[0, c * rows:(c + 1) * rows, :]
    tail = ref[0, 4 * rows:4 * rows + half, :]
    dst[0:half, 512:576] = tail[:, :64]
    dst[half:rows, 512:576] = tail[:, 64:]


def unpack_rows(p, rows):
    half = rows // 2
    tail = p[4 * rows:]
    tail = jnp.concatenate([tail[:, :64], tail[:, 64:]], axis=0)
    return jnp.concatenate([p[c * rows:(c + 1) * rows] for c in range(4)] + [tail], axis=1)


W_SCRATCH = [pltpu.VMEM((DIM, FFN), BF), pltpu.VMEM((DIM, FFN), BF), pltpu.VMEM((FFN, DIM), BF)]


def fwd_body(h_ref, p_ref, t_ref, z_ref, wg_ref, wu_ref, wd_ref):
    @pl.when(pl.program_id(0) == 0)
    def _():
        unpack_weights(p_ref, 0, wg_ref, wu_ref, wd_ref)

    h = h_ref[...].astype(F32)
    n = (h * inv_rms_of(h)).astype(BF)
    u = dot_nn(n, wg_ref[...])
    v = dot_nn(n, wu_ref[...])
    a = (u * jax.nn.sigmoid(u) * v).astype(BF)
    t = (h + dot_nn(a, wd_ref[...])).astype(BF)
    t_ref[...] = t
    t = t.astype(F32)
    store_packed(z_ref, (t * inv_rms_of(t)).astype(BF), TB)


def top_forward(h, packs):
    return pl.pallas_call(
        fwd_body,
        grid=(CHUNKS,),
        in_specs=[rows_spec(TB, DIM), whole(N_DEV, 1, PROWS, 128)],
        out_specs=[rows_spec(TB, DIM), rows_spec(1, ZROWS, 128)],
        out_shape=[jax.ShapeDtypeStruct((TOK, DIM), BF), jax.ShapeDtypeStruct((CHUNKS, ZROWS, 128), BF)],
        scratch_shapes=W_SCRATCH,
        compiler_params=pltpu.CompilerParams(vmem_limit_bytes=VMEM_LIMIT),
        cost_estimate=pl.CostEstimate(flops=6 * TOK * DIM * FFN, bytes_accessed=10 * 2**20, transcendentals=TOK * FFN),
        name='top_forward',
    )(h, packs)


def peers_barrier(me):
    sem = pltpu.get_barrier_semaphore()
    for off in range(1, N_DEV):
        pl.semaphore_signal(sem, inc=1, device_id=(lax.rem(me + off, N_DEV),), device_id_type=MESH)
    pl.semaphore_wait(sem, N_DEV - 1)


def all_send(me, src_of, dst, send_sem, recv_sem):
    copies = []
    for off in range(1, N_DEV):
        to = lax.rem(me + off, N_DEV)
        copy = pltpu.make_async_remote_copy(
            src_ref=src_of(to), dst_ref=dst.at[me], send_sem=send_sem.at[off], recv_sem=recv_sem.at[me],
            device_id=(to,), device_id_type=MESH)
        copy.start()
        copies.append(copy)
    return copies


def all_wait(me, src_of, dst, send_sem, recv_sem):
    for off in range(1, N_DEV):
        frm = lax.rem(me + N_DEV - off, N_DEV)
        copy = pltpu.make_async_remote_copy(
            src_ref=src_of(frm), dst_ref=dst.at[frm], send_sem=send_sem.at[off], recv_sem=recv_sem.at[frm],
            device_id=(frm,), device_id_type=MESH)
        copy.wait_recv()


def labels_body(x_ref, o_ref, buf, send_sem, recv_sem):
    me = lax.axis_index(AXIS)
    peers_barrier(me)
    src = lambda j: x_ref
    copies = all_send(me, src, buf, send_sem, recv_sem)
    all_wait(me, src, buf, send_sem, recv_sem)
    for copy in copies:
        copy.wait_send()
    for j in range(N_DEV):
        o_ref[j] = jnp.where(me == j, x_ref[...], buf[j])


def gather_labels(x):
    return pl.pallas_call(
        labels_body,
        in_specs=[VM],
        out_specs=VM,
        out_shape=jax.ShapeDtypeStruct((N_DEV, 8, TOK), F32),
        scratch_shapes=[pltpu.VMEM((N_DEV, 8, TOK), F32), pltpu.SemaphoreType.DMA((N_DEV,)), pltpu.SemaphoreType.DMA((N_DEV,))],
        compiler_params=pltpu.CompilerParams(collective_id=1, has_side_effects=True),
        cost_estimate=pl.CostEstimate(flops=2 * 10**9, bytes_accessed=2**20, transcendentals=0),
        name='gather_labels',
    )(x)


def stats_body(st_ref, w_ref, o_ref, buf1, own, buf2, send1, recv1, send2, recv2):
    me = lax.axis_index(AXIS)
    peers_barrier(me)
    part = lambda j: st_ref.at[:, pl.ds(pl.multiple_of(j * TB, TB), TB)]
    copies = all_send(me, part, buf1, send1, recv1)
    all_wait(me, part, buf1, send1, recv1)
    mine = st_ref[:, pl.ds(pl.multiple_of(me * TB, TB), TB)]
    rows = [jnp.where(me == j, mine, buf1[j]) for j in range(N_DEV)]
    m = functools.reduce(jnp.maximum, [r[0:1] for r in rows])
    s = sum(r[1:2] * jnp.exp(r[0:1] - m) for r in rows)
    t = sum(r[2:3] for r in rows)
    own[...] = jnp.concatenate([m, 1.0 / s, w_ref[0:1, :] * (m + jnp.log(s) - t), jnp.zeros((5, TB), F32)], axis=0)
    src = lambda j: own
    copies += all_send(me, src, buf2, send2, recv2)
    all_wait(me, src, buf2, send2, recv2)
    for copy in copies:
        copy.wait_send()
    for j in range(N_DEV):
        o_ref[:, j * TB:(j + 1) * TB] = jnp.where(me == j, own[...], buf2[j])


def exchange_stats(st, w_own, cid):
    return pl.pallas_call(
        stats_body,
        in_specs=[VM, VM],
        out_specs=VM,
        out_shape=jax.ShapeDtypeStruct((8, CHUNK_TOK), F32),
        scratch_shapes=[
            pltpu.VMEM((N_DEV, 8, TB), F32), pltpu.VMEM((8, TB), F32), pltpu.VMEM((N_DEV, 8, TB), F32),
            pltpu.SemaphoreType.DMA((N_DEV,)), pltpu.SemaphoreType.DMA((N_DEV,)),
            pltpu.SemaphoreType.DMA((N_DEV,)), pltpu.SemaphoreType.DMA((N_DEV,)),
        ],
        compiler_params=pltpu.CompilerParams(collective_id=cid, has_side_effects=True),
        cost_estimate=pl.CostEstimate(flops=2 * 10**9, bytes_accessed=2**20, transcendentals=0),
        name='exchange_stats',
    )(st, w_own)


def pass1_body(z_ref, w_ref, tok_ref, e_ref, ms_ref, st_ref, z_s):
    load_packed(z_s, z_ref, TB)
    z = z_s[...]
    tokc = jnp.concatenate([tok_ref[...], jnp.zeros((120, TB), F32)], axis=0).T
    tgt = tokc[:, 0:1]
    lane = lax.broadcasted_iota(jnp.int32, (TB, 128), 1)
    ids = lax.broadcasted_iota(jnp.int32, (1, SW), 1).astype(F32)
    ms = jnp.zeros((TB, 128), F32)
    tl = jnp.zeros((TB, 1), F32)
    m_list, s_list = [], []
    for s in range(STRIPS):
        l = dot_nn(z, w_ref[:, s * SW:(s + 1) * SW])
        m = jnp.max(l, axis=1, keepdims=True)
        e = jnp.exp(l - m)
        e_ref[:, s * SW:(s + 1) * SW] = e
        s_list.append(jnp.sum(e, axis=1, keepdims=True))
        m_list.append(m)
        tl = tl + jnp.sum(jnp.where(ids == tgt - float(s * SW), l, 0.0), axis=1, keepdims=True)
        ms = jnp.where(lane == s, m, ms)
    m_all = functools.reduce(jnp.maximum, m_list)
    s_all = sum(sv * jnp.exp(mv - m_all) for sv, mv in zip(s_list, m_list))
    ms_ref[...] = ms
    st = jnp.where(lane == 0, m_all, jnp.where(lane == 1, s_all, jnp.where(lane == 2, tl, 0.0)))
    st_ref[...] = st.T[0:8, :]


def head_pass1(z_all, w, tok):
    return pl.pallas_call(
        pass1_body,
        grid=(N_DEV,),
        in_specs=[
            rows_spec(1, ZROWS, 128),
            whole(DIM, VLOC),
            lanes_spec(8, TB),
        ],
        out_specs=[
            rows_spec(TB, VLOC),
            rows_spec(TB, 128),
            lanes_spec(8, TB),
        ],
        out_shape=[
            jax.ShapeDtypeStruct((CHUNK_TOK, VLOC), F32),
            jax.ShapeDtypeStruct((CHUNK_TOK, 128), F32),
            jax.ShapeDtypeStruct((8, CHUNK_TOK), F32),
        ],
        scratch_shapes=[pltpu.VMEM((TB, DIM), BF)],
        compiler_params=pltpu.CompilerParams(vmem_limit_bytes=VMEM_LIMIT),
        cost_estimate=pl.CostEstimate(flops=2 * CHUNK_TOK * DIM * VLOC, bytes_accessed=4 * CHUNK_TOK * VLOC, transcendentals=CHUNK_TOK * VLOC),
        name='head_pass1',
    )(z_all, w, tok)


def pass2_body(has_acc, *refs):
    if has_acc:
        z_ref, w_ref, tok_ref, res_ref, e_ref, ms_ref, acc_ref, dz_ref, gw_ref, z_s, q_s = refs
    else:
        z_ref, w_ref, tok_ref, res_ref, e_ref, ms_ref, dz_ref, gw_ref, z_s, q_s = refs
        acc_ref = None

    @pl.when(pl.program_id(0) == 0)
    def _():
        if has_acc:
            gw_ref[...] = acc_ref[...]
        else:
            gw_ref[...] = jnp.zeros_like(gw_ref)

    load_packed(z_s, z_ref, TB)
    z = z_s[...]
    tokc = jnp.concatenate([tok_ref[...], res_ref[...], jnp.zeros((112, TB), F32)], axis=0).T
    tgt, w_tok, m_glob, s_inv = (tokc[:, i:i + 1] for i in (0, 1, 8, 9))
    ids = lax.broadcasted_iota(jnp.int32, (1, SW), 1).astype(F32)
    for s in range(STRIPS):
        cols = slice(s * SW, (s + 1) * SW)
        scale = jnp.exp(ms_ref[:, s:s + 1] - m_glob) * s_inv
        p = e_ref[:, cols] * scale
        p = jnp.where(ids == tgt - float(s * SW), p - 1.0, p)
        q = (w_tok * p).astype(BF)
        q_s[:, cols] = q
        gw_ref[:, cols] += dot_tn(z, q)
    dz = dot_nt(q_s[...], w_ref[...])
    store_packed(dz_ref, dz, TB)


def head_pass2(z_all, w, tok, res, e, ms, acc):
    in_specs = [
        rows_spec(1, ZROWS, 128),
        whole(DIM, VLOC),
        lanes_spec(8, TB),
        lanes_spec(8, TB),
        rows_spec(TB, VLOC),
        rows_spec(TB, 128),
    ]
    args = [z_all, w, tok, res, e, ms]
    if acc is not None:
        in_specs.append(pl.BlockSpec((DIM, VLOC), lambda i: (0, 0), pipeline_mode=pl.Buffered(1)))
        args.append(acc)
    return pl.pallas_call(
        functools.partial(pass2_body, acc is not None),
        grid=(N_DEV,),
        in_specs=in_specs,
        out_specs=[
            rows_spec(1, ZROWS, 128),
            pl.BlockSpec((DIM, VLOC), lambda i: (0, 0), pipeline_mode=pl.Buffered(1)),
        ],
        out_shape=[
            jax.ShapeDtypeStruct((N_DEV, ZROWS, 128), F32),
            jax.ShapeDtypeStruct((DIM, VLOC), F32),
        ],
        scratch_shapes=[pltpu.VMEM((TB, DIM), BF), pltpu.VMEM((TB, VLOC), BF)],
        compiler_params=pltpu.CompilerParams(vmem_limit_bytes=VMEM_LIMIT),
        cost_estimate=pl.CostEstimate(flops=4 * CHUNK_TOK * DIM * VLOC, bytes_accessed=4 * CHUNK_TOK * VLOC, transcendentals=0),
        name='head_pass2',
    )(*args)


BT = 512


def bwd_body(top, off, *refs):
    if top:
        h_ref, p_ref, t_ref, d0_ref, d1_ref, go_ref, buf_ref, *scratch = refs
    else:
        h_ref, p_ref, g_ref, buf_in, go_ref, buf_ref, *scratch = refs
    _, wg_ref, wu_ref, wd_ref, n_s, k_s, a_s, du_s, dv_s, pk_s, sem = scratch
    unpack_weights(p_ref, 0, wg_ref, wu_ref, wd_ref)

    for i in range(TOK // BT):
        rows = slice(i * BT, (i + 1) * BT)
        h = h_ref[rows, :].astype(F32)
        r = inv_rms_of(h)
        n = (h * r).astype(BF)
        if top:
            g = norm_grad(t_ref[rows, :].astype(F32), unpack_rows((d0_ref, d1_ref)[i], TB))
        else:
            g = g_ref[rows, :]
        k = g.astype(BF)
        u = dot_nn(n, wg_ref[...])
        v = dot_nn(n, wu_ref[...])
        e = dot_nt(k, wd_ref[...])
        sg = jax.nn.sigmoid(u)
        us = u * sg
        a_s[rows, :] = (us * v).astype(BF)
        du = (e * v * sg * (1.0 + u * (1.0 - sg))).astype(BF)
        dv = (e * us).astype(BF)
        n_s[rows, :] = n
        k_s[rows, :] = k
        du_s[rows, :] = du
        dv_s[rows, :] = dv
        dn = dot_nt(du, wg_ref[...]) + dot_nt(dv, wu_ref[...])
        go_ref[rows, :] = (g + r * dn - h * (r * r * r) * jnp.mean(h * dn, axis=-1, keepdims=True)).astype(go_ref.dtype)

    n = n_s[...]
    k = k_s[...]
    for c in range(6):
        gg = dot_tn(n, du_s[:, c * 256:(c + 1) * 256])
        gu = dot_tn(n, dv_s[:, c * 256:(c + 1) * 256])
        for j in range(2):
            base = (2 * c + j) * 72
            for d in range(N_DEV):
                pk_s[d, base:base + 36, :] = gg[36 * d:36 * d + 36, j * 128:(j + 1) * 128]
                pk_s[d, base + 36:base + 72, :] = gu[36 * d:36 * d + 36, j * 128:(j + 1) * 128]
    copy_a = pltpu.make_async_copy(pk_s.at[:, pl.ds(0, 864), :], buf_ref.at[:, pl.ds(off, 864), :], sem.at[0])
    copy_a.start()
    for c in range(4):
        gd = dot_tn(a_s[:, c * 384:(c + 1) * 384], k)
        for j in range(4):
            d = c * 4 + j
            x = gd[96 * j:96 * j + 96, :]
            for b in range(4):
                pk_s[d, 864 + 96 * b:864 + 96 * b + 96, :] = x[:, 128 * b:128 * b + 128]
            pk_s[d, 1248:1296, :] = jnp.concatenate([x[:48, 512:], x[48:, 512:]], axis=1)
    copy_b = pltpu.make_async_copy(pk_s.at[:, pl.ds(864, 432), :], buf_ref.at[:, pl.ds(off + 864, 432), :], sem.at[1])
    copy_b.start()
    copy_a.wait()
    copy_b.wait()


def block_backward(h, packs, wslot, g_args, buf, slot, slots, out_dtype):
    top = len(g_args) == 3
    args = [h, packs, *g_args]
    in_specs = [whole(TOK, DIM), pl.BlockSpec((N_DEV, 1, PROWS, 128), lambda i: (0, wslot, 0, 0))]
    in_specs += [whole(*x.shape) for x in g_args]
    aliases = {}
    if not top:
        args.append(jnp.zeros((8, 128), F32) if buf is None else buf)
        in_specs.append(HB)
        aliases = {} if buf is None else {3: 1}
    return pl.pallas_call(
        functools.partial(bwd_body, top, slot * PROWS),
        grid=(1,),
        in_specs=in_specs,
        out_specs=[whole(TOK, DIM), HB],
        out_shape=[jax.ShapeDtypeStruct((TOK, DIM), out_dtype), jax.ShapeDtypeStruct((N_DEV, slots * PROWS, 128), F32)],
        scratch_shapes=[pltpu.SMEM((1,), jnp.int32)] + W_SCRATCH + [
            pltpu.VMEM((TOK, DIM), BF), pltpu.VMEM((TOK, DIM), BF), pltpu.VMEM((TOK, FFN), BF),
            pltpu.VMEM((TOK, FFN), BF), pltpu.VMEM((TOK, FFN), BF), pltpu.VMEM((N_DEV, PROWS, 128), F32),
            pltpu.SemaphoreType.DMA((2,)),
        ],
        input_output_aliases=aliases,
        compiler_params=pltpu.CompilerParams(vmem_limit_bytes=VMEM_LIMIT),
        cost_estimate=pl.CostEstimate(flops=16 * TOK * DIM * FFN, bytes_accessed=24 * 2**20, transcendentals=TOK * FFN),
        name='block_backward',
    )(*args)


def unpack_body(has_prev, p_ref, *refs):
    gg_ref, gu_ref, gd_ref = refs[3:] if has_prev else refs
    for c in range(12):
        gg_ref[0, :, c * 128:(c + 1) * 128] = p_ref[c * 72:c * 72 + 36, :]
        gu_ref[0, :, c * 128:(c + 1) * 128] = p_ref[c * 72 + 36:c * 72 + 72, :]
    for b in range(4):
        gd_ref[0, :, b * 128:(b + 1) * 128] = p_ref[864 + 96 * b:864 + 96 * b + 96, :]
    tail = p_ref[1248:1296, :]
    gd_ref[0, 0:48, 512:576] = tail[:, :64]
    gd_ref[0, 48:96, 512:576] = tail[:, 64:]


def unpack_grads(packed, group, prev):
    prev = list(prev or ())
    back = lambda i: (group[0] - i, 0, 0)
    return pl.pallas_call(
        functools.partial(unpack_body, bool(prev)),
        grid=(len(group),),
        in_specs=[rows_spec(PROWS, 128)] + [HB] * len(prev),
        out_specs=[
            pl.BlockSpec((1, 36, FFN), back),
            pl.BlockSpec((1, 36, FFN), back),
            pl.BlockSpec((1, 96, DIM), back),
        ],
        out_shape=[
            jax.ShapeDtypeStruct((LAYERS, 36, FFN), F32),
            jax.ShapeDtypeStruct((LAYERS, 36, FFN), F32),
            jax.ShapeDtypeStruct((LAYERS, 96, DIM), F32),
        ],
        input_output_aliases={1 + i: i for i in range(len(prev))},
        name='unpack_grads',
    )(packed, *prev)


def pack_body(wg_ref, wu_ref, wd_ref, p_ref):
    for c in range(12):
        p_ref[0, c * 72:c * 72 + 36, :] = wg_ref[0, :, c * 128:(c + 1) * 128]
        p_ref[0, c * 72 + 36:c * 72 + 72, :] = wu_ref[0, :, c * 128:(c + 1) * 128]
    for b in range(4):
        p_ref[0, 864 + 96 * b:864 + 96 * b + 96, :] = wd_ref[0, :, b * 128:(b + 1) * 128]
    p_ref[0, 1248:1296, :] = jnp.concatenate([wd_ref[0, 0:48, 512:576], wd_ref[0, 48:96, 512:576]], axis=1)


def pack_weights(wg, wu, wd):
    return pl.pallas_call(
        pack_body,
        grid=(LAYERS,),
        in_specs=[
            rows_spec(1, 36, FFN),
            rows_spec(1, 36, FFN),
            rows_spec(1, 96, DIM),
        ],
        out_specs=rows_spec(1, PROWS, 128),
        out_shape=jax.ShapeDtypeStruct((LAYERS, PROWS, 128), BF),
        name='pack_weights',
    )(wg, wu, wd)


def unpack_weights(p_ref, slot, wg_s, wu_s, wd_s):
    for d in range(N_DEV):
        for c in range(12):
            cols = slice(c * 128, (c + 1) * 128)
            wg_s[36 * d:36 * d + 36, cols] = p_ref[d, slot, c * 72:c * 72 + 36, :]
            wu_s[36 * d:36 * d + 36, cols] = p_ref[d, slot, c * 72 + 36:c * 72 + 72, :]
        for b in range(4):
            wd_s[96 * d:96 * d + 96, 128 * b:128 * b + 128] = p_ref[d, slot, 864 + 96 * b:864 + 96 * b + 96, :]
        tail = p_ref[d, slot, 1248:1296, :]
        wd_s[96 * d:96 * d + 48, 512:576] = tail[:, :64]
        wd_s[96 * d + 48:96 * d + 96, 512:576] = tail[:, 64:]


GROUPS = ((4, 3), (2, 1, 0))


def solution(mesh):
    def device_step(hidden, w_gate, w_up, w_down, w_out, targets, loss_mask):
        me = lax.axis_index(AXIS)
        gather = functools.partial(lax.all_gather, axis_name=AXIS)
        barrier = lax.optimization_barrier
        lab = jnp.concatenate([targets.astype(F32)[None], loss_mask.astype(F32)[None], jnp.zeros((6, TOK), F32)], axis=0)
        lab = gather_labels(lab)
        packs = pack_weights(w_gate, w_up, w_down)
        pack_top = gather(packs[4:])
        w_vocab = lax.all_to_all(w_out.reshape(36, N_DEV, VLOC), AXIS, 1, 0).reshape(DIM, VLOC)
        pack_top, w_vocab, lab = barrier((pack_top, w_vocab, lab))
        t, z_packed = top_forward(hidden[4], pack_top)

        mask = lab[:, 1, :]
        w_tok = mask / jnp.sum(mask)
        tgt = lab[:, 0, :] - (me * VLOC).astype(F32)
        w_own = lax.dynamic_slice(w_tok, (me, 0), (1, TOK))

        z_all = [gather(z_packed[c]) for c in range(CHUNKS)]
        rest = gather(packs[:4])
        acc, loss, dz_own = None, jnp.zeros((), F32), []
        for c in range(CHUNKS):
            sl = slice(c * TB, (c + 1) * TB)
            zero = jnp.zeros((6, CHUNK_TOK), F32)
            tok = jnp.concatenate([tgt[:, sl].reshape(1, CHUNK_TOK), w_tok[:, sl].reshape(1, CHUNK_TOK), zero], axis=0)
            if c == 1:
                tok, acc, rest = barrier((tok, acc, rest))
            e, ms, st = head_pass1(z_all[c], w_vocab, tok)
            res = exchange_stats(st, w_own[:, sl], 2 + c)
            loss = loss + jnp.sum(res[2])
            dz, acc = head_pass2(z_all[c], w_vocab, tok, res, e, ms, acc)
            if c == 1:
                dz, dz_own[0] = barrier((dz, dz_own[0]))
            dz_own.append(lax.psum_scatter(dz, AXIS, scatter_dimension=0, tiled=False))
        acc, dz_own[1] = barrier((acc, dz_own[1]))
        grad_out = lax.all_to_all(acc.reshape(N_DEV, 36, VLOC), AXIS, 0, 1)

        g_args = [t, *dz_own]
        outs, red = None, None
        for group in GROUPS:
            buf = None
            for i, l in enumerate(group):
                pk, ws = (pack_top, 0) if l == 4 else (rest, l)
                g, buf = block_backward(hidden[l], pk, ws, g_args, buf, i, len(group), BF if l == 0 else F32)
                g_args = [g]
            if red is not None:
                buf, red, grad_out = barrier((buf, red, grad_out))
                outs = unpack_grads(red, GROUPS[0], None)
            red = lax.psum_scatter(buf, AXIS, scatter_dimension=0, tiled=False)
        grad_gate, grad_up, grad_down = unpack_grads(red, GROUPS[1], outs)
        grad_out = grad_out.reshape(36, VOCAB)
        return grad_gate, grad_up, grad_down, grad_out, g, loss

    stacked = P(None, AXIS, None)
    row = P(AXIS, None)
    return jax.shard_map(device_step, mesh=mesh, in_specs=(stacked, stacked, stacked, stacked, row, P(AXIS), P(AXIS)), out_specs=(stacked, stacked, stacked, row, row, P()), check_vma=False)
```

time: 1310 us -> 1090 us (0.83)
  waiting for transfers between devices: 520 us -> 387 us
  local copies, waits for them, and re-layouts: 175 us -> 68.9 us
  Pallas kernels: 494 us -> 587 us
  blocking collectives: 66.6 us -> 0 us
    pallas_call x9 -> x14, Pallas kernels: 301 us -> 388 us  [the longest x5 139 us: block_backward(): pl.pallas_call(functools.partial(bwd_body, top, slot * PROWS), grid=(1,),...]
    all_to_all x1, waiting for transfers between devices: 114 us -> 34.7 us  [device_step(): grad_out = lax.all_to_all(acc.reshape(N_DEV, 36, VLOC), AXIS, 0, 1)]
    all_gather x1 -> x0, blocking collectives: 66.6 us -> none  [device_step(): lab = gather(jnp.stack([targets, loss_mask]))]
    pmax x1 -> x0, waiting for transfers between devices: 65.3 us -> none  [device_step(): m_glob = lax.pmax(st[0:1], AXIS)]
    reduce_scatter x2, waiting for transfers between devices: 47.8 us -> 111 us  [device_step(): dz_own.append(lax.psum_scatter(dz, AXIS, scatter_dimension=0, tiled=False))]
    psum x1 -> x0, waiting for transfers between devices: 62.4 us -> none  [device_step(): lax.psum(jnp.concatenate([st[1:2] * jnp.exp(st[0:1] - m_glob), st[2:3]],...]
    unnamed x147 -> x32, local copies, waits for them, and re-layouts: 63.2 us -> 26.4 us
    reshape x10 -> x0, local copies, waits for them, and re-layouts: 30.2 us -> none  [the longest x5 15.1 us: unpack_weights(): wu = p[:, 432:864].reshape(DIM, FFN)]
  transfers between devices with their start and end apart: 12 -> 10, of which waited for: 8 -> 5; matrix products, arithmetic and copies ran while one was open for 11% -> 7% of each run, Pallas kernels for 20% -> 47%
where the time goes in v2:
time: 1090 us; the launch traced here: 1080 us
  Pallas kernels  587 us (54%)
  waiting for transfers between devices  387 us (36%)
  local copies, waits for them, and re-layouts  68.9 us (6%)
  between operations  17.1 us (2%)
    pallas_call x2, Pallas kernels, head_pass2(): pl.pallas_call(functools.partial(pass2_body, acc is not None), grid=(N_DE...  199 us
    reduce_scatter x2, waiting for transfers between devices, device_step(): red = lax.psum_scatter(buf, AXIS, scatter_dimension=0, tiled=False)  197 us
    pallas_call x5, Pallas kernels, block_backward(): pl.pallas_call(functools.partial(bwd_body, top, slot * PROWS), grid=(1,),...  139 us
    pallas_call x2, Pallas kernels, head_pass1(): pl.pallas_call(pass1_body, grid=(N_DEV,), in_specs=[rows_spec(1, ZROWS, 1...  124 us
    reduce_scatter x2, waiting for transfers between devices, device_step(): dz_own.append(lax.psum_scatter(dz, AXIS, scatter_dimension=0, tiled=False))  111 us
    pallas_call x1, Pallas kernels, gather_labels(): pl.pallas_call(labels_body, in_specs=[VM], out_specs=VM, out_shape=jax.Sh...  62.1 us
    all_gather x2, waiting for transfers between devices, device_step(): z_all = [gather(z_packed[c]) for c in range(CHUNKS)]  43.5 us
    pallas_call x2, Pallas kernels, exchange_stats(): pl.pallas_call(stats_body, in_specs=[VM, VM], out_specs=VM, out_shape=jax...  39.3 us
  transfers between devices with their start and end apart: 10, of which 5 were waited for; matrix products, arithmetic and copies ran while one was open for 7% of the time, Pallas kernels for 47%

profile of v2, /device:TPU:0, one launch (start us, length us, event | category | flops | bytes accessed | tf_op | source)
XLA Modules:
  0.0 1078.5 jit_solution(16856069208493406536)
XLA Ops:
  7.2 4.4 pack_weights.1
  13.4 4.3 copy.66
  18.1 3.9 copy.51
  22.0 5.3 all-to-all-start
  27.4 5.3 fusion
  34.9 62.1 %gather_labels.1 = f32[16,8,1024]{2,1,0:T(8,128)} custom-call(f32[8,1024]{1,0:T(8,128)} %maximum_maximum_fusion.2.x_ref), custom_call_target="tpu_custom_call" | custom-call | flops 2000000000 | bytes 1048576 | tf_op jit(solution)/shard_map/gather_labels/pallas_call | solution.py:168
  97.0 4.7 reshape_squeeze.3.w_ref.refs_1_
  101.7 13.0 %top_forward.1 = (bf16[1024,576]{1,0:T(8,128)(2,1)}, bf16[2,2304,128]{2,1,0:T(8,128)(2,1)}) custom-call(bf16[1024,576]{1,0:T(8,128)(2,1)} %bitcast.68, bf16[16,1,1296,128]{3,2,1,0:T(8,128)(2,1)} %bitcast.78), custom_call_target="tpu_custom_call" | custom-call | flops 5435817984 | bytes 10485760 | tf_op jit(solution)/shard_map/top_forward/pallas_call | solution.py:114
  114.7 2.5 fusion.1
  125.2 43.4 %all-gather.7.cloned.1.call-done.z_ref.refs_0_ = bf16[16,2304,128]{2,1,0:T(8,128)(2,1)} async-done(((bf16[1,2304,128]{2,1,0:T(8,128)(2,1)}), bf16[16,2304,128]{2,1,0:T(8,128)(2,1)}) %all-gather.7.cloned.1.call-update) | async-done | bytes 9437200 | tf_op jit(solution)/shard_map/all_gather | solution.py:515
  168.6 61.7 %head_pass1.2 = (f32[8192,3072]{1,0:T(8,128)}, f32[8192,128]{1,0:T(8,128)}, f32[8,8192]{1,0:T(8,128)}) custom-call(bf16[16,2304,128]{2,1,0:T(8,128)(2,1)} %all-gather.7.cloned.1.call-done.z_ref.refs_0_, bf16[576,3072]{1,0:T(8,128)(2,1)} %reshape_squeeze.3.w_ref.refs_1_, f32[8,8192]{1,0:T(8,128)} %get-tuple-element.133.tok_ref.refs_2_), custom_call_target="tpu_custom_call" | custom-call | flops 28991029248 | bytes 100663296 | tf_op jit(solution)/shard_map/head_pass1/pallas_call | solution.py:245
  230.2 20.2 %exchange_stats.2.refs_3_ = f32[8,8192]{1,0:T(8,128)} custom-call(f32[8,8192]{1,0:T(8,128)} %get-tuple-element.51.st_ref, f32[1,512]{1,0:T(1,128)} %get-tuple-element.132.w_ref), custom_call_target="tpu_custom_call" | custom-call | flops 2000000000 | bytes 1048576 | tf_op jit(solution)/shard_map/exchange_stats/pallas_call | solution.py:202
  250.4 98.3 %head_pass2.2 = (f32[16,2304,128]{2,1,0:T(8,128)}, f32[576,3072]{1,0:T(8,128)}) custom-call(bf16[16,2304,128]{2,1,0:T(8,128)(2,1)} %all-gather.7.cloned.1.call-done.z_ref.refs_0_, bf16[576,3072]{1,0:T(8,128)(2,1)} %reshape_squeeze.3.w_ref.refs_1_, f32[8,8192]{1,0:T(8,128)} %get-tuple-element.133.tok_ref.refs_2_, f32[8,8192]{1,0:T(8,128)} %exchange_stats.2.refs_3_, ...), custom_call_target="tpu_custom_call" | custom-call | flops 57982058496 | bytes 100663296 | tf_op jit(solution)/shard_map/head_pass2/pallas_call | solution.py:314
  349.1 61.9 %head_pass1.3 = (f32[8192,3072]{1,0:T(8,128)}, f32[8192,128]{1,0:T(8,128)}, f32[8,8192]{1,0:T(8,128)}) custom-call(bf16[16,2304,128]{2,1,0:T(8,128)(2,1)} %all-gather.9.cloned.1.call-done.z_ref.refs_0_, bf16[576,3072]{1,0:T(8,128)(2,1)} %reshape_squeeze.3.w_ref.refs_1_, f32[8,8192]{1,0:T(8,128)} %get-tuple-element.57.tok_ref.refs_2_), custom_call_target="tpu_custom_call" | custom-call | flops 28991029248 | bytes 100663296 | tf_op jit(solution)/shard_map/head_pass1/pallas_call | solution.py:245
  411.0 19.1 %exchange_stats.3.refs_3_ = f32[8,8192]{1,0:T(8,128)} custom-call(f32[8,8192]{1,0:T(8,128)} %get-tuple-element.58.st_ref, f32[1,512]{1,0:T(1,128)} %get-tuple-element.131.w_ref), custom_call_target="tpu_custom_call" | custom-call | flops 2000000000 | bytes 1048576 | tf_op jit(solution)/shard_map/exchange_stats/pallas_call | solution.py:202
  430.1 100.2 %head_pass2.3 = (f32[16,2304,128]{2,1,0:T(8,128)}, f32[576,3072]{1,0:T(8,128)}) custom-call(bf16[16,2304,128]{2,1,0:T(8,128)(2,1)} %all-gather.9.cloned.1.call-done.z_ref.refs_0_, bf16[576,3072]{1,0:T(8,128)(2,1)} %reshape_squeeze.3.w_ref.refs_1_, f32[8,8192]{1,0:T(8,128)} %get-tuple-element.57.tok_ref.refs_2_, f32[8,8192]{1,0:T(8,128)} %exchange_stats.3.refs_3_, ...), custom_call_target="tpu_custom_call" | custom-call | flops 57982058496 | bytes 100663296 | tf_op jit(solution)/shard_map/head_pass2/pallas_call | solution.py:314
  533.2 111.2 %reduce-scatter.7.cloned.1.call-done = f32[1,2304,128]{2,1,0:T(8,128)} async-done(((f32[16,2304,128]{2,1,0:T(8,128)}), f32[1,2304,128]{2,1,0:T(8,128)}) %reduce-scatter.7.cloned.1.call-update) | async-done | bytes 1179664 | tf_op jit(solution)/shard_map/reduce_scatter | solution.py:530
  644.4 28.5 %block_backward.5 = (f32[1024,576]{1,0:T(8,128)}, f32[16,2592,128]{2,1,0:T(8,128)}) custom-call(bf16[1024,576]{1,0:T(8,128)(2,1)} %bitcast.69, bf16[16,1,1296,128]{3,2,1,0:T(8,128)(2,1)} %bitcast.79, bf16[1024,576]{1,0:T(8,128)(2,1)} %get-tuple-element.56.refs_2_, f32[2304,128]{1,0:T(8,128)} %bitcast.80, f32[2304,128]{1,0:T(8,128)} %bitcast.81), custom_call_target="tpu_custom_call" | custom-call | flops 14495514624 | bytes 25165824 | tf_op jit(solution)/shard_map/block_backward/pallas_call | solution.py:405
  672.9 27.7 %block_backward.6 = (f32[1024,576]{1,0:T(8,128)}, f32[16,2592,128]{2,1,0:T(8,128)}) custom-call(bf16[1024,576]{1,0:T(8,128)(2,1)} %bitcast.70, bf16[16,4,1296,128]{3,2,1,0:T(8,128)(2,1)} %bitcast.55, f32[1024,576]{1,0:T(8,128)} %get-tuple-element.68.refs_2_, f32[16,2592,128]{2,1,0:T(8,128)} %get-tuple-element.69.refs_3_), custom_call_target="tpu_custom_call", output_to_operand_aliasing={{1}: (3, {})} | custom-call | flops 14495514624 | bytes 25165824 | tf_op jit(solution)/shard_map/block_backward/pallas_call | solution.py:405
  700.6 11.5 %broadcast_in_dim_reshape.8 = f32[16,36,1,3072]{3,2,1,0:T(1,128)} reshape(f32[576,3072]{1,0:T(8,128)} %get-tuple-element.77) | data formatting | bytes 14155776 | tf_op jit(solution)/shard_map/broadcast_in_dim;reshape | solution.py:532
  712.1 3.6 all-to-all-start.1
  721.1 27.7 %block_backward.7 = (f32[1024,576]{1,0:T(8,128)}, f32[16,3888,128]{2,1,0:T(8,128)}) custom-call(bf16[1024,576]{1,0:T(8,128)(2,1)} %bitcast.71, bf16[16,4,1296,128]{3,2,1,0:T(8,128)(2,1)} %bitcast.56, f32[1024,576]{1,0:T(8,128)} %get-tuple-element.70.refs_2_, f32[8,128]{1,0:T(8,128)} %broadcast_in_dim.15.refs_3_), custom_call_target="tpu_custom_call" | custom-call | flops 14495514624 | bytes 25165824 | tf_op jit(solution)/shard_map/block_backward/pallas_call | solution.py:405
  748.8 27.8 %block_backward.8 = (f32[1024,576]{1,0:T(8,128)}, f32[16,3888,128]{2,1,0:T(8,128)}) custom-call(bf16[1024,576]{1,0:T(8,128)(2,1)} %bitcast.64, bf16[16,4,1296,128]{3,2,1,0:T(8,128)(2,1)} %bitcast.57, f32[1024,576]{1,0:T(8,128)} %get-tuple-element.71.refs_2_, f32[16,3888,128]{2,1,0:T(8,128)} %get-tuple-element.72.refs_3_), custom_call_target="tpu_custom_call", output_to_operand_aliasing={{1}: (3, {})} | custom-call | flops 14495514624 | bytes 25165824 | tf_op jit(solution)/shard_map/block_backward/pallas_call | solution.py:405
  776.6 27.8 %block_backward.9 = (bf16[1024,576]{1,0:T(8,128)(2,1)}, f32[16,3888,128]{2,1,0:T(8,128)}) custom-call(bf16[1024,576]{1,0:T(8,128)(2,1)} %bitcast.63, bf16[16,4,1296,128]{3,2,1,0:T(8,128)(2,1)} %bitcast.58, f32[1024,576]{1,0:T(8,128)} %get-tuple-element.73.refs_2_, f32[16,3888,128]{2,1,0:T(8,128)} %get-tuple-element.74.refs_3_), custom_call_target="tpu_custom_call", output_to_operand_aliasing={{1}: (3, {})} | custom-call | flops 14495514624 | bytes 25165824 | tf_op jit(solution)/shard_map/block_backward/pallas_call | solution.py:405
  804.4 34.7 %all-to-all-done.1 = f32[16,36,1,3072]{3,2,1,0:T(1,128)} async-done(((f32[16,36,1,3072]{3,2,1,0:T(1,128)}), f32[16,36,1,3072]{3,2,1,0:T(1,128)}, u32[]{:S(2)}, u32[]{:S(2)}) %all-to-all-start.1) | async-done | bytes 7077920 | tf_op jit(solution)/shard_map/all_to_all | solution.py:532
  839.1 10.1 copy.75
  849.2 32.6 %reduce-scatter.9.cloned.1.call-done = f32[1,2592,128]{2,1,0:T(8,128)} async-done(((f32[16,2592,128]{2,1,0:T(8,128)}), f32[1,2592,128]{2,1,0:T(8,128)}) %reduce-scatter.9.cloned.1.call-update) | async-done | bytes 1327120 | tf_op jit(solution)/shard_map/reduce_scatter | solution.py:545
  887.9 2.4 unpack_grads.2
  890.3 3.9 pad.9
  894.2 7.7 copy.71
  901.9 164.8 %reduce-scatter.11.cloned.1.call-done = f32[1,3888,128]{2,1,0:T(8,128)} async-done(((f32[16,3888,128]{2,1,0:T(8,128)}), f32[1,3888,128]{2,1,0:T(8,128)}) %reduce-scatter.11.cloned.1.call-update) | async-done | bytes 1990672 | tf_op jit(solution)/shard_map/reduce_scatter | solution.py:545
  1066.7 3.7 unpack_grads.3
  (66 shorter events, 25.6 us)
Async XLA Ops:
  7.2 94.5 %all-gather.11.cloned.1.call-start = ((), (), s32[]{:S(2)}) async-start(), calls=%async_computation.12 | async-start | bytes 5640192 | tf_op jit(solution)/shard_map/all_gather | solution.py:505
  22.0 5.4 copy-start.6
  22.0 5.4 copy-start.7
  22.0 75.0 %all-to-all-start = ((bf16[1,36,16,3072]{3,1,0,2:T(8,128)(2,1)}), bf16[1,36,16,3072]{3,1,0,2:T(8,128)(2,1)}, u32[]{:S(2)}, u32[]{:S(2)}) async-start(bf16[1,36,16,3072]{3,1,0,2:T(8,128)(2,1)} %copy.51), calls=%async_computation | async-start | bytes 7864320 | tf_op jit(solution)/shard_map/all_to_all | solution.py:506
  27.3 141.2 %all-gather.7.cloned.1.call-start = ((), (), s32[]{:S(2)}) async-start(), calls=%async_computation.6 | async-start | bytes 10027008 | tf_op jit(solution)/shard_map/all_gather | solution.py:515
  114.7 2.6 copy-start
  117.2 231.8 %all-gather.13.cloned.1.call-start = ((), (), s32[]{:S(2)}) async-start(), calls=%async_computation.13 | async-start | bytes 22560768 | tf_op jit(solution)/shard_map/all_gather | solution.py:516
  118.5 230.6 %all-gather.9.cloned.1.call-start = ((), (), s32[]{:S(2)}) async-start(), calls=%async_computation.7 | async-start | bytes 10027008 | tf_op jit(solution)/shard_map/all_gather | solution.py:515
  119.1 411.2 %reduce-scatter.5.cloned.1.call-start = ((), (), s32[]{:S(2)}) async-start(), calls=%async_computation.8 | async-start | bytes 20054016 | tf_op jit(solution)/shard_map/reduce_scatter | solution.py:530
  348.8 295.6 %reduce-scatter.7.cloned.1.call-start = ((), (), s32[]{:S(2)}) async-start(), calls=%async_computation.9 | async-start | bytes 20054016 | tf_op jit(solution)/shard_map/reduce_scatter | solution.py:530
  530.3 1.3 copy-start.4
  530.3 351.5 %reduce-scatter.9.cloned.1.call-start = ((), (), s32[]{:S(2)}) async-start(), calls=%async_computation.10 | async-start | bytes 22560768 | tf_op jit(solution)/shard_map/reduce_scatter | solution.py:545
  712.1 3.6 copy-start.3
  712.1 127.0 %all-to-all-start.1 = ((f32[16,36,1,3072]{3,2,1,0:T(1,128)}), f32[16,36,1,3072]{3,2,1,0:T(1,128)}, u32[]{:S(2)}, u32[]{:S(2)}) async-start(f32[16,36,1,3072]{3,2,1,0:T(1,128)} %broadcast_in_dim_reshape.8), calls=%async_computation.4 | async-start | bytes 14155776 | tf_op jit(solution)/shard_map/all_to_all | solution.py:532
  715.7 1.5 copy-start.2
  715.7 3.0 copy-start.1
  715.7 351.0 %reduce-scatter.11.cloned.1.call-start = ((), (), s32[]{:S(2)}) async-start(), calls=%async_computation.11 | async-start | bytes 33841152 | tf_op jit(solution)/shard_map/reduce_scatter | solution.py:545
  881.8 4.7 copy-start.5
Sparse Core Ops, SparseCore 0:
  13.5 82.5 all-gather.10
  117.4 51.1 all-gather.6
  170.8 96.0 all-gather.12
  269.0 52.2 all-gather.8
  348.9 119.4 reduce-scatter.4
  530.5 113.8 reduce-scatter.6
  700.8 181.0 reduce-scatter.8
  886.9 179.7 reduce-scatter.10

commit v3 on v2

--- a/solution.py
+++ b/solution.py
@@ -17,16 +17,22 @@
 VOCAB = 49152
 VLOC = VOCAB // N_DEV
 TOKENS = TOK * N_DEV
-CHUNKS = 2
-TB = TOK // CHUNKS
-CHUNK_TOK = TB * N_DEV
-ZROWS = TB * 9 // 2
+SPLITS = ((0, 640), (640, 384))
 STRIPS = 4
 SW = VLOC // STRIPS
 PROWS = 1296
 BF = jnp.bfloat16
 F32 = jnp.float32
 MESH = pl.DeviceIdType.MESH
+LANE = 128
+D4 = 4 * LANE
+HL = LANE // 2
+Q = DIM // N_DEV
+Q2 = 2 * Q
+PD = FFN // N_DEV
+PH = PD // 2
+A0 = 12 * Q2
+TL0 = A0 + 4 * PD
 VMEM_LIMIT = 62 * 1024 * 1024
 
 
@@ -71,52 +77,56 @@
 def store_packed(ref, val, rows):
     half = rows // 2
     for c in range(4):
-        ref[0, c * rows:(c + 1) * rows, :] = val[:, c * 128:(c + 1) * 128]
-    ref[0, 4 * rows:4 * rows + half, :] = jnp.concatenate([val[:half, 512:], val[half:, 512:]], axis=1)
+        ref[0, c * rows:(c + 1) * rows, :] = val[:, c * LANE:(c + 1) * LANE]
+    ref[0, 4 * rows:4 * rows + half, :] = jnp.concatenate([val[:half, D4:], val[half:, D4:]], axis=1)
 
 
 def load_packed(dst, ref, rows):
     half = rows // 2
     for c in range(4):
-        dst[:, c * 128:(c + 1) * 128] = ref[0, c * rows:(c + 1) * rows, :]
+        dst[:, c * LANE:(c + 1) * LANE] = ref[0, c * rows:(c + 1) * rows, :]
     tail = ref[0, 4 * rows:4 * rows + half, :]
-    dst[0:half, 512:576] = tail[:, :64]
-    dst[half:rows, 512:576] = tail[:, 64:]
+    dst[0:half, D4:DIM] = tail[:, :HL]
+    dst[half:rows, D4:DIM] = tail[:, HL:]
 
 
 def unpack_rows(p, rows):
     half = rows // 2
     tail = p[4 * rows:]
-    tail = jnp.concatenate([tail[:, :64], tail[:, 64:]], axis=0)
+    tail = jnp.concatenate([tail[:, :HL], tail[:, HL:]], axis=0)
     return jnp.concatenate([p[c * rows:(c + 1) * rows] for c in range(4)] + [tail], axis=1)
 
 
 W_SCRATCH = [pltpu.VMEM((DIM, FFN), BF), pltpu.VMEM((DIM, FFN), BF), pltpu.VMEM((FFN, DIM), BF)]
 
 
-def fwd_body(h_ref, p_ref, t_ref, z_ref, wg_ref, wu_ref, wd_ref):
-    @pl.when(pl.program_id(0) == 0)
-    def _():
-        unpack_weights(p_ref, 0, wg_ref, wu_ref, wd_ref)
-
-    h = h_ref[...].astype(F32)
-    n = (h * inv_rms_of(h)).astype(BF)
-    u = dot_nn(n, wg_ref[...])
-    v = dot_nn(n, wu_ref[...])
-    a = (u * jax.nn.sigmoid(u) * v).astype(BF)
-    t = (h + dot_nn(a, wd_ref[...])).astype(BF)
-    t_ref[...] = t
-    t = t.astype(F32)
-    store_packed(z_ref, (t * inv_rms_of(t)).astype(BF), TB)
+def fwd_body(h_ref, p_ref, t_ref, z0_ref, z1_ref, wg_ref, wu_ref, wd_ref):
+    unpack_weights(p_ref, 0, wg_ref, wu_ref, wd_ref)
+    for (off, tb), z_ref in zip(SPLITS, (z0_ref, z1_ref)):
+        rows = slice(off, off + tb)
+        h = h_ref[rows, :].astype(F32)
+        n = (h * inv_rms_of(h)).astype(BF)
+        u = dot_nn(n, wg_ref[...])
+        v = dot_nn(n, wu_ref[...])
+        a = (u * jax.nn.sigmoid(u) * v).astype(BF)
+        t = (h + dot_nn(a, wd_ref[...])).astype(BF)
+        t_ref[rows, :] = t
+        t = t.astype(F32)
+        store_packed(z_ref, (t * inv_rms_of(t)).astype(BF), tb)
+
+
+def packed_rows(tb):
+    return tb * 9 // 2
 
 
 def top_forward(h, packs):
+    zs = [(1, packed_rows(tb), LANE) for _, tb in SPLITS]
     return pl.pallas_call(
         fwd_body,
-        grid=(CHUNKS,),
-        in_specs=[rows_spec(TB, DIM), whole(N_DEV, 1, PROWS, 128)],
-        out_specs=[rows_spec(TB, DIM), rows_spec(1, ZROWS, 128)],
-        out_shape=[jax.ShapeDtypeStruct((TOK, DIM), BF), jax.ShapeDtypeStruct((CHUNKS, ZROWS, 128), BF)],
+        grid=(1,),
+        in_specs=[whole(TOK, DIM), whole(N_DEV, 1, PROWS, LANE)],
+        out_specs=[whole(TOK, DIM)] + [whole(*z) for z in zs],
+        out_shape=[jax.ShapeDtypeStruct((TOK, DIM), BF)] + [jax.ShapeDtypeStruct(z, BF) for z in zs],
         scratch_shapes=W_SCRATCH,
         compiler_params=pltpu.CompilerParams(vmem_limit_bytes=VMEM_LIMIT),
         cost_estimate=pl.CostEstimate(flops=6 * TOK * DIM * FFN, bytes_accessed=10 * 2**20, transcendentals=TOK * FFN),
@@ -179,6 +189,7 @@
 
 def stats_body(st_ref, w_ref, o_ref, buf1, own, buf2, send1, recv1, send2, recv2):
     me = lax.axis_index(AXIS)
+    TB = w_ref.shape[1]
     peers_barrier(me)
     part = lambda j: st_ref.at[:, pl.ds(pl.multiple_of(j * TB, TB), TB)]
     copies = all_send(me, part, buf1, send1, recv1)
@@ -199,11 +210,12 @@
 
 
 def exchange_stats(st, w_own, cid):
+    TB = w_own.shape[1]
     return pl.pallas_call(
         stats_body,
         in_specs=[VM, VM],
         out_specs=VM,
-        out_shape=jax.ShapeDtypeStruct((8, CHUNK_TOK), F32),
+        out_shape=jax.ShapeDtypeStruct(st.shape, F32),
         scratch_shapes=[
             pltpu.VMEM((N_DEV, 8, TB), F32), pltpu.VMEM((8, TB), F32), pltpu.VMEM((N_DEV, 8, TB), F32),
             pltpu.SemaphoreType.DMA((N_DEV,)), pltpu.SemaphoreType.DMA((N_DEV,)),
@@ -216,13 +228,14 @@
 
 
 def pass1_body(z_ref, w_ref, tok_ref, e_ref, ms_ref, st_ref, z_s):
+    TB = z_s.shape[0]
     load_packed(z_s, z_ref, TB)
     z = z_s[...]
     tokc = jnp.concatenate([tok_ref[...], jnp.zeros((120, TB), F32)], axis=0).T
     tgt = tokc[:, 0:1]
-    lane = lax.broadcasted_iota(jnp.int32, (TB, 128), 1)
+    lane = lax.broadcasted_iota(jnp.int32, (TB, LANE), 1)
     ids = lax.broadcasted_iota(jnp.int32, (1, SW), 1).astype(F32)
-    ms = jnp.zeros((TB, 128), F32)
+    ms = jnp.zeros((TB, LANE), F32)
     tl = jnp.zeros((TB, 1), F32)
     m_list, s_list = [], []
     for s in range(STRIPS):
@@ -242,22 +255,25 @@
 
 
 def head_pass1(z_all, w, tok):
+    CHUNK_TOK = tok.shape[1]
+    TB = CHUNK_TOK // N_DEV
+    ZROWS = packed_rows(TB)
     return pl.pallas_call(
         pass1_body,
         grid=(N_DEV,),
         in_specs=[
-            rows_spec(1, ZROWS, 128),
+            rows_spec(1, ZROWS, LANE),
             whole(DIM, VLOC),
             lanes_spec(8, TB),
         ],
         out_specs=[
             rows_spec(TB, VLOC),
-            rows_spec(TB, 128),
+            rows_spec(TB, LANE),
             lanes_spec(8, TB),
         ],
         out_shape=[
             jax.ShapeDtypeStruct((CHUNK_TOK, VLOC), F32),
-            jax.ShapeDtypeStruct((CHUNK_TOK, 128), F32),
+            jax.ShapeDtypeStruct((CHUNK_TOK, LANE), F32),
             jax.ShapeDtypeStruct((8, CHUNK_TOK), F32),
         ],
         scratch_shapes=[pltpu.VMEM((TB, DIM), BF)],
@@ -281,6 +297,7 @@
         else:
             gw_ref[...] = jnp.zeros_like(gw_ref)
 
+    TB = z_s.shape[0]
     load_packed(z_s, z_ref, TB)
     z = z_s[...]
     tokc = jnp.concatenate([tok_ref[...], res_ref[...], jnp.zeros((112, TB), F32)], axis=0).T
@@ -299,13 +316,16 @@
 
 
 def head_pass2(z_all, w, tok, res, e, ms, acc):
+    CHUNK_TOK = tok.shape[1]
+    TB = CHUNK_TOK // N_DEV
+    ZROWS = packed_rows(TB)
     in_specs = [
-        rows_spec(1, ZROWS, 128),
+        rows_spec(1, ZROWS, LANE),
         whole(DIM, VLOC),
         lanes_spec(8, TB),
         lanes_spec(8, TB),
         rows_spec(TB, VLOC),
-        rows_spec(TB, 128),
+        rows_spec(TB, LANE),
     ]
     args = [z_all, w, tok, res, e, ms]
     if acc is not None:
@@ -316,11 +336,11 @@
         grid=(N_DEV,),
         in_specs=in_specs,
         out_specs=[
-            rows_spec(1, ZROWS, 128),
+            rows_spec(1, ZROWS, LANE),
             pl.BlockSpec((DIM, VLOC), lambda i: (0, 0), pipeline_mode=pl.Buffered(1)),
         ],
         out_shape=[
-            jax.ShapeDtypeStruct((N_DEV, ZROWS, 128), F32),
+            jax.ShapeDtypeStruct((N_DEV, ZROWS, LANE), F32),
             jax.ShapeDtypeStruct((DIM, VLOC), F32),
         ],
         scratch_shapes=[pltpu.VMEM((TB, DIM), BF), pltpu.VMEM((TB, VLOC), BF)],
@@ -328,9 +348,6 @@
         cost_estimate=pl.CostEstimate(flops=4 * CHUNK_TOK * DIM * VLOC, bytes_accessed=4 * CHUNK_TOK * VLOC, transcendentals=0),
         name='head_pass2',
     )(*args)
-
-
-BT = 512
 
 
 def bwd_body(top, off, *refs):
@@ -341,13 +358,13 @@
     _, wg_ref, wu_ref, wd_ref, n_s, k_s, a_s, du_s, dv_s, pk_s, sem = scratch
     unpack_weights(p_ref, 0, wg_ref, wu_ref, wd_ref)
 
-    for i in range(TOK // BT):
-        rows = slice(i * BT, (i + 1) * BT)
+    for i, (lo, tb) in enumerate(SPLITS):
+        rows = slice(lo, lo + tb)
         h = h_ref[rows, :].astype(F32)
         r = inv_rms_of(h)
         n = (h * r).astype(BF)
         if top:
-            g = norm_grad(t_ref[rows, :].astype(F32), unpack_rows((d0_ref, d1_ref)[i], TB))
+            g = norm_grad(t_ref[rows, :].astype(F32), unpack_rows((d0_ref, d1_ref)[i], tb))
         else:
             g = g_ref[rows, :]
         k = g.astype(BF)
@@ -372,21 +389,21 @@
         gg = dot_tn(n, du_s[:, c * 256:(c + 1) * 256])
         gu = dot_tn(n, dv_s[:, c * 256:(c + 1) * 256])
         for j in range(2):
-            base = (2 * c + j) * 72
+            base = (2 * c + j) * Q2
             for d in range(N_DEV):
-                pk_s[d, base:base + 36, :] = gg[36 * d:36 * d + 36, j * 128:(j + 1) * 128]
-                pk_s[d, base + 36:base + 72, :] = gu[36 * d:36 * d + 36, j * 128:(j + 1) * 128]
-    copy_a = pltpu.make_async_copy(pk_s.at[:, pl.ds(0, 864), :], buf_ref.at[:, pl.ds(off, 864), :], sem.at[0])
+                pk_s[d, base:base + Q, :] = gg[Q * d:Q * d + Q, j * LANE:(j + 1) * LANE]
+                pk_s[d, base + Q:base + Q2, :] = gu[Q * d:Q * d + Q, j * LANE:(j + 1) * LANE]
+    copy_a = pltpu.make_async_copy(pk_s.at[:, pl.ds(0, A0), :], buf_ref.at[:, pl.ds(off, A0), :], sem.at[0])
     copy_a.start()
     for c in range(4):
         gd = dot_tn(a_s[:, c * 384:(c + 1) * 384], k)
         for j in range(4):
             d = c * 4 + j
-            x = gd[96 * j:96 * j + 96, :]
+            x = gd[PD * j:PD * j + PD, :]
             for b in range(4):
-                pk_s[d, 864 + 96 * b:864 + 96 * b + 96, :] = x[:, 128 * b:128 * b + 128]
-            pk_s[d, 1248:1296, :] = jnp.concatenate([x[:48, 512:], x[48:, 512:]], axis=1)
-    copy_b = pltpu.make_async_copy(pk_s.at[:, pl.ds(864, 432), :], buf_ref.at[:, pl.ds(off + 864, 432), :], sem.at[1])
+                pk_s[d, A0 + PD * b:A0 + PD * b + PD, :] = x[:, LANE * b:LANE * b + LANE]
+            pk_s[d, TL0:1296, :] = jnp.concatenate([x[:PH, D4:], x[PH:, D4:]], axis=1)
+    copy_b = pltpu.make_async_copy(pk_s.at[:, pl.ds(A0, 432), :], buf_ref.at[:, pl.ds(off + A0, 432), :], sem.at[1])
     copy_b.start()
     copy_a.wait()
     copy_b.wait()
@@ -395,11 +412,11 @@
 def block_backward(h, packs, wslot, g_args, buf, slot, slots, out_dtype):
     top = len(g_args) == 3
     args = [h, packs, *g_args]
-    in_specs = [whole(TOK, DIM), pl.BlockSpec((N_DEV, 1, PROWS, 128), lambda i: (0, wslot, 0, 0))]
+    in_specs = [whole(TOK, DIM), pl.BlockSpec((N_DEV, 1, PROWS, LANE), lambda i: (0, wslot, 0, 0))]
     in_specs += [whole(*x.shape) for x in g_args]
     aliases = {}
     if not top:
-        args.append(jnp.zeros((8, 128), F32) if buf is None else buf)
+        args.append(jnp.zeros((8, LANE), F32) if buf is None else buf)
         in_specs.append(HB)
         aliases = {} if buf is None else {3: 1}
     return pl.pallas_call(
@@ -407,10 +424,10 @@
         grid=(1,),
         in_specs=in_specs,
         out_specs=[whole(TOK, DIM), HB],
-        out_shape=[jax.ShapeDtypeStruct((TOK, DIM), out_dtype), jax.ShapeDtypeStruct((N_DEV, slots * PROWS, 128), F32)],
+        out_shape=[jax.ShapeDtypeStruct((TOK, DIM), out_dtype), jax.ShapeDtypeStruct((N_DEV, slots * PROWS, LANE), F32)],
         scratch_shapes=[pltpu.SMEM((1,), jnp.int32)] + W_SCRATCH + [
             pltpu.VMEM((TOK, DIM), BF), pltpu.VMEM((TOK, DIM), BF), pltpu.VMEM((TOK, FFN), BF),
-            pltpu.VMEM((TOK, FFN), BF), pltpu.VMEM((TOK, FFN), BF), pltpu.VMEM((N_DEV, PROWS, 128), F32),
+            pltpu.VMEM((TOK, FFN), BF), pltpu.VMEM((TOK, FFN), BF), pltpu.VMEM((N_DEV, PROWS, LANE), F32),
             pltpu.SemaphoreType.DMA((2,)),
         ],
         input_output_aliases=aliases,
@@ -420,16 +437,115 @@
     )(*args)
 
 
+def cube_body(pieces, x_ref, o_ref, own, r0, r1, r2, r3, send, recv, local):
+    me = lax.axis_index(AXIS)
+    pos = [me // 8, me // 4 % 2, me // 2 % 2, me % 2]
+    weight = (8, 4, 2, 1)
+    mate = [me + w * (1 - 2 * p) for w, p in zip(weight, pos)]
+    sem = pltpu.get_barrier_semaphore()
+    for j in mate:
+        pl.semaphore_signal(sem, inc=1, device_id=(j,), device_id_type=MESH)
+    pl.semaphore_wait(sem, 4)
+    core = pos[3]
+    size = o_ref.shape[0] // (3 * pieces)
+    units = [(k, (k + 3 * p) * size) for p in range(pieces) for k in range(3)]
+
+    def pick(ref, k, stage, rows, flip):
+        index = [slice(None)] * 3
+        for j in range(stage):
+            d = (k + j) % 3
+            index[d] = pos[d]
+        d = (k + stage) % 3
+        index[d] = 1 - pos[d] if flip else pos[d]
+        return ref.at[(*index, rows)]
+
+    def landing(k, stage, rows):
+        return (r1.at[:, :, rows], r2.at[:, rows], r3.at[rows])[stage]
+
+    def first(u):
+        k, base = units[u]
+        rows = pl.ds(base, size)
+        out = pltpu.make_async_remote_copy(
+            src_ref=x_ref.at[:, :, :, 1 - core, rows], dst_ref=r0.at[:, :, :, rows], send_sem=send.at[0, u],
+            recv_sem=recv.at[0, u], device_id=(mate[3],), device_id_type=MESH)
+        return out, pltpu.make_async_copy(x_ref.at[:, :, :, core, rows], own.at[:, :, :, rows], local.at[u])
+
+    def later(u, stage):
+        k, base = units[u]
+        rows = pl.ds(base, size)
+        return pltpu.make_async_remote_copy(
+            src_ref=pick(own, k, stage, rows, True), dst_ref=landing(k, stage, rows), send_sem=send.at[stage + 1, u],
+            recv_sem=recv.at[stage + 1, u], device_id=(mate[(k + stage) % 3],), device_id_type=MESH)
+
+    def add(dst, src):
+        step = PH
+
+        def body(i, carry):
+            rows = pl.ds(pl.multiple_of(i * step, step), step)
+            lead = (slice(None),) * (len(dst.shape) - 2)
+            dst[(*lead, rows)] += src[(*lead, rows)]
+            return carry
+
+        lax.fori_loop(0, size // step, body, 0)
+
+    many = range(len(units))
+    for u in many:
+        for copy in first(u):
+            copy.start()
+    for stage in range(4):
+        for u in many:
+            k, base = units[u]
+            rows = pl.ds(base, size)
+            if stage == 0:
+                out, loc = first(u)
+                loc.wait()
+                out.wait_recv()
+                add(own.at[:, :, :, rows], r0.at[:, :, :, rows])
+            else:
+                later(u, stage - 1).wait_recv()
+                add(pick(own, k, stage - 1, rows, False), landing(k, stage - 1, rows))
+            if stage < 3:
+                if u > 0:
+                    later(u - 1, stage).start()
+                if u == many[-1]:
+                    later(u, stage).start()
+            else:
+                o_ref[rows, :] = own[(*pos[:3], rows)]
+    for u in many:
+        first(u)[0].wait_send()
+        for stage in range(3):
+            later(u, stage).wait_send()
+
+
+def cube_reduce_scatter(x, pieces, cid):
+    rows = x.shape[1]
+    units = 3 * pieces
+    return pl.pallas_call(
+        functools.partial(cube_body, pieces),
+        in_specs=[HB],
+        out_specs=VM,
+        out_shape=jax.ShapeDtypeStruct((rows, LANE), F32),
+        scratch_shapes=[
+            pltpu.VMEM((2, 2, 2, rows, LANE), F32), pltpu.VMEM((2, 2, 2, rows, LANE), F32), pltpu.VMEM((2, 2, rows, LANE), F32),
+            pltpu.VMEM((2, rows, LANE), F32), pltpu.VMEM((rows, LANE), F32),
+            pltpu.SemaphoreType.DMA((4, units)), pltpu.SemaphoreType.DMA((4, units)), pltpu.SemaphoreType.DMA((units,)),
+        ],
+        compiler_params=pltpu.CompilerParams(collective_id=cid, has_side_effects=True, vmem_limit_bytes=VMEM_LIMIT),
+        cost_estimate=pl.CostEstimate(flops=50 * 10**9, bytes_accessed=2**20, transcendentals=0),
+        name='cube_reduce_scatter',
+    )(x.reshape(2, 2, 2, 2, rows, LANE))
+
+
 def unpack_body(has_prev, p_ref, *refs):
     gg_ref, gu_ref, gd_ref = refs[3:] if has_prev else refs
     for c in range(12):
-        gg_ref[0, :, c * 128:(c + 1) * 128] = p_ref[c * 72:c * 72 + 36, :]
-        gu_ref[0, :, c * 128:(c + 1) * 128] = p_ref[c * 72 + 36:c * 72 + 72, :]
+        gg_ref[0, :, c * LANE:(c + 1) * LANE] = p_ref[c * Q2:c * Q2 + Q, :]
+        gu_ref[0, :, c * LANE:(c + 1) * LANE] = p_ref[c * Q2 + Q:c * Q2 + Q2, :]
     for b in range(4):
-        gd_ref[0, :, b * 128:(b + 1) * 128] = p_ref[864 + 96 * b:864 + 96 * b + 96, :]
-    tail = p_ref[1248:1296, :]
-    gd_ref[0, 0:48, 512:576] = tail[:, :64]
-    gd_ref[0, 48:96, 512:576] = tail[:, 64:]
+        gd_ref[0, :, b * LANE:(b + 1) * LANE] = p_ref[A0 + PD * b:A0 + PD * b + PD, :]
+    tail = p_ref[TL0:1296, :]
+    gd_ref[0, 0:PH, D4:DIM] = tail[:, :HL]
+    gd_ref[0, PH:PD, D4:DIM] = tail[:, HL:]
 
 
 def unpack_grads(packed, group, prev):
@@ -438,16 +554,16 @@
     return pl.pallas_call(
         functools.partial(unpack_body, bool(prev)),
         grid=(len(group),),
-        in_specs=[rows_spec(PROWS, 128)] + [HB] * len(prev),
+        in_specs=[rows_spec(PROWS, LANE)] + [HB] * len(prev),
         out_specs=[
-            pl.BlockSpec((1, 36, FFN), back),
-            pl.BlockSpec((1, 36, FFN), back),
-            pl.BlockSpec((1, 96, DIM), back),
+            pl.BlockSpec((1, Q, FFN), back),
+            pl.BlockSpec((1, Q, FFN), back),
+            pl.BlockSpec((1, PD, DIM), back),
         ],
         out_shape=[
-            jax.ShapeDtypeStruct((LAYERS, 36, FFN), F32),
-            jax.ShapeDtypeStruct((LAYERS, 36, FFN), F32),
-            jax.ShapeDtypeStruct((LAYERS, 96, DIM), F32),
+            jax.ShapeDtypeStruct((LAYERS, Q, FFN), F32),
+            jax.ShapeDtypeStruct((LAYERS, Q, FFN), F32),
+            jax.ShapeDtypeStruct((LAYERS, PD, DIM), F32),
         ],
         input_output_aliases={1 + i: i for i in range(len(prev))},
         name='unpack_grads',
@@ -456,11 +572,11 @@
 
 def pack_body(wg_ref, wu_ref, wd_ref, p_ref):
     for c in range(12):
-        p_ref[0, c * 72:c * 72 + 36, :] = wg_ref[0, :, c * 128:(c + 1) * 128]
-        p_ref[0, c * 72 + 36:c * 72 + 72, :] = wu_ref[0, :, c * 128:(c + 1) * 128]
+        p_ref[0, c * Q2:c * Q2 + Q, :] = wg_ref[0, :, c * LANE:(c + 1) * LANE]
+        p_ref[0, c * Q2 + Q:c * Q2 + Q2, :] = wu_ref[0, :, c * LANE:(c + 1) * LANE]
     for b in range(4):
-        p_ref[0, 864 + 96 * b:864 + 96 * b + 96, :] = wd_ref[0, :, b * 128:(b + 1) * 128]
-    p_ref[0, 1248:1296, :] = jnp.concatenate([wd_ref[0, 0:48, 512:576], wd_ref[0, 48:96, 512:576]], axis=1)
+        p_ref[0, A0 + PD * b:A0 + PD * b + PD, :] = wd_ref[0, :, b * LANE:(b + 1) * LANE]
+    p_ref[0, TL0:1296, :] = jnp.concatenate([wd_ref[0, 0:PH, D4:DIM], wd_ref[0, PH:PD, D4:DIM]], axis=1)
 
 
 def pack_weights(wg, wu, wd):
@@ -468,12 +584,12 @@
         pack_body,
         grid=(LAYERS,),
         in_specs=[
-            rows_spec(1, 36, FFN),
-            rows_spec(1, 36, FFN),
-            rows_spec(1, 96, DIM),
-        ],
-        out_specs=rows_spec(1, PROWS, 128),
-        out_shape=jax.ShapeDtypeStruct((LAYERS, PROWS, 128), BF),
+            rows_spec(1, Q, FFN),
+            rows_spec(1, Q, FFN),
+            rows_spec(1, PD, DIM),
+        ],
+        out_specs=rows_spec(1, PROWS, LANE),
+        out_shape=jax.ShapeDtypeStruct((LAYERS, PROWS, LANE), BF),
         name='pack_weights',
     )(wg, wu, wd)
 
@@ -481,14 +597,14 @@
 def unpack_weights(p_ref, slot, wg_s, wu_s, wd_s):
     for d in range(N_DEV):
         for c in range(12):
-            cols = slice(c * 128, (c + 1) * 128)
-            wg_s[36 * d:36 * d + 36, cols] = p_ref[d, slot, c * 72:c * 72 + 36, :]
-            wu_s[36 * d:36 * d + 36, cols] = p_ref[d, slot, c * 72 + 36:c * 72 + 72, :]
+            cols = slice(c * LANE, (c + 1) * LANE)
+            wg_s[Q * d:Q * d + Q, cols] = p_ref[d, slot, c * Q2:c * Q2 + Q, :]
+            wu_s[Q * d:Q * d + Q, cols] = p_ref[d, slot, c * Q2 + Q:c * Q2 + Q2, :]
         for b in range(4):
-            wd_s[96 * d:96 * d + 96, 128 * b:128 * b + 128] = p_ref[d, slot, 864 + 96 * b:864 + 96 * b + 96, :]
-        tail = p_ref[d, slot, 1248:1296, :]
-        wd_s[96 * d:96 * d + 48, 512:576] = tail[:, :64]
-        wd_s[96 * d + 48:96 * d + 96, 512:576] = tail[:, 64:]
+            wd_s[PD * d:PD * d + PD, LANE * b:LANE * b + LANE] = p_ref[d, slot, A0 + PD * b:A0 + PD * b + PD, :]
+        tail = p_ref[d, slot, TL0:1296, :]
+        wd_s[PD * d:PD * d + PH, D4:DIM] = tail[:, :HL]
+        wd_s[PD * d + PH:PD * d + PD, D4:DIM] = tail[:, HL:]
 
 
 GROUPS = ((4, 3), (2, 1, 0))
@@ -501,22 +617,25 @@
         barrier = lax.optimization_barrier
         lab = jnp.concatenate([targets.astype(F32)[None], loss_mask.astype(F32)[None], jnp.zeros((6, TOK), F32)], axis=0)
         lab = gather_labels(lab)
+        w_gate, lab = barrier((w_gate, lab))
         packs = pack_weights(w_gate, w_up, w_down)
         pack_top = gather(packs[4:])
-        w_vocab = lax.all_to_all(w_out.reshape(36, N_DEV, VLOC), AXIS, 1, 0).reshape(DIM, VLOC)
+        w_out, lab = barrier((w_out, lab))
+        w_vocab = lax.all_to_all(w_out.reshape(Q, N_DEV, VLOC), AXIS, 1, 0).reshape(DIM, VLOC)
         pack_top, w_vocab, lab = barrier((pack_top, w_vocab, lab))
-        t, z_packed = top_forward(hidden[4], pack_top)
+        t, *z_packed = top_forward(hidden[4], pack_top)
 
         mask = lab[:, 1, :]
         w_tok = mask / jnp.sum(mask)
         tgt = lab[:, 0, :] - (me * VLOC).astype(F32)
         w_own = lax.dynamic_slice(w_tok, (me, 0), (1, TOK))
 
-        z_all = [gather(z_packed[c]) for c in range(CHUNKS)]
+        z_all = [lax.all_gather(z, AXIS, tiled=True) for z in z_packed]
         rest = gather(packs[:4])
         acc, loss, dz_own = None, jnp.zeros((), F32), []
-        for c in range(CHUNKS):
-            sl = slice(c * TB, (c + 1) * TB)
+        for c, (lo, tb) in enumerate(SPLITS):
+            sl = slice(lo, lo + tb)
+            CHUNK_TOK = tb * N_DEV
             zero = jnp.zeros((6, CHUNK_TOK), F32)
             tok = jnp.concatenate([tgt[:, sl].reshape(1, CHUNK_TOK), w_tok[:, sl].reshape(1, CHUNK_TOK), zero], axis=0)
             if c == 1:
@@ -527,24 +646,27 @@
             dz, acc = head_pass2(z_all[c], w_vocab, tok, res, e, ms, acc)
             if c == 1:
                 dz, dz_own[0] = barrier((dz, dz_own[0]))
-            dz_own.append(lax.psum_scatter(dz, AXIS, scatter_dimension=0, tiled=False))
+                dz_own.append(cube_reduce_scatter(dz, 2, 4))
+            else:
+                dz_own.append(lax.psum_scatter(dz, AXIS, scatter_dimension=0, tiled=False))
         acc, dz_own[1] = barrier((acc, dz_own[1]))
-        grad_out = lax.all_to_all(acc.reshape(N_DEV, 36, VLOC), AXIS, 0, 1)
+        grad_out = lax.all_to_all(acc.reshape(N_DEV, Q, VLOC), AXIS, 0, 1)
 
         g_args = [t, *dz_own]
-        outs, red = None, None
+        bufs = []
         for group in GROUPS:
             buf = None
             for i, l in enumerate(group):
                 pk, ws = (pack_top, 0) if l == 4 else (rest, l)
                 g, buf = block_backward(hidden[l], pk, ws, g_args, buf, i, len(group), BF if l == 0 else F32)
                 g_args = [g]
-            if red is not None:
-                buf, red, grad_out = barrier((buf, red, grad_out))
-                outs = unpack_grads(red, GROUPS[0], None)
-            red = lax.psum_scatter(buf, AXIS, scatter_dimension=0, tiled=False)
-        grad_gate, grad_up, grad_down = unpack_grads(red, GROUPS[1], outs)
-        grad_out = grad_out.reshape(36, VOCAB)
+            bufs.append(buf)
+        red = lax.psum_scatter(bufs[0], AXIS, scatter_dimension=0, tiled=False)
+        red_low = cube_reduce_scatter(bufs[1], 3, 5)
+        red, grad_out, red_low = barrier((red, grad_out, red_low))
+        outs = unpack_grads(red, GROUPS[0], None)
+        grad_gate, grad_up, grad_down = unpack_grads(red_low, GROUPS[1], outs)
+        grad_out = grad_out.reshape(Q, VOCAB)
         return grad_gate, grad_up, grad_down, grad_out, g, loss
 
     stacked = P(None, AXIS, None)

time: 1090 us -> 992 us (0.910)
  waiting for transfers between devices: 387 us -> 109 us
  Pallas kernels: 587 us -> 773 us
    pallas_call x4 -> x6, Pallas kernels: 141 us -> 364 us  [the longest x2 225 us: cube_reduce_scatter(): pl.pallas_call(functools.partial(cube_body, pieces), in_specs=[HB], out_s...]
    reduce_scatter x2 -> x1, waiting for transfers between devices: 197 us -> 0.01 us  [device_step(): red = lax.psum_scatter(bufs[0], AXIS, scatter_dimension=0, tiled=False)]
    reduce_scatter x2 -> x1, waiting for transfers between devices: 111 us -> 0.01 us  [device_step(): dz_own.append(lax.psum_scatter(dz, AXIS, scatter_dimension=0, tiled=False))]
    pallas_call x1, Pallas kernels: 62.1 us -> 14.3 us  [gather_labels(): pl.pallas_call(labels_body, in_specs=[VM], out_specs=VM, out_shape=jax.Sh...]
    all_to_all x2, waiting for transfers between devices: 34.7 us -> 54.1 us  [the longest x1 54.1 us: device_step(): lax.all_to_all(w_out.reshape(Q, N_DEV, VLOC), AXIS, 1, 0).reshape(DIM, VLOC)]
    all_gather x2, waiting for transfers between devices: 43.5 us -> 55 us  [device_step(): z_all = [lax.all_gather(z, AXIS, tiled=True) for z in z_packed]]
    unnamed x32 -> x28, local copies, waits for them, and re-layouts: 26.4 us -> 27.8 us
  transfers between devices with their start and end apart: 10 -> 8, of which waited for: 5 -> 2; matrix products, arithmetic and copies ran while one was open for 7% -> 6% of each run, Pallas kernels for 47% -> 63%
where the time goes in v3:
time: 992 us; the launch traced here: 986 us
  Pallas kernels  773 us (78%)
  waiting for transfers between devices  109 us (11%)
  local copies, waits for them, and re-layouts  68.3 us (7%)
  between operations  17 us (2%)
  other arithmetic  10.6 us (1%)
    pallas_call x2, Pallas kernels, cube_reduce_scatter(): pl.pallas_call(functools.partial(cube_body, pieces), in_specs=[HB], out_s...  225 us
    pallas_call x2, Pallas kernels, head_pass2(): pl.pallas_call(functools.partial(pass2_body, acc is not None), grid=(N_DE...  209 us
    pallas_call x5, Pallas kernels, block_backward(): pl.pallas_call(functools.partial(bwd_body, top, slot * PROWS), grid=(1,),...  140 us
    pallas_call x2, Pallas kernels, head_pass1(): pl.pallas_call(pass1_body, grid=(N_DEV,), in_specs=[rows_spec(1, ZROWS, L...  122 us
    all_gather x2, waiting for transfers between devices, device_step(): z_all = [lax.all_gather(z, AXIS, tiled=True) for z in z_packed]  55 us
    all_to_all x1, waiting for transfers between devices, device_step(): lax.all_to_all(w_out.reshape(Q, N_DEV, VLOC), AXIS, 1, 0).reshape(DIM, VLOC)  54.1 us
    pallas_call x2, Pallas kernels, exchange_stats(): pl.pallas_call(stats_body, in_specs=[VM, VM], out_specs=VM, out_shape=jax...  40.3 us
    unnamed x28, local copies, waits for them, and re-layouts  27.8 us
  transfers between devices with their start and end apart: 8, of which 2 were waited for; matrix products, arithmetic and copies ran while one was open for 6% of the time, Pallas kernels for 63%

profile of v3, /device:TPU:0, one launch (start us, length us, event | category | flops | bytes accessed | tf_op | source)
XLA Modules:
  0.0 986.1 jit_solution(15261733397169473442)
XLA Ops:
  9.4 14.3 %gather_labels.1 = f32[16,8,1024]{2,1,0:T(8,128)} custom-call(f32[8,1024]{1,0:T(8,128)} %maximum_maximum_fusion.2.x_ref), custom_call_target="tpu_custom_call" | custom-call | flops 2000000000 | bytes 1048576 | tf_op jit(solution)/shard_map/gather_labels/pallas_call | solution.py:178
  23.6 4.5 pack_weights.1
  29.9 4.3 copy.66
  34.6 3.9 copy.51
  38.5 3.3 all-to-all-start
  42.2 5.3 fusion
  48.9 54.1 %all-to-all-done = bf16[1,36,16,3072]{3,1,0,2:T(8,128)(2,1)} async-done(((bf16[1,36,16,3072]{3,1,0,2:T(8,128)(2,1)}), bf16[1,36,16,3072]{3,1,0,2:T(8,128)(2,1)}, u32[]{:S(2)}, u32[]{:S(2)}) %all-to-all-start) | async-done | bytes 3538976 | tf_op jit(solution)/shard_map/all_to_all | solution.py:624
  103.0 4.7 reshape_squeeze.3.w_ref.refs_1_
  107.7 12.9 %top_forward.1 = (bf16[1024,576]{1,0:T(8,128)(2,1)}, bf16[1,2880,128]{2,1,0:T(8,128)(2,1)}, bf16[1,1728,128]{2,1,0:T(8,128)(2,1)}) custom-call(bf16[1024,576]{1,0:T(8,128)(2,1)} %bitcast.68, bf16[16,1,1296,128]{3,2,1,0:T(8,128)(2,1)} %bitcast.78), custom_call_target="tpu_custom_call" | custom-call | flops 5435817984 | bytes 10485760 | tf_op jit(solution)/shard_map/top_forward/pallas_call | solution.py:124
  123.7 1.9 slice_subtract_fusion
  127.5 55.0 %all-gather.7.cloned.1.call-done.z_ref.refs_0_ = bf16[16,2880,128]{2,1,0:T(8,128)(2,1)} async-done(((bf16[1,2880,128]{2,1,0:T(8,128)(2,1)}), bf16[16,2880,128]{2,1,0:T(8,128)(2,1)}) %all-gather.7.cloned.1.call-update) | async-done | bytes 11796496 | tf_op jit(solution)/shard_map/all_gather | solution.py:633
  182.5 75.1 %head_pass1.2 = (f32[10240,3072]{1,0:T(8,128)}, f32[10240,128]{1,0:T(8,128)}, f32[8,10240]{1,0:T(8,128)}) custom-call(bf16[16,2880,128]{2,1,0:T(8,128)(2,1)} %all-gather.7.cloned.1.call-done.z_ref.refs_0_, bf16[576,3072]{1,0:T(8,128)(2,1)} %reshape_squeeze.3.w_ref.refs_1_, f32[8,10240]{1,0:T(8,128)} %maximum_maximum_fusion.tok_ref.refs_2_), custom_call_target="tpu_custom_call" | custom-call | flops 36238786560 | bytes 125829120 | tf_op jit(solution)/shard_map/head_pass1/pallas_call | solution.py:261
  257.6 22.5 %exchange_stats.2.refs_3_ = f32[8,10240]{1,0:T(8,128)} custom-call(f32[8,10240]{1,0:T(8,128)} %get-tuple-element.60.st_ref, f32[1,640]{1,0:T(1,128)} %slice.74.w_ref), custom_call_target="tpu_custom_call" | custom-call | flops 2000000000 | bytes 1048576 | tf_op jit(solution)/shard_map/exchange_stats/pallas_call | solution.py:214
  280.1 122.1 %head_pass2.2 = (f32[16,2880,128]{2,1,0:T(8,128)}, f32[576,3072]{1,0:T(8,128)}) custom-call(bf16[16,2880,128]{2,1,0:T(8,128)(2,1)} %all-gather.7.cloned.1.call-done.z_ref.refs_0_, bf16[576,3072]{1,0:T(8,128)(2,1)} %reshape_squeeze.3.w_ref.refs_1_, f32[8,10240]{1,0:T(8,128)} %maximum_maximum_fusion.tok_ref.refs_2_, f32[8,10240]{1,0:T(8,128)} %exchange_stats.2.refs_3_, ...), custom_call_target="tpu_custom_call" | custom-call | flops 72477573120 | bytes 125829120 | tf_op jit(solution)/shard_map/head_pass2/pallas_call | solution.py:334
  406.3 46.5 %head_pass1.3 = (f32[6144,3072]{1,0:T(8,128)}, f32[6144,128]{1,0:T(8,128)}, f32[8,6144]{1,0:T(8,128)}) custom-call(bf16[16,1728,128]{2,1,0:T(8,128)(2,1)} %all-gather.9.cloned.1.call-done.z_ref.refs_0_, bf16[576,3072]{1,0:T(8,128)(2,1)} %reshape_squeeze.3.w_ref.refs_1_, f32[8,6144]{1,0:T(8,128)} %maximum_maximum_fusion.1.tok_ref.refs_2_), custom_call_target="tpu_custom_call" | custom-call | flops 21743271936 | bytes 75497472 | tf_op jit(solution)/shard_map/head_pass1/pallas_call | solution.py:261
  452.8 17.8 %exchange_stats.3.refs_3_ = f32[8,6144]{1,0:T(8,128)} custom-call(f32[8,6144]{1,0:T(8,128)} %get-tuple-element.68.st_ref, f32[1,384]{1,0:T(1,128)} %slice.76.w_ref), custom_call_target="tpu_custom_call" | custom-call | flops 2000000000 | bytes 1048576 | tf_op jit(solution)/shard_map/exchange_stats/pallas_call | solution.py:214
  470.6 86.6 %head_pass2.3 = (f32[16,1728,128]{2,1,0:T(8,128)}, f32[576,3072]{1,0:T(8,128)}) custom-call(bf16[16,1728,128]{2,1,0:T(8,128)(2,1)} %all-gather.9.cloned.1.call-done.z_ref.refs_0_, bf16[576,3072]{1,0:T(8,128)(2,1)} %reshape_squeeze.3.w_ref.refs_1_, f32[8,6144]{1,0:T(8,128)} %maximum_maximum_fusion.1.tok_ref.refs_2_, f32[8,6144]{1,0:T(8,128)} %exchange_stats.3.refs_3_, ...), custom_call_target="tpu_custom_call" | custom-call | flops 43486543872 | bytes 75497472 | tf_op jit(solution)/shard_map/head_pass2/pallas_call | solution.py:334
  557.2 57.8 %cube_reduce_scatter.2.refs_4_ = f32[1728,128]{1,0:T(8,128)} custom-call(f32[2,2,2,2,1728,128]{5,4,3,2,1,0:T(8,128)} %bitcast.81), custom_call_target="tpu_custom_call" | custom-call | flops 49999998976 | bytes 1048576 | tf_op jit(solution)/shard_map/cube_reduce_scatter/pallas_call | solution.py:523
  615.0 28.1 %block_backward.5 = (f32[1024,576]{1,0:T(8,128)}, f32[16,2592,128]{2,1,0:T(8,128)}) custom-call(bf16[1024,576]{1,0:T(8,128)(2,1)} %bitcast.69, bf16[16,1,1296,128]{3,2,1,0:T(8,128)(2,1)} %bitcast.79, bf16[1024,576]{1,0:T(8,128)(2,1)} %get-tuple-element.65.refs_2_, f32[2880,128]{1,0:T(8,128)} %bitcast.80, f32[1728,128]{1,0:T(8,128)} %cube_reduce_scatter.2.refs_4_), custom_call_target="tpu_custom_call" | custom-call | flops 14495514624 | bytes 25165824 | tf_op jit(solution)/shard_map/block_backward/pallas_call | solution.py:422
  643.1 28.1 %block_backward.6 = (f32[1024,576]{1,0:T(8,128)}, f32[16,2592,128]{2,1,0:T(8,128)}) custom-call(bf16[1024,576]{1,0:T(8,128)(2,1)} %bitcast.70, bf16[16,4,1296,128]{3,2,1,0:T(8,128)(2,1)} %bitcast.56, f32[1024,576]{1,0:T(8,128)} %get-tuple-element.78.refs_2_, f32[16,2592,128]{2,1,0:T(8,128)} %get-tuple-element.79.refs_3_), custom_call_target="tpu_custom_call", output_to_operand_aliasing={{1}: (3, {})} | custom-call | flops 14495514624 | bytes 25165824 | tf_op jit(solution)/shard_map/block_backward/pallas_call | solution.py:422
  681.3 11.5 %broadcast_in_dim_reshape.8 = f32[16,36,1,3072]{3,2,1,0:T(1,128)} reshape(f32[576,3072]{1,0:T(8,128)} %get-tuple-element.81) | data formatting | bytes 14155776 | tf_op jit(solution)/shard_map/broadcast_in_dim;reshape | solution.py:653
  692.8 3.6 all-to-all-start.1
  697.0 28.0 %block_backward.7 = (f32[1024,576]{1,0:T(8,128)}, f32[16,3888,128]{2,1,0:T(8,128)}) custom-call(bf16[1024,576]{1,0:T(8,128)(2,1)} %bitcast.71, bf16[16,4,1296,128]{3,2,1,0:T(8,128)(2,1)} %bitcast.57, f32[1024,576]{1,0:T(8,128)} %get-tuple-element.82.refs_2_, f32[8,128]{1,0:T(8,128)} %broadcast_in_dim.23.refs_3_), custom_call_target="tpu_custom_call" | custom-call | flops 14495514624 | bytes 25165824 | tf_op jit(solution)/shard_map/block_backward/pallas_call | solution.py:422
  725.1 28.1 %block_backward.8 = (f32[1024,576]{1,0:T(8,128)}, f32[16,3888,128]{2,1,0:T(8,128)}) custom-call(bf16[1024,576]{1,0:T(8,128)(2,1)} %bitcast.65, bf16[16,4,1296,128]{3,2,1,0:T(8,128)(2,1)} %bitcast.58, f32[1024,576]{1,0:T(8,128)} %get-tuple-element.83.refs_2_, f32[16,3888,128]{2,1,0:T(8,128)} %get-tuple-element.84.refs_3_), custom_call_target="tpu_custom_call", output_to_operand_aliasing={{1}: (3, {})} | custom-call | flops 14495514624 | bytes 25165824 | tf_op jit(solution)/shard_map/block_backward/pallas_call | solution.py:422
  753.2 27.8 %block_backward.9 = (bf16[1024,576]{1,0:T(8,128)(2,1)}, f32[16,3888,128]{2,1,0:T(8,128)}) custom-call(bf16[1024,576]{1,0:T(8,128)(2,1)} %bitcast.64, bf16[16,4,1296,128]{3,2,1,0:T(8,128)(2,1)} %bitcast.59, f32[1024,576]{1,0:T(8,128)} %get-tuple-element.85.refs_2_, f32[16,3888,128]{2,1,0:T(8,128)} %get-tuple-element.86.refs_3_), custom_call_target="tpu_custom_call", output_to_operand_aliasing={{1}: (3, {})} | custom-call | flops 14495514624 | bytes 25165824 | tf_op jit(solution)/shard_map/block_backward/pallas_call | solution.py:422
  781.0 2.4 copy.58
  783.4 167.0 %cube_reduce_scatter.3.p_ref = f32[3888,128]{1,0:T(8,128)} custom-call(f32[2,2,2,2,3888,128]{5,4,3,2,1,0:T(8,128)} %bitcast.55), custom_call_target="tpu_custom_call" | custom-call | flops 49999998976 | bytes 1048576 | tf_op jit(solution)/shard_map/cube_reduce_scatter/pallas_call | solution.py:523
  950.4 10.1 %copy.75 = f32[16,36,1,3072]{3,0,1,2:T(8,128)} copy(f32[16,36,1,3072]{3,2,1,0:T(1,128)} %all-to-all-done.1) | data formatting | bytes 14155776 | tf_op jit(solution)/shard_map/all_to_all | solution.py:653
  960.5 3.9 pad.9
  964.3 7.7 copy.71
  972.0 2.2 unpack_grads.2
  974.2 3.7 unpack_grads.3
  (59 shorter events, 24.5 us)
Async XLA Ops:
  7.2 100.6 %all-gather.11.cloned.1.call-start = ((), (), s32[]{:S(2)}) async-start(), calls=%async_computation.8 | async-start | bytes 5640192 | tf_op jit(solution)/shard_map/all_gather | solution.py:622
  38.5 64.6 %all-to-all-start = ((bf16[1,36,16,3072]{3,1,0,2:T(8,128)(2,1)}), bf16[1,36,16,3072]{3,1,0,2:T(8,128)(2,1)}, u32[]{:S(2)}, u32[]{:S(2)}) async-start(bf16[1,36,16,3072]{3,1,0,2:T(8,128)(2,1)} %copy.51), calls=%async_computation | async-start | bytes 7864320 | tf_op jit(solution)/shard_map/all_to_all | solution.py:624
  41.7 140.8 %all-gather.7.cloned.1.call-start = ((), (), s32[]{:S(2)}) async-start(), calls=%async_computation.4 | async-start | bytes 12533760 | tf_op jit(solution)/shard_map/all_gather | solution.py:633
  107.7 13.0 %copy-start = (bf16[5,1296,128]{2,1,0:T(8,128)(2,1)S(1)}, bf16[5,1296,128]{2,1,0:T(8,128)(2,1)}, u32[]{:S(2)}) copy-start(bf16[5,1296,128]{2,1,0:T(8,128)(2,1)} %pack_weights.1) | copy-start | bytes 4976644
  120.6 285.6 %all-gather.13.cloned.1.call-start = ((), (), s32[]{:S(2)}) async-start(), calls=%async_computation.9 | async-start | bytes 22560768 | tf_op jit(solution)/shard_map/all_gather | solution.py:634
  121.9 284.4 %all-gather.9.cloned.1.call-start = ((), (), s32[]{:S(2)}) async-start(), calls=%async_computation.5 | async-start | bytes 7520256 | tf_op jit(solution)/shard_map/all_gather | solution.py:633
  125.7 431.5 %reduce-scatter.3.cloned.1.call-start = ((), (), s32[]{:S(2)}) async-start(), calls=%async_computation.6 | async-start | bytes 25067520 | tf_op jit(solution)/shard_map/reduce_scatter | solution.py:651
  402.2 1.3 copy-start.4
  402.2 558.2 %reduce-scatter.5.cloned.1.call-start = ((), (), s32[]{:S(2)}) async-start(), calls=%async_computation.7 | async-start | bytes 22560768 | tf_op jit(solution)/shard_map/reduce_scatter | solution.py:664
  671.2 1.3 copy-start.3
  671.2 2.7 copy-start.2
  671.2 4.1 copy-start.1
  692.8 257.5 %all-to-all-start.1 = ((f32[16,36,1,3072]{3,2,1,0:T(1,128)}), f32[16,36,1,3072]{3,2,1,0:T(1,128)}, u32[]{:S(2)}, u32[]{:S(2)}) async-start(f32[16,36,1,3072]{3,2,1,0:T(1,128)} %broadcast_in_dim_reshape.8), calls=%async_computation.3 | async-start | bytes 14155776 | tf_op jit(solution)/shard_map/all_to_all | solution.py:653
Sparse Core Ops, SparseCore 0:
  30.0 75.2 all-gather.10
  120.8 61.6 all-gather.6
  184.7 97.4 all-gather.12
  284.3 44.6 all-gather.8
  402.3 136.9 reduce-scatter.2
  671.4 231.2 reduce-scatter.4

commit v4 on v3

--- a/solution.py
+++ b/solution.py
@@ -32,6 +32,7 @@
 PD = FFN // N_DEV
 PH = PD // 2
 A0 = 12 * Q2
+GROWS = VLOC // LANE * Q
 TL0 = A0 + 4 * PD
 VMEM_LIMIT = 62 * 1024 * 1024
 
@@ -162,29 +163,36 @@
         copy.wait_recv()
 
 
-def labels_body(x_ref, o_ref, buf, send_sem, recv_sem):
+def start_body(x_ref, w_ref, o_ref, wo_ref, buf, send_sem, recv_sem, send_w, recv_w, local):
     me = lax.axis_index(AXIS)
     peers_barrier(me)
     src = lambda j: x_ref
+    part = lambda j: w_ref.at[:, pl.ds(pl.multiple_of(j * VLOC, VLOC), VLOC)]
     copies = all_send(me, src, buf, send_sem, recv_sem)
+    copies += all_send(me, part, wo_ref, send_w, recv_w)
+    mine = pltpu.make_async_copy(part(me), wo_ref.at[me], local)
+    mine.start()
     all_wait(me, src, buf, send_sem, recv_sem)
+    for j in range(N_DEV):
+        o_ref[j] = jnp.where(me == j, x_ref[...], buf[j])
+    all_wait(me, part, wo_ref, send_w, recv_w)
+    mine.wait()
     for copy in copies:
         copy.wait_send()
-    for j in range(N_DEV):
-        o_ref[j] = jnp.where(me == j, x_ref[...], buf[j])
-
-
-def gather_labels(x):
-    return pl.pallas_call(
-        labels_body,
-        in_specs=[VM],
-        out_specs=VM,
-        out_shape=jax.ShapeDtypeStruct((N_DEV, 8, TOK), F32),
-        scratch_shapes=[pltpu.VMEM((N_DEV, 8, TOK), F32), pltpu.SemaphoreType.DMA((N_DEV,)), pltpu.SemaphoreType.DMA((N_DEV,))],
+
+
+def start_exchange(x, w):
+    sems = pltpu.SemaphoreType.DMA((N_DEV,))
+    return pl.pallas_call(
+        start_body,
+        in_specs=[VM, HB],
+        out_specs=[VM, HB],
+        out_shape=[jax.ShapeDtypeStruct((N_DEV, 8, TOK), F32), jax.ShapeDtypeStruct((N_DEV, Q, VLOC), BF)],
+        scratch_shapes=[pltpu.VMEM((N_DEV, 8, TOK), F32), sems, sems, sems, sems, pltpu.SemaphoreType.DMA],
         compiler_params=pltpu.CompilerParams(collective_id=1, has_side_effects=True),
-        cost_estimate=pl.CostEstimate(flops=2 * 10**9, bytes_accessed=2**20, transcendentals=0),
-        name='gather_labels',
-    )(x)
+        cost_estimate=pl.CostEstimate(flops=50 * 10**9, bytes_accessed=2**20, transcendentals=0),
+        name='start_exchange',
+    )(x, w)
 
 
 def stats_body(st_ref, w_ref, o_ref, buf1, own, buf2, send1, recv1, send2, recv2):
@@ -285,7 +293,7 @@
 
 def pass2_body(has_acc, *refs):
     if has_acc:
-        z_ref, w_ref, tok_ref, res_ref, e_ref, ms_ref, acc_ref, dz_ref, gw_ref, z_s, q_s = refs
+        z_ref, w_ref, tok_ref, res_ref, e_ref, ms_ref, acc_ref, dz_ref, pk_ref, z_s, q_s, gw_ref = refs
     else:
         z_ref, w_ref, tok_ref, res_ref, e_ref, ms_ref, dz_ref, gw_ref, z_s, q_s = refs
         acc_ref = None
@@ -313,6 +321,12 @@
         gw_ref[:, cols] += dot_tn(z, q)
     dz = dot_nt(q_s[...], w_ref[...])
     store_packed(dz_ref, dz, TB)
+    if has_acc:
+        @pl.when(pl.program_id(0) == N_DEV - 1)
+        def _():
+            for d in range(N_DEV):
+                for c in range(VLOC // LANE):
+                    pk_ref[d, c * Q:(c + 1) * Q, :] = gw_ref[Q * d:Q * d + Q, c * LANE:(c + 1) * LANE]
 
 
 def head_pass2(z_all, w, tok, res, e, ms, acc):
@@ -328,6 +342,7 @@
         rows_spec(TB, LANE),
     ]
     args = [z_all, w, tok, res, e, ms]
+    g_shape = (DIM, VLOC) if acc is None else (N_DEV, GROWS, LANE)
     if acc is not None:
         in_specs.append(pl.BlockSpec((DIM, VLOC), lambda i: (0, 0), pipeline_mode=pl.Buffered(1)))
         args.append(acc)
@@ -337,25 +352,48 @@
         in_specs=in_specs,
         out_specs=[
             rows_spec(1, ZROWS, LANE),
-            pl.BlockSpec((DIM, VLOC), lambda i: (0, 0), pipeline_mode=pl.Buffered(1)),
+            pl.BlockSpec(g_shape, lambda i: tuple(0 * d for d in g_shape), pipeline_mode=pl.Buffered(1)),
         ],
         out_shape=[
             jax.ShapeDtypeStruct((N_DEV, ZROWS, LANE), F32),
-            jax.ShapeDtypeStruct((DIM, VLOC), F32),
-        ],
-        scratch_shapes=[pltpu.VMEM((TB, DIM), BF), pltpu.VMEM((TB, VLOC), BF)],
+            jax.ShapeDtypeStruct(g_shape, F32),
+        ],
+        scratch_shapes=[pltpu.VMEM((TB, DIM), BF), pltpu.VMEM((TB, VLOC), BF)] + ([] if acc is None else [pltpu.VMEM((DIM, VLOC), F32)]),
         compiler_params=pltpu.CompilerParams(vmem_limit_bytes=VMEM_LIMIT),
         cost_estimate=pl.CostEstimate(flops=4 * CHUNK_TOK * DIM * VLOC, bytes_accessed=4 * CHUNK_TOK * VLOC, transcendentals=0),
         name='head_pass2',
     )(*args)
 
 
-def bwd_body(top, off, *refs):
+def bwd_body(top, off, masks, n_in, *refs):
+    h_ref, p_ref = refs[:2]
     if top:
-        h_ref, p_ref, t_ref, d0_ref, d1_ref, go_ref, buf_ref, *scratch = refs
+        t_ref, d0_ref, d1_ref = refs[2:5]
     else:
-        h_ref, p_ref, g_ref, buf_in, go_ref, buf_ref, *scratch = refs
-    _, wg_ref, wu_ref, wd_ref, n_s, k_s, a_s, du_s, dv_s, pk_s, sem = scratch
+        g_ref = refs[2]
+    go_ref, buf_ref = refs[n_in:n_in + 2]
+    scratch = refs[n_in + 2:]
+    moves = []
+    if masks:
+        me = lax.axis_index(AXIS)
+        pos = [me // w % 2 for w in (1, 2, 4, 8)]
+        gp_ref = refs[n_in - 1 if top else n_in - 2]
+        ga_ref, *scratch = scratch
+        *scratch, send, recv, local = scratch
+        barrier = pltpu.get_barrier_semaphore()
+        mates = [me + sum(2**b * (1 - 2 * pos[b]) for b in range(4) if m >> b & 1) for m in masks]
+        for j in mates:
+            pl.semaphore_signal(barrier, inc=1, device_id=(j,), device_id_type=MESH)
+        pl.semaphore_wait(barrier, len(masks))
+        for i, j in enumerate(mates):
+            moves.append(pltpu.make_async_remote_copy(
+                src_ref=gp_ref.at[j], dst_ref=ga_ref.at[me], send_sem=send.at[i], recv_sem=recv.at[i],
+                device_id=(j,), device_id_type=MESH))
+        if top:
+            moves.append(pltpu.make_async_copy(gp_ref.at[me], ga_ref.at[me], local))
+        for move in moves:
+            move.start()
+    wg_ref, wu_ref, wd_ref, n_s, k_s, a_s, du_s, dv_s, pk_s, sem = scratch
     unpack_weights(p_ref, 0, wg_ref, wu_ref, wd_ref)
 
     for i, (lo, tb) in enumerate(SPLITS):
@@ -407,34 +445,64 @@
     copy_b.start()
     copy_a.wait()
     copy_b.wait()
-
-
-def block_backward(h, packs, wslot, g_args, buf, slot, slots, out_dtype):
+    for move in moves:
+        move.wait()
+
+
+def block_backward(h, packs, wslot, g_args, buf, slot, slots, out_dtype, masks=(), moved=(), cid=None):
     top = len(g_args) == 3
     args = [h, packs, *g_args]
     in_specs = [whole(TOK, DIM), pl.BlockSpec((N_DEV, 1, PROWS, LANE), lambda i: (0, wslot, 0, 0))]
     in_specs += [whole(*x.shape) for x in g_args]
+    out_specs = [whole(TOK, DIM), HB]
+    out_shape = [jax.ShapeDtypeStruct((TOK, DIM), out_dtype), jax.ShapeDtypeStruct((N_DEV, slots * PROWS, LANE), F32)]
+    scratch = W_SCRATCH + [
+        pltpu.VMEM((TOK, DIM), BF), pltpu.VMEM((TOK, DIM), BF), pltpu.VMEM((TOK, FFN), BF),
+        pltpu.VMEM((TOK, FFN), BF), pltpu.VMEM((TOK, FFN), BF), pltpu.VMEM((N_DEV, PROWS, LANE), F32),
+        pltpu.SemaphoreType.DMA((2,)),
+    ]
     aliases = {}
-    if not top:
-        args.append(jnp.zeros((8, LANE), F32) if buf is None else buf)
+    if buf is not None:
+        aliases[len(args)] = 1
+        args.append(buf)
         in_specs.append(HB)
-        aliases = {} if buf is None else {3: 1}
-    return pl.pallas_call(
-        functools.partial(bwd_body, top, slot * PROWS),
+    if masks:
+        sems = pltpu.SemaphoreType.DMA((len(masks),))
+        scratch += [sems, sems, pltpu.SemaphoreType.DMA]
+        if len(moved) == 2:
+            aliases[len(args) + 1] = 2
+        args += moved
+        in_specs += [HB] * len(moved)
+        out_specs.append(HB)
+        out_shape.append(jax.ShapeDtypeStruct(moved[0].shape, F32))
+    return pl.pallas_call(
+        functools.partial(bwd_body, top, slot * PROWS, masks, len(args)),
         grid=(1,),
         in_specs=in_specs,
-        out_specs=[whole(TOK, DIM), HB],
-        out_shape=[jax.ShapeDtypeStruct((TOK, DIM), out_dtype), jax.ShapeDtypeStruct((N_DEV, slots * PROWS, LANE), F32)],
-        scratch_shapes=[pltpu.SMEM((1,), jnp.int32)] + W_SCRATCH + [
-            pltpu.VMEM((TOK, DIM), BF), pltpu.VMEM((TOK, DIM), BF), pltpu.VMEM((TOK, FFN), BF),
-            pltpu.VMEM((TOK, FFN), BF), pltpu.VMEM((TOK, FFN), BF), pltpu.VMEM((N_DEV, PROWS, LANE), F32),
-            pltpu.SemaphoreType.DMA((2,)),
-        ],
+        out_specs=out_specs,
+        out_shape=out_shape,
+        scratch_shapes=scratch,
         input_output_aliases=aliases,
-        compiler_params=pltpu.CompilerParams(vmem_limit_bytes=VMEM_LIMIT),
+        compiler_params=pltpu.CompilerParams(vmem_limit_bytes=VMEM_LIMIT, collective_id=cid, has_side_effects=bool(masks)),
         cost_estimate=pl.CostEstimate(flops=16 * TOK * DIM * FFN, bytes_accessed=24 * 2**20, transcendentals=TOK * FFN),
         name='block_backward',
     )(*args)
+
+
+def head_unpack_body(p_ref, o_ref):
+    for c in range(VLOC // LANE):
+        o_ref[:, c * LANE:(c + 1) * LANE] = p_ref[0, c * Q:(c + 1) * Q, :]
+
+
+def unpack_head(p):
+    return pl.pallas_call(
+        head_unpack_body,
+        grid=(N_DEV,),
+        in_specs=[rows_spec(1, GROWS, LANE)],
+        out_specs=lanes_spec(Q, VLOC),
+        out_shape=jax.ShapeDtypeStruct((Q, VOCAB), F32),
+        name='unpack_head',
+    )(p)
 
 
 def cube_body(pieces, x_ref, o_ref, own, r0, r1, r2, r3, send, recv, local):
@@ -616,13 +684,12 @@
         gather = functools.partial(lax.all_gather, axis_name=AXIS)
         barrier = lax.optimization_barrier
         lab = jnp.concatenate([targets.astype(F32)[None], loss_mask.astype(F32)[None], jnp.zeros((6, TOK), F32)], axis=0)
-        lab = gather_labels(lab)
-        w_gate, lab = barrier((w_gate, lab))
         packs = pack_weights(w_gate, w_up, w_down)
+        packs, lab = barrier((packs, lab))
         pack_top = gather(packs[4:])
-        w_out, lab = barrier((w_out, lab))
-        w_vocab = lax.all_to_all(w_out.reshape(Q, N_DEV, VLOC), AXIS, 1, 0).reshape(DIM, VLOC)
+        lab, w_vocab = start_exchange(lab, w_out)
         pack_top, w_vocab, lab = barrier((pack_top, w_vocab, lab))
+        w_vocab = w_vocab.reshape(DIM, VLOC)
         t, *z_packed = top_forward(hidden[4], pack_top)
 
         mask = lab[:, 1, :]
@@ -649,24 +716,27 @@
                 dz_own.append(cube_reduce_scatter(dz, 2, 4))
             else:
                 dz_own.append(lax.psum_scatter(dz, AXIS, scatter_dimension=0, tiled=False))
-        acc, dz_own[1] = barrier((acc, dz_own[1]))
-        grad_out = lax.all_to_all(acc.reshape(N_DEV, Q, VLOC), AXIS, 0, 1)
-
         g_args = [t, *dz_own]
-        bufs = []
+        bufs, moved = [], [acc]
         for group in GROUPS:
             buf = None
             for i, l in enumerate(group):
                 pk, ws = (pack_top, 0) if l == 4 else (rest, l)
-                g, buf = block_backward(hidden[l], pk, ws, g_args, buf, i, len(group), BF if l == 0 else F32)
+                args = (hidden[l], pk, ws, g_args, buf, i, len(group), BF if l == 0 else F32)
+                if l > 2:
+                    g, buf, got = block_backward(*args, tuple(range(2, 16, 2) if l == 4 else range(1, 16, 2)), moved, l + 3)
+                    moved.append(got)
+                else:
+                    g, buf = block_backward(*args)
                 g_args = [g]
             bufs.append(buf)
+        grad_out = unpack_head(moved[2])
         red = lax.psum_scatter(bufs[0], AXIS, scatter_dimension=0, tiled=False)
+        bufs[1], grad_out = barrier((bufs[1], grad_out))
         red_low = cube_reduce_scatter(bufs[1], 3, 5)
-        red, grad_out, red_low = barrier((red, grad_out, red_low))
+        red, red_low = barrier((red, red_low))
         outs = unpack_grads(red, GROUPS[0], None)
         grad_gate, grad_up, grad_down = unpack_grads(red_low, GROUPS[1], outs)
-        grad_out = grad_out.reshape(Q, VOCAB)
         return grad_gate, grad_up, grad_down, grad_out, g, loss
 
     stacked = P(None, AXIS, None)

time: 992 us -> 967 us (0.975)
  Pallas kernels: 773 us -> 848 us
  waiting for transfers between devices: 109 us -> 57 us
  local copies, waits for them, and re-layouts: 68.3 us -> 25.7 us
    pallas_call x6 -> x7, Pallas kernels: 154 us -> 279 us  [the longest x5 195 us: block_backward(): pl.pallas_call(functools.partial(bwd_body, top, slot * PROWS, masks, len(...]
    all_to_all x2 -> x0, waiting for transfers between devices: 54.1 us -> none  [the longest x1 54.1 us: device_step(): lax.all_to_all(w_out.reshape(Q, N_DEV, VLOC), AXIS, 1, 0).reshape(DIM, VLOC)]
    pallas_call x2, Pallas kernels: 225 us -> 173 us  [cube_reduce_scatter(): pl.pallas_call(functools.partial(cube_body, pieces), in_specs=[HB], out_s...]
    another operation x4 -> x0, local copies, waits for them, and re-layouts: 20.5 us -> none  [the longest x1 11.5 us: device_step(): grad_out = lax.all_to_all(acc.reshape(N_DEV, Q, VLOC), AXIS, 0, 1)]
    unnamed x28 -> x25, local copies, waits for them, and re-layouts: 27.8 us -> 11.7 us
    all_to_all x1 -> x0, local copies, waits for them, and re-layouts: 10.1 us -> none  [device_step(): grad_out = lax.all_to_all(acc.reshape(N_DEV, Q, VLOC), AXIS, 0, 1)]
  transfers between devices with their start and end apart: 8 -> 6, of which waited for: 2 -> 2; matrix products, arithmetic and copies ran while one was open for 6% -> 3% of each run, Pallas kernels for 63% -> 68%
where the time goes in v4:
time: 967 us; the launch traced here: 959 us
  Pallas kernels  848 us (88%)
  waiting for transfers between devices  57 us (6%)
  local copies, waits for them, and re-layouts  25.7 us (3%)
  between operations  16.9 us (2%)
  other arithmetic  10.6 us (1%)
    pallas_call x2, Pallas kernels, head_pass2(): pl.pallas_call(functools.partial(pass2_body, acc is not None), grid=(N_DE...  211 us
    pallas_call x5, Pallas kernels, block_backward(): pl.pallas_call(functools.partial(bwd_body, top, slot * PROWS, masks, len(...  195 us
    pallas_call x2, Pallas kernels, cube_reduce_scatter(): pl.pallas_call(functools.partial(cube_body, pieces), in_specs=[HB], out_s...  173 us
    pallas_call x2, Pallas kernels, head_pass1(): pl.pallas_call(pass1_body, grid=(N_DEV,), in_specs=[rows_spec(1, ZROWS, L...  122 us
    pallas_call x1, Pallas kernels, start_exchange(): pl.pallas_call(start_body, in_specs=[VM, HB], out_specs=[VM, HB], out_sha...  72.9 us
    all_gather x2, waiting for transfers between devices, device_step(): z_all = [lax.all_gather(z, AXIS, tiled=True) for z in z_packed]  51.7 us
    pallas_call x2, Pallas kernels, exchange_stats(): pl.pallas_call(stats_body, in_specs=[VM, VM], out_specs=VM, out_shape=jax...  40.3 us
  transfers between devices with their start and end apart: 6, of which 2 were waited for; matrix products, arithmetic and copies ran while one was open for 3% of the time, Pallas kernels for 68%

profile of v4, /device:TPU:0, one launch (start us, length us, event | category | flops | bytes accessed | tf_op | source)
XLA Modules:
  0.0 959.1 jit_solution(15143146135649139345)
XLA Ops:
  9.3 4.4 pack_weights.1
  13.8 1.7 slice.53
  15.6 5.3 fusion
  22.3 72.9 %start_exchange.1 = (f32[16,8,1024]{2,1,0:T(8,128)}, bf16[16,36,3072]{2,1,0:T(8,128)(2,1)}) custom-call(f32[8,1024]{1,0:T(8,128)} %maximum_maximum_fusion.2.x_ref, bf16[36,49152]{1,0:T(8,128)(2,1)} %w_ref.1), custom_call_target="tpu_custom_call" | custom-call | flops 49999998976 | bytes 1048576 | tf_op jit(solution)/shard_map/start_exchange/pallas_call | solution.py:186
  95.2 5.2 all-gather.11.cloned.1.call-done
  100.3 12.9 %top_forward.1 = (bf16[1024,576]{1,0:T(8,128)(2,1)}, bf16[1,2880,128]{2,1,0:T(8,128)(2,1)}, bf16[1,1728,128]{2,1,0:T(8,128)(2,1)}) custom-call(bf16[1024,576]{1,0:T(8,128)(2,1)} %bitcast.44, bf16[16,1,1296,128]{3,2,1,0:T(8,128)(2,1)} %bitcast.53), custom_call_target="tpu_custom_call" | custom-call | flops 5435817984 | bytes 10485760 | tf_op jit(solution)/shard_map/top_forward/pallas_call | solution.py:125
  114.6 1.8 slice_reduce_fusion.1
  116.4 1.9 slice_subtract_fusion
  118.9 4.7 reshape.40.w_ref.refs_1_
  124.9 51.7 %all-gather.7.cloned.1.call-done.z_ref.refs_0_ = bf16[16,2880,128]{2,1,0:T(8,128)(2,1)} async-done(((bf16[1,2880,128]{2,1,0:T(8,128)(2,1)}), bf16[16,2880,128]{2,1,0:T(8,128)(2,1)}) %all-gather.7.cloned.1.call-update) | async-done | bytes 11796496 | tf_op jit(solution)/shard_map/all_gather | solution.py:700
  176.6 75.1 %head_pass1.2 = (f32[10240,3072]{1,0:T(8,128)}, f32[10240,128]{1,0:T(8,128)}, f32[8,10240]{1,0:T(8,128)}) custom-call(bf16[16,2880,128]{2,1,0:T(8,128)(2,1)} %all-gather.7.cloned.1.call-done.z_ref.refs_0_, bf16[576,3072]{1,0:T(8,128)(2,1)} %reshape.40.w_ref.refs_1_, f32[8,10240]{1,0:T(8,128)} %maximum_maximum_fusion.tok_ref.refs_2_), custom_call_target="tpu_custom_call" | custom-call | flops 36238786560 | bytes 125829120 | tf_op jit(solution)/shard_map/head_pass1/pallas_call | solution.py:269
  251.7 22.5 %exchange_stats.2.refs_3_ = f32[8,10240]{1,0:T(8,128)} custom-call(f32[8,10240]{1,0:T(8,128)} %get-tuple-element.61.st_ref, f32[1,640]{1,0:T(1,128)} %slice.73.w_ref), custom_call_target="tpu_custom_call" | custom-call | flops 2000000000 | bytes 1048576 | tf_op jit(solution)/shard_map/exchange_stats/pallas_call | solution.py:222
  274.2 122.1 %head_pass2.2 = (f32[16,2880,128]{2,1,0:T(8,128)}, f32[576,3072]{1,0:T(8,128)}) custom-call(bf16[16,2880,128]{2,1,0:T(8,128)(2,1)} %all-gather.7.cloned.1.call-done.z_ref.refs_0_, bf16[576,3072]{1,0:T(8,128)(2,1)} %reshape.40.w_ref.refs_1_, f32[8,10240]{1,0:T(8,128)} %maximum_maximum_fusion.tok_ref.refs_2_, f32[8,10240]{1,0:T(8,128)} %exchange_stats.2.refs_3_, ...), custom_call_target="tpu_custom_call" | custom-call | flops 72477573120 | bytes 125829120 | tf_op jit(solution)/shard_map/head_pass2/pallas_call | solution.py:349
  397.6 1.4 copy.40
  400.5 46.5 %head_pass1.3 = (f32[6144,3072]{1,0:T(8,128)}, f32[6144,128]{1,0:T(8,128)}, f32[8,6144]{1,0:T(8,128)}) custom-call(bf16[16,1728,128]{2,1,0:T(8,128)(2,1)} %all-gather.9.cloned.1.call-done.z_ref.refs_0_, bf16[576,3072]{1,0:T(8,128)(2,1)} %reshape.40.w_ref.refs_1_, f32[8,6144]{1,0:T(8,128)} %maximum_maximum_fusion.1.tok_ref.refs_2_), custom_call_target="tpu_custom_call" | custom-call | flops 21743271936 | bytes 75497472 | tf_op jit(solution)/shard_map/head_pass1/pallas_call | solution.py:269
  447.0 17.8 %exchange_stats.3.refs_3_ = f32[8,6144]{1,0:T(8,128)} custom-call(f32[8,6144]{1,0:T(8,128)} %get-tuple-element.69.st_ref, f32[1,384]{1,0:T(1,128)} %slice.74.w_ref), custom_call_target="tpu_custom_call" | custom-call | flops 2000000000 | bytes 1048576 | tf_op jit(solution)/shard_map/exchange_stats/pallas_call | solution.py:222
  464.8 88.6 %head_pass2.3 = (f32[16,1728,128]{2,1,0:T(8,128)}, f32[16,864,128]{2,1,0:T(8,128)}) custom-call(bf16[16,1728,128]{2,1,0:T(8,128)(2,1)} %all-gather.9.cloned.1.call-done.z_ref.refs_0_, bf16[576,3072]{1,0:T(8,128)(2,1)} %reshape.40.w_ref.refs_1_, f32[8,6144]{1,0:T(8,128)} %maximum_maximum_fusion.1.tok_ref.refs_2_, f32[8,6144]{1,0:T(8,128)} %exchange_stats.3.refs_3_, ...), custom_call_target="tpu_custom_call" | custom-call | flops 43486543872 | bytes 75497472 | tf_op jit(solution)/shard_map/head_pass2/pallas_call | solution.py:349
  553.4 57.5 %cube_reduce_scatter.2.refs_4_ = f32[1728,128]{1,0:T(8,128)} custom-call(f32[2,2,2,2,1728,128]{5,4,3,2,1,0:T(8,128)} %bitcast.56), custom_call_target="tpu_custom_call" | custom-call | flops 49999998976 | bytes 1048576 | tf_op jit(solution)/shard_map/cube_reduce_scatter/pallas_call | solution.py:591
  610.9 55.4 %block_backward.5 = (f32[1024,576]{1,0:T(8,128)}, f32[16,2592,128]{2,1,0:T(8,128)}, f32[16,864,128]{2,1,0:T(8,128)}) custom-call(bf16[1024,576]{1,0:T(8,128)(2,1)} %bitcast.45, bf16[16,1,1296,128]{3,2,1,0:T(8,128)(2,1)} %bitcast.54, bf16[1024,576]{1,0:T(8,128)(2,1)} %get-tuple-element.66.refs_2_, f32[2880,128]{1,0:T(8,128)} %bitcast.55, ...), custom_call_target="tpu_custom_call" | custom-call | flops 14495514624 | bytes 25165824 | tf_op jit(solution)/shard_map/block_backward/pallas_call | solution.py:478
  666.3 55.3 %block_backward.6 = (f32[1024,576]{1,0:T(8,128)}, f32[16,2592,128]{2,1,0:T(8,128)}, f32[16,864,128]{2,1,0:T(8,128)}) custom-call(bf16[1024,576]{1,0:T(8,128)(2,1)} %bitcast.42, bf16[16,4,1296,128]{3,2,1,0:T(8,128)(2,1)} %bitcast.35, f32[1024,576]{1,0:T(8,128)} %get-tuple-element.78.refs_2_, ...), custom_call_target="tpu_custom_call", output_to_operand_aliasing={{1}: (3, {}), {2}: (5, {})} | custom-call | flops 14495514624 | bytes 25165824 | tf_op jit(solution)/shard_map/block_backward/pallas_call | solution.py:478
  724.3 1.5 copy.43
  725.8 1.4 copy.42
  727.2 1.7 slice_reduce_fusion
  728.9 1.6 slice_reduce_fusion.2
  731.8 11.8 %unpack_head.1 = f32[36,49152]{1,0:T(8,128)} custom-call(f32[16,864,128]{2,1,0:T(8,128)} %get-tuple-element.88.p_ref), custom_call_target="tpu_custom_call" | custom-call | tf_op jit(solution)/shard_map/unpack_head/pallas_call | solution.py:498
  743.6 28.0 %block_backward.7 = (f32[1024,576]{1,0:T(8,128)}, f32[16,3888,128]{2,1,0:T(8,128)}) custom-call(bf16[1024,576]{1,0:T(8,128)(2,1)} %bitcast.46, bf16[16,4,1296,128]{3,2,1,0:T(8,128)(2,1)} %bitcast.36, f32[1024,576]{1,0:T(8,128)} %get-tuple-element.82.refs_2_), custom_call_target="tpu_custom_call" | custom-call | flops 14495514624 | bytes 25165824 | tf_op jit(solution)/shard_map/block_backward/pallas_call | solution.py:478
  771.5 28.0 %block_backward.8 = (f32[1024,576]{1,0:T(8,128)}, f32[16,3888,128]{2,1,0:T(8,128)}) custom-call(bf16[1024,576]{1,0:T(8,128)(2,1)} %bitcast.41, bf16[16,4,1296,128]{3,2,1,0:T(8,128)(2,1)} %bitcast.37, f32[1024,576]{1,0:T(8,128)} %get-tuple-element.83.refs_2_, f32[16,3888,128]{2,1,0:T(8,128)} %get-tuple-element.84.refs_3_), custom_call_target="tpu_custom_call", output_to_operand_aliasing={{1}: (3, {})} | custom-call | flops 14495514624 | bytes 25165824 | tf_op jit(solution)/shard_map/block_backward/pallas_call | solution.py:478
  799.5 28.0 %block_backward.9 = (bf16[1024,576]{1,0:T(8,128)(2,1)}, f32[16,3888,128]{2,1,0:T(8,128)}) custom-call(bf16[1024,576]{1,0:T(8,128)(2,1)} %bitcast.40, bf16[16,4,1296,128]{3,2,1,0:T(8,128)(2,1)} %bitcast.38, f32[1024,576]{1,0:T(8,128)} %get-tuple-element.85.refs_2_, f32[16,3888,128]{2,1,0:T(8,128)} %get-tuple-element.86.refs_3_), custom_call_target="tpu_custom_call", output_to_operand_aliasing={{1}: (3, {})} | custom-call | flops 14495514624 | bytes 25165824 | tf_op jit(solution)/shard_map/block_backward/pallas_call | solution.py:478
  827.6 2.4 copy.37
  829.9 115.1 %cube_reduce_scatter.3.p_ref = f32[3888,128]{1,0:T(8,128)} custom-call(f32[2,2,2,2,3888,128]{5,4,3,2,1,0:T(8,128)} %bitcast.39), custom_call_target="tpu_custom_call" | custom-call | flops 49999998976 | bytes 1048576 | tf_op jit(solution)/shard_map/cube_reduce_scatter/pallas_call | solution.py:591
  945.1 2.2 unpack_grads.2
  947.3 3.7 unpack_grads.3
  (48 shorter events, 12.1 us)
Async XLA Ops:
  7.2 93.2 %all-gather.11.cloned.1.call-start = ((), (), s32[]{:S(2)}) async-start(), calls=%async_computation.6 | async-start | bytes 5640192 | tf_op jit(solution)/shard_map/all_gather | solution.py:689
  15.5 161.1 %all-gather.7.cloned.1.call-start = ((), (), s32[]{:S(2)}) async-start(), calls=%async_computation.2 | async-start | bytes 12533760 | tf_op jit(solution)/shard_map/all_gather | solution.py:700
  100.3 13.0 %copy-start = (bf16[5,1296,128]{2,1,0:T(8,128)(2,1)S(1)}, bf16[5,1296,128]{2,1,0:T(8,128)(2,1)}, u32[]{:S(2)}) copy-start(bf16[5,1296,128]{2,1,0:T(8,128)(2,1)} %pack_weights.1) | copy-start | bytes 4976644
  113.3 287.2 %all-gather.13.cloned.1.call-start = ((), (), s32[]{:S(2)}) async-start(), calls=%async_computation.7 | async-start | bytes 22560768 | tf_op jit(solution)/shard_map/all_gather | solution.py:701
  114.5 285.9 %all-gather.9.cloned.1.call-start = ((), (), s32[]{:S(2)}) async-start(), calls=%async_computation.3 | async-start | bytes 7520256 | tf_op jit(solution)/shard_map/all_gather | solution.py:700
  118.4 435.0 %reduce-scatter.3.cloned.1.call-start = ((), (), s32[]{:S(2)}) async-start(), calls=%async_computation.4 | async-start | bytes 25067520 | tf_op jit(solution)/shard_map/reduce_scatter | solution.py:718
  396.4 1.3 copy-start.4
  396.4 548.7 %reduce-scatter.5.cloned.1.call-start = ((), (), s32[]{:S(2)}) async-start(), calls=%async_computation.5 | async-start | bytes 22560768 | tf_op jit(solution)/shard_map/reduce_scatter | solution.py:734
  721.6 1.3 copy-start.3
  721.7 2.7 copy-start.2
  721.7 4.1 copy-start.1
Sparse Core Ops, SparseCore 0:
  15.6 84.6 all-gather.10
  113.4 63.1 all-gather.6
  178.9 97.4 all-gather.12
  278.4 44.6 all-gather.8
  396.5 136.8 reduce-scatter.2
  721.8 126.7 reduce-scatter.4

commit v5 on v4

--- a/solution.py
+++ b/solution.py
@@ -235,10 +235,11 @@
     )(st, w_own)
 
 
-def pass1_body(z_ref, w_ref, tok_ref, e_ref, ms_ref, st_ref, z_s):
+def pass1_body(z_ref, w_ref, tok_ref, e_ref, ms_ref, st_ref, zt_ref, z_s):
     TB = z_s.shape[0]
     load_packed(z_s, z_ref, TB)
     z = z_s[...]
+    zt_ref[...] = z.T
     tokc = jnp.concatenate([tok_ref[...], jnp.zeros((120, TB), F32)], axis=0).T
     tgt = tokc[:, 0:1]
     lane = lax.broadcasted_iota(jnp.int32, (TB, LANE), 1)
@@ -278,11 +279,13 @@
             rows_spec(TB, VLOC),
             rows_spec(TB, LANE),
             lanes_spec(8, TB),
+            lanes_spec(DIM, TB),
         ],
         out_shape=[
             jax.ShapeDtypeStruct((CHUNK_TOK, VLOC), F32),
             jax.ShapeDtypeStruct((CHUNK_TOK, LANE), F32),
             jax.ShapeDtypeStruct((8, CHUNK_TOK), F32),
+            jax.ShapeDtypeStruct((DIM, CHUNK_TOK), BF),
         ],
         scratch_shapes=[pltpu.VMEM((TB, DIM), BF)],
         compiler_params=pltpu.CompilerParams(vmem_limit_bytes=VMEM_LIMIT),
@@ -293,9 +296,9 @@
 
 def pass2_body(has_acc, *refs):
     if has_acc:
-        z_ref, w_ref, tok_ref, res_ref, e_ref, ms_ref, acc_ref, dz_ref, pk_ref, z_s, q_s, gw_ref = refs
+        z_ref, w_ref, tok_ref, res_ref, e_ref, ms_ref, acc_ref, dz_ref, pk_ref, q_s, gw_ref = refs
     else:
-        z_ref, w_ref, tok_ref, res_ref, e_ref, ms_ref, dz_ref, gw_ref, z_s, q_s = refs
+        z_ref, w_ref, tok_ref, res_ref, e_ref, ms_ref, dz_ref, gw_ref, q_s = refs
         acc_ref = None
 
     @pl.when(pl.program_id(0) == 0)
@@ -305,9 +308,8 @@
         else:
             gw_ref[...] = jnp.zeros_like(gw_ref)
 
-    TB = z_s.shape[0]
-    load_packed(z_s, z_ref, TB)
-    z = z_s[...]
+    TB = q_s.shape[0]
+    z = z_ref[...]
     tokc = jnp.concatenate([tok_ref[...], res_ref[...], jnp.zeros((112, TB), F32)], axis=0).T
     tgt, w_tok, m_glob, s_inv = (tokc[:, i:i + 1] for i in (0, 1, 8, 9))
     ids = lax.broadcasted_iota(jnp.int32, (1, SW), 1).astype(F32)
@@ -318,7 +320,7 @@
         p = jnp.where(ids == tgt - float(s * SW), p - 1.0, p)
         q = (w_tok * p).astype(BF)
         q_s[:, cols] = q
-        gw_ref[:, cols] += dot_tn(z, q)
+        gw_ref[:, cols] += dot_nn(z, q)
     dz = dot_nt(q_s[...], w_ref[...])
     store_packed(dz_ref, dz, TB)
     if has_acc:
@@ -334,7 +336,7 @@
     TB = CHUNK_TOK // N_DEV
     ZROWS = packed_rows(TB)
     in_specs = [
-        rows_spec(1, ZROWS, LANE),
+        lanes_spec(DIM, TB),
         whole(DIM, VLOC),
         lanes_spec(8, TB),
         lanes_spec(8, TB),
@@ -358,7 +360,7 @@
             jax.ShapeDtypeStruct((N_DEV, ZROWS, LANE), F32),
             jax.ShapeDtypeStruct(g_shape, F32),
         ],
-        scratch_shapes=[pltpu.VMEM((TB, DIM), BF), pltpu.VMEM((TB, VLOC), BF)] + ([] if acc is None else [pltpu.VMEM((DIM, VLOC), F32)]),
+        scratch_shapes=[pltpu.VMEM((TB, VLOC), BF)] + ([] if acc is None else [pltpu.VMEM((DIM, VLOC), F32)]),
         compiler_params=pltpu.CompilerParams(vmem_limit_bytes=VMEM_LIMIT),
         cost_estimate=pl.CostEstimate(flops=4 * CHUNK_TOK * DIM * VLOC, bytes_accessed=4 * CHUNK_TOK * VLOC, transcendentals=0),
         name='head_pass2',
@@ -675,6 +677,7 @@
         wd_s[PD * d + PH:PD * d + PD, D4:DIM] = tail[:, HL:]
 
 
+PEERS = ((1,), (3, 5, 9, 15), (2, 4, 8, 14), (7, 11, 13), (6, 10, 12))
 GROUPS = ((4, 3), (2, 1, 0))
 
 
@@ -707,10 +710,10 @@
             tok = jnp.concatenate([tgt[:, sl].reshape(1, CHUNK_TOK), w_tok[:, sl].reshape(1, CHUNK_TOK), zero], axis=0)
             if c == 1:
                 tok, acc, rest = barrier((tok, acc, rest))
-            e, ms, st = head_pass1(z_all[c], w_vocab, tok)
+            e, ms, st, z_t = head_pass1(z_all[c], w_vocab, tok)
             res = exchange_stats(st, w_own[:, sl], 2 + c)
             loss = loss + jnp.sum(res[2])
-            dz, acc = head_pass2(z_all[c], w_vocab, tok, res, e, ms, acc)
+            dz, acc = head_pass2(z_t, w_vocab, tok, res, e, ms, acc)
             if c == 1:
                 dz, dz_own[0] = barrier((dz, dz_own[0]))
                 dz_own.append(cube_reduce_scatter(dz, 2, 4))
@@ -723,14 +726,11 @@
             for i, l in enumerate(group):
                 pk, ws = (pack_top, 0) if l == 4 else (rest, l)
                 args = (hidden[l], pk, ws, g_args, buf, i, len(group), BF if l == 0 else F32)
-                if l > 2:
-                    g, buf, got = block_backward(*args, tuple(range(2, 16, 2) if l == 4 else range(1, 16, 2)), moved, l + 3)
-                    moved.append(got)
-                else:
-                    g, buf = block_backward(*args)
+                g, buf, got = block_backward(*args, PEERS[l], moved, l + 6)
+                moved = [acc, got]
                 g_args = [g]
             bufs.append(buf)
-        grad_out = unpack_head(moved[2])
+        grad_out = unpack_head(moved[1])
         red = lax.psum_scatter(bufs[0], AXIS, scatter_dimension=0, tiled=False)
         bufs[1], grad_out = barrier((bufs[1], grad_out))
         red_low = cube_reduce_scatter(bufs[1], 3, 5)

time: 967 us -> 946 us (0.978)
  Pallas kernels: 848 us -> 827 us
    pallas_call x5, Pallas kernels: 195 us -> 178 us  [block_backward(): pl.pallas_call(functools.partial(bwd_body, top, slot * PROWS, masks, len(...]
  transfers between devices with their start and end apart: 6 -> 6, of which waited for: 2 -> 2; matrix products, arithmetic and copies ran while one was open for 3% -> 3% of each run, Pallas kernels for 68% -> 72%
where the time goes in v5:
time: 946 us; the launch traced here: 938 us
  Pallas kernels  827 us (87%)
  waiting for transfers between devices  57.1 us (6%)
  local copies, waits for them, and re-layouts  25.4 us (3%)
  between operations  17 us (2%)
  other arithmetic  10.6 us (1%)
    pallas_call x2, Pallas kernels, head_pass2(): pl.pallas_call(functools.partial(pass2_body, acc is not None), grid=(N_DE...  206 us
    pallas_call x5, Pallas kernels, block_backward(): pl.pallas_call(functools.partial(bwd_body, top, slot * PROWS, masks, len(...  178 us
    pallas_call x2, Pallas kernels, cube_reduce_scatter(): pl.pallas_call(functools.partial(cube_body, pieces), in_specs=[HB], out_s...  174 us
    pallas_call x2, Pallas kernels, head_pass1(): pl.pallas_call(pass1_body, grid=(N_DEV,), in_specs=[rows_spec(1, ZROWS, L...  122 us
    pallas_call x1, Pallas kernels, start_exchange(): pl.pallas_call(start_body, in_specs=[VM, HB], out_specs=[VM, HB], out_sha...  72.9 us
    all_gather x2, waiting for transfers between devices, device_step(): z_all = [lax.all_gather(z, AXIS, tiled=True) for z in z_packed]  51.8 us
    pallas_call x2, Pallas kernels, exchange_stats(): pl.pallas_call(stats_body, in_specs=[VM, VM], out_specs=VM, out_shape=jax...  40.3 us
  transfers between devices with their start and end apart: 6, of which 2 were waited for; matrix products, arithmetic and copies ran while one was open for 3% of the time, Pallas kernels for 72%

profile of v5, /device:TPU:0, one launch (start us, length us, event | category | flops | bytes accessed | tf_op | source)
XLA Modules:
  0.0 938.0 jit_solution(14138061017674122926)
XLA Ops:
  9.3 4.4 pack_weights.1
  13.8 1.7 slice.53
  15.6 5.3 fusion
  22.3 72.9 %start_exchange.1 = (f32[16,8,1024]{2,1,0:T(8,128)}, bf16[16,36,3072]{2,1,0:T(8,128)(2,1)}) custom-call(f32[8,1024]{1,0:T(8,128)} %maximum_maximum_fusion.2.x_ref, bf16[36,49152]{1,0:T(8,128)(2,1)} %w_ref.1), custom_call_target="tpu_custom_call" | custom-call | flops 49999998976 | bytes 1048576 | tf_op jit(solution)/shard_map/start_exchange/pallas_call | solution.py:186
  95.2 5.2 all-gather.11.cloned.1.call-done
  100.4 12.9 %top_forward.1 = (bf16[1024,576]{1,0:T(8,128)(2,1)}, bf16[1,2880,128]{2,1,0:T(8,128)(2,1)}, bf16[1,1728,128]{2,1,0:T(8,128)(2,1)}) custom-call(bf16[1024,576]{1,0:T(8,128)(2,1)} %bitcast.44, bf16[16,1,1296,128]{3,2,1,0:T(8,128)(2,1)} %bitcast.53), custom_call_target="tpu_custom_call" | custom-call | flops 5435817984 | bytes 10485760 | tf_op jit(solution)/shard_map/top_forward/pallas_call | solution.py:125
  114.6 1.8 slice_reduce_fusion.1
  116.4 1.9 slice_subtract_fusion
  118.8 4.7 reshape.40.w_ref.refs_1_
  124.9 51.8 %all-gather.7.cloned.1.call-done.z_ref = bf16[16,2880,128]{2,1,0:T(8,128)(2,1)} async-done(((bf16[1,2880,128]{2,1,0:T(8,128)(2,1)}), bf16[16,2880,128]{2,1,0:T(8,128)(2,1)}) %all-gather.7.cloned.1.call-update) | async-done | bytes 11796496 | tf_op jit(solution)/shard_map/all_gather | solution.py:703
  176.6 75.0 %head_pass1.2 = (f32[10240,3072]{1,0:T(8,128)}, f32[10240,128]{1,0:T(8,128)}, f32[8,10240]{1,0:T(8,128)}, bf16[576,10240]{1,0:T(8,128)(2,1)}) custom-call(bf16[16,2880,128]{2,1,0:T(8,128)(2,1)} %all-gather.7.cloned.1.call-done.z_ref, bf16[576,3072]{1,0:T(8,128)(2,1)} %reshape.40.w_ref.refs_1_, f32[8,10240]{1,0:T(8,128)} %maximum_maximum_fusion.tok_ref.refs_2_), custom_call_target="tpu_custom_call" | custom-call | flops 36238786560 | bytes 125829120 | tf_op jit(solution)/shard_map/head_pass1/pallas_call | solution.py:270
  251.7 22.5 %exchange_stats.2.refs_3_ = f32[8,10240]{1,0:T(8,128)} custom-call(f32[8,10240]{1,0:T(8,128)} %get-tuple-element.67.st_ref, f32[1,640]{1,0:T(1,128)} %slice.73.w_ref), custom_call_target="tpu_custom_call" | custom-call | flops 2000000000 | bytes 1048576 | tf_op jit(solution)/shard_map/exchange_stats/pallas_call | solution.py:222
  274.2 118.7 %head_pass2.2 = (f32[16,2880,128]{2,1,0:T(8,128)}, f32[576,3072]{1,0:T(8,128)}) custom-call(bf16[576,10240]{1,0:T(8,128)(2,1)} %get-tuple-element.66.refs_0_, bf16[576,3072]{1,0:T(8,128)(2,1)} %reshape.40.w_ref.refs_1_, f32[8,10240]{1,0:T(8,128)} %maximum_maximum_fusion.tok_ref.refs_2_, f32[8,10240]{1,0:T(8,128)} %exchange_stats.2.refs_3_, ...), custom_call_target="tpu_custom_call" | custom-call | flops 72477573120 | bytes 125829120 | tf_op jit(solution)/shard_map/head_pass2/pallas_call | solution.py:351
  394.2 1.4 copy.43
  397.1 46.9 %head_pass1.3 = (f32[6144,3072]{1,0:T(8,128)}, f32[6144,128]{1,0:T(8,128)}, f32[8,6144]{1,0:T(8,128)}, bf16[576,6144]{1,0:T(8,128)(2,1)}) custom-call(bf16[16,1728,128]{2,1,0:T(8,128)(2,1)} %all-gather.9.cloned.1.call-done.z_ref, bf16[576,3072]{1,0:T(8,128)(2,1)} %reshape.40.w_ref.refs_1_, f32[8,6144]{1,0:T(8,128)} %maximum_maximum_fusion.1.tok_ref.refs_2_), custom_call_target="tpu_custom_call" | custom-call | flops 21743271936 | bytes 75497472 | tf_op jit(solution)/shard_map/head_pass1/pallas_call | solution.py:270
  444.0 17.8 %exchange_stats.3.refs_3_ = f32[8,6144]{1,0:T(8,128)} custom-call(f32[8,6144]{1,0:T(8,128)} %get-tuple-element.76.st_ref, f32[1,384]{1,0:T(1,128)} %slice.74.w_ref), custom_call_target="tpu_custom_call" | custom-call | flops 2000000000 | bytes 1048576 | tf_op jit(solution)/shard_map/exchange_stats/pallas_call | solution.py:222
  461.8 87.1 %head_pass2.3 = (f32[16,1728,128]{2,1,0:T(8,128)}, f32[16,864,128]{2,1,0:T(8,128)}) custom-call(bf16[576,6144]{1,0:T(8,128)(2,1)} %get-tuple-element.75.refs_0_, bf16[576,3072]{1,0:T(8,128)(2,1)} %reshape.40.w_ref.refs_1_, f32[8,6144]{1,0:T(8,128)} %maximum_maximum_fusion.1.tok_ref.refs_2_, f32[8,6144]{1,0:T(8,128)} %exchange_stats.3.refs_3_, ...), custom_call_target="tpu_custom_call" | custom-call | flops 43486543872 | bytes 75497472 | tf_op jit(solution)/shard_map/head_pass2/pallas_call | solution.py:351
  548.9 57.8 %cube_reduce_scatter.2.refs_4_ = f32[1728,128]{1,0:T(8,128)} custom-call(f32[2,2,2,2,1728,128]{5,4,3,2,1,0:T(8,128)} %bitcast.56), custom_call_target="tpu_custom_call" | custom-call | flops 49999998976 | bytes 1048576 | tf_op jit(solution)/shard_map/cube_reduce_scatter/pallas_call | solution.py:593
  606.7 35.6 %block_backward.5 = (f32[1024,576]{1,0:T(8,128)}, f32[16,2592,128]{2,1,0:T(8,128)}, f32[16,864,128]{2,1,0:T(8,128)}) custom-call(bf16[1024,576]{1,0:T(8,128)(2,1)} %bitcast.45, bf16[16,1,1296,128]{3,2,1,0:T(8,128)(2,1)} %bitcast.54, bf16[1024,576]{1,0:T(8,128)(2,1)} %get-tuple-element.72.refs_2_, f32[2880,128]{1,0:T(8,128)} %bitcast.55, ...), custom_call_target="tpu_custom_call" | custom-call | flops 14495514624 | bytes 25165824 | tf_op jit(solution)/shard_map/block_backward/pallas_call | solution.py:480
  642.3 34.9 %block_backward.6 = (f32[1024,576]{1,0:T(8,128)}, f32[16,2592,128]{2,1,0:T(8,128)}, f32[16,864,128]{2,1,0:T(8,128)}) custom-call(bf16[1024,576]{1,0:T(8,128)(2,1)} %bitcast.42, bf16[16,4,1296,128]{3,2,1,0:T(8,128)(2,1)} %bitcast.35, f32[1024,576]{1,0:T(8,128)} %get-tuple-element.85.refs_2_, ...), custom_call_target="tpu_custom_call", output_to_operand_aliasing={{1}: (3, {}), {2}: (5, {})} | custom-call | flops 14495514624 | bytes 25165824 | tf_op jit(solution)/shard_map/block_backward/pallas_call | solution.py:480
  678.5 1.4 copy.47
  680.0 1.4 copy.46
  681.4 1.8 copy.45
  683.2 1.7 slice_reduce_fusion
  684.9 1.6 slice_reduce_fusion.2
  687.8 31.3 %block_backward.7 = (f32[1024,576]{1,0:T(8,128)}, f32[16,3888,128]{2,1,0:T(8,128)}, f32[16,864,128]{2,1,0:T(8,128)}) custom-call(bf16[1024,576]{1,0:T(8,128)(2,1)} %bitcast.46, bf16[16,4,1296,128]{3,2,1,0:T(8,128)(2,1)} %bitcast.36, f32[1024,576]{1,0:T(8,128)} %get-tuple-element.89.refs_2_, ...), custom_call_target="tpu_custom_call", output_to_operand_aliasing={{2}: (4, {})} | custom-call | flops 14495514624 | bytes 25165824 | tf_op jit(solution)/shard_map/block_backward/pallas_call | solution.py:480
  719.0 47.7 %block_backward.8 = (f32[1024,576]{1,0:T(8,128)}, f32[16,3888,128]{2,1,0:T(8,128)}, f32[16,864,128]{2,1,0:T(8,128)}) custom-call(bf16[1024,576]{1,0:T(8,128)(2,1)} %bitcast.41, bf16[16,4,1296,128]{3,2,1,0:T(8,128)(2,1)} %bitcast.37, f32[1024,576]{1,0:T(8,128)} %get-tuple-element.91.refs_2_, ...), custom_call_target="tpu_custom_call", output_to_operand_aliasing={{1}: (3, {}), {2}: (5, {})} | custom-call | flops 14495514624 | bytes 25165824 | tf_op jit(solution)/shard_map/block_backward/pallas_call | solution.py:480
  766.7 28.0 %block_backward.9 = (bf16[1024,576]{1,0:T(8,128)(2,1)}, f32[16,3888,128]{2,1,0:T(8,128)}, f32[16,864,128]{2,1,0:T(8,128)}) custom-call(bf16[1024,576]{1,0:T(8,128)(2,1)} %bitcast.40, bf16[16,4,1296,128]{3,2,1,0:T(8,128)(2,1)} %bitcast.38, f32[1024,576]{1,0:T(8,128)} %get-tuple-element.94.refs_2_, ...), custom_call_target="tpu_custom_call", output_to_operand_aliasing={{1}: (3, {}), {2}: (5, {})} | custom-call | flops 14495514624 | bytes 25165824 | tf_op jit(solution)/shard_map/block_backward/pallas_call | solution.py:480
  794.8 11.5 %unpack_head.1 = f32[36,49152]{1,0:T(8,128)} custom-call(f32[16,864,128]{2,1,0:T(8,128)} %get-tuple-element.98.p_ref), custom_call_target="tpu_custom_call" | custom-call | tf_op jit(solution)/shard_map/unpack_head/pallas_call | solution.py:500
  807.7 116.2 %cube_reduce_scatter.3.p_ref = f32[3888,128]{1,0:T(8,128)} custom-call(f32[2,2,2,2,3888,128]{5,4,3,2,1,0:T(8,128)} %bitcast.39), custom_call_target="tpu_custom_call" | custom-call | flops 49999998976 | bytes 1048576 | tf_op jit(solution)/shard_map/cube_reduce_scatter/pallas_call | solution.py:593
  924.0 2.2 unpack_grads.2
  926.2 3.7 unpack_grads.3
  (50 shorter events, 12.0 us)
Async XLA Ops:
  7.2 93.2 %all-gather.11.cloned.1.call-start = ((), (), s32[]{:S(2)}) async-start(), calls=%async_computation.6 | async-start | bytes 5640192 | tf_op jit(solution)/shard_map/all_gather | solution.py:692
  15.5 161.1 %all-gather.7.cloned.1.call-start = ((), (), s32[]{:S(2)}) async-start(), calls=%async_computation.2 | async-start | bytes 12533760 | tf_op jit(solution)/shard_map/all_gather | solution.py:703
  100.4 13.0 %copy-start = (bf16[5,1296,128]{2,1,0:T(8,128)(2,1)S(1)}, bf16[5,1296,128]{2,1,0:T(8,128)(2,1)}, u32[]{:S(2)}) copy-start(bf16[5,1296,128]{2,1,0:T(8,128)(2,1)} %pack_weights.1) | copy-start | bytes 4976644
  113.3 283.8 %all-gather.13.cloned.1.call-start = ((), (), s32[]{:S(2)}) async-start(), calls=%async_computation.7 | async-start | bytes 22560768 | tf_op jit(solution)/shard_map/all_gather | solution.py:704
  114.6 282.5 %all-gather.9.cloned.1.call-start = ((), (), s32[]{:S(2)}) async-start(), calls=%async_computation.3 | async-start | bytes 7520256 | tf_op jit(solution)/shard_map/all_gather | solution.py:703
  118.4 430.5 %reduce-scatter.3.cloned.1.call-start = ((), (), s32[]{:S(2)}) async-start(), calls=%async_computation.4 | async-start | bytes 25067520 | tf_op jit(solution)/shard_map/reduce_scatter | solution.py:721
  393.0 1.3 copy-start.4
  393.0 531.0 %reduce-scatter.5.cloned.1.call-start = ((), (), s32[]{:S(2)}) async-start(), calls=%async_computation.5 | async-start | bytes 22560768 | tf_op jit(solution)/shard_map/reduce_scatter | solution.py:734
  677.2 1.3 copy-start.3
  677.3 2.7 copy-start.2
  677.3 4.1 copy-start.1
  794.8 11.5 %copy-start.5 = (bf16[1024,576]{1,0:T(8,128)(2,1)S(1)}, bf16[1024,576]{1,0:T(8,128)(2,1)}, u32[]{:S(2)}) copy-start(bf16[1024,576]{1,0:T(8,128)(2,1)} %get-tuple-element.126) | copy-start | bytes 3538948
Sparse Core Ops, SparseCore 0:
  15.7 84.6 all-gather.10
  113.4 63.1 all-gather.6
  178.9 97.4 all-gather.12
  278.4 44.6 all-gather.8
  393.1 136.9 reduce-scatter.2
  677.4 145.1 reduce-scatter.4

commit v6 on v5

--- a/solution.py
+++ b/solution.py
@@ -677,7 +677,7 @@
         wd_s[PD * d + PH:PD * d + PD, D4:DIM] = tail[:, HL:]
 
 
-PEERS = ((1,), (3, 5, 9, 15), (2, 4, 8, 14), (7, 11, 13), (6, 10, 12))
+PEERS = ((1, 15), (3, 5, 9), (2, 4, 8, 14), (7, 11, 13), (6, 10, 12))
 GROUPS = ((4, 3), (2, 1, 0))
 
 
@@ -702,12 +702,15 @@
 
         z_all = [lax.all_gather(z, AXIS, tiled=True) for z in z_packed]
         rest = gather(packs[:4])
+        hs = [hidden[l] for l in range(LAYERS)]
         acc, loss, dz_own = None, jnp.zeros((), F32), []
         for c, (lo, tb) in enumerate(SPLITS):
             sl = slice(lo, lo + tb)
             CHUNK_TOK = tb * N_DEV
             zero = jnp.zeros((6, CHUNK_TOK), F32)
             tok = jnp.concatenate([tgt[:, sl].reshape(1, CHUNK_TOK), w_tok[:, sl].reshape(1, CHUNK_TOK), zero], axis=0)
+            if c == 0:
+                tok, *hs = barrier((tok, *hs))
             if c == 1:
                 tok, acc, rest = barrier((tok, acc, rest))
             e, ms, st, z_t = head_pass1(z_all[c], w_vocab, tok)
@@ -725,7 +728,7 @@
             buf = None
             for i, l in enumerate(group):
                 pk, ws = (pack_top, 0) if l == 4 else (rest, l)
-                args = (hidden[l], pk, ws, g_args, buf, i, len(group), BF if l == 0 else F32)
+                args = (hs[l], pk, ws, g_args, buf, i, len(group), BF if l == 0 else F32)
                 g, buf, got = block_backward(*args, PEERS[l], moved, l + 6)
                 moved = [acc, got]
                 g_args = [g]

time: 946 us -> 933 us (0.986)
    pallas_call x5, Pallas kernels: 178 us -> 161 us  [block_backward(): pl.pallas_call(functools.partial(bwd_body, top, slot * PROWS, masks, len(...]
    pallas_call x2, Pallas kernels: 174 us -> 185 us  [cube_reduce_scatter(): pl.pallas_call(functools.partial(cube_body, pieces), in_specs=[HB], out_s...]
  transfers between devices with their start and end apart: 6 -> 6, of which waited for: 2 -> 2; matrix products, arithmetic and copies ran while one was open for 3% -> 3% of each run, Pallas kernels for 72% -> 73%
where the time goes in v6:
time: 933 us; the launch traced here: 924 us
  Pallas kernels  822 us (88%)
  waiting for transfers between devices  49.4 us (5%)
  local copies, waits for them, and re-layouts  24.9 us (3%)
  between operations  16.9 us (2%)
  other arithmetic  10.6 us (1%)
    pallas_call x2, Pallas kernels, head_pass2(): pl.pallas_call(functools.partial(pass2_body, acc is not None), grid=(N_DE...  206 us
    pallas_call x2, Pallas kernels, cube_reduce_scatter(): pl.pallas_call(functools.partial(cube_body, pieces), in_specs=[HB], out_s...  185 us
    pallas_call x5, Pallas kernels, block_backward(): pl.pallas_call(functools.partial(bwd_body, top, slot * PROWS, masks, len(...  161 us
    pallas_call x2, Pallas kernels, head_pass1(): pl.pallas_call(pass1_body, grid=(N_DEV,), in_specs=[rows_spec(1, ZROWS, L...  122 us
    pallas_call x1, Pallas kernels, start_exchange(): pl.pallas_call(start_body, in_specs=[VM, HB], out_specs=[VM, HB], out_sha...  72.8 us
    all_gather x2, waiting for transfers between devices, device_step(): z_all = [lax.all_gather(z, AXIS, tiled=True) for z in z_packed]  44 us
    pallas_call x2, Pallas kernels, exchange_stats(): pl.pallas_call(stats_body, in_specs=[VM, VM], out_specs=VM, out_shape=jax...  40.3 us
  transfers between devices with their start and end apart: 6, of which 2 were waited for; matrix products, arithmetic and copies ran while one was open for 3% of the time, Pallas kernels for 73%

profile of v6, /device:TPU:0, one launch (start us, length us, event | category | flops | bytes accessed | tf_op | source)
XLA Modules:
  0.0 924.3 jit_solution(14654264157474284184)
XLA Ops:
  9.4 4.4 pack_weights.1
  13.8 1.7 slice.52
  15.6 5.1 fusion
  20.7 1.5 copy.47
  22.2 72.8 %start_exchange.1 = (f32[16,8,1024]{2,1,0:T(8,128)}, bf16[16,36,3072]{2,1,0:T(8,128)(2,1)}) custom-call(f32[8,1024]{1,0:T(8,128)} %maximum_maximum_fusion.2.x_ref, bf16[36,49152]{1,0:T(8,128)(2,1)} %w_ref.1), custom_call_target="tpu_custom_call" | custom-call | flops 49999998976 | bytes 1048576 | tf_op jit(solution)/shard_map/start_exchange/pallas_call | solution.py:186
  95.0 5.3 all-gather.11.cloned.1.call-done
  100.3 12.9 %top_forward.1 = (bf16[1024,576]{1,0:T(8,128)(2,1)}, bf16[1,2880,128]{2,1,0:T(8,128)(2,1)}, bf16[1,1728,128]{2,1,0:T(8,128)(2,1)}) custom-call(bf16[1024,576]{1,0:T(8,128)(2,1)} %bitcast.44, bf16[16,1,1296,128]{3,2,1,0:T(8,128)(2,1)} %bitcast.53), custom_call_target="tpu_custom_call" | custom-call | flops 5435817984 | bytes 10485760 | tf_op jit(solution)/shard_map/top_forward/pallas_call | solution.py:125
  114.5 2.5 copy.43
  117.0 2.5 copy.44
  121.0 1.4 copy.46
  122.4 1.8 slice_reduce_fusion.1
  124.2 1.9 slice_subtract_fusion
  127.4 4.7 reshape.42.w_ref.refs_1_
  132.7 44.0 %all-gather.7.cloned.1.call-done.z_ref = bf16[16,2880,128]{2,1,0:T(8,128)(2,1)} async-done(((bf16[1,2880,128]{2,1,0:T(8,128)(2,1)}), bf16[16,2880,128]{2,1,0:T(8,128)(2,1)}) %all-gather.7.cloned.1.call-update) | async-done | bytes 11796496 | tf_op jit(solution)/shard_map/all_gather | solution.py:703
  176.7 75.0 %head_pass1.2 = (f32[10240,3072]{1,0:T(8,128)}, f32[10240,128]{1,0:T(8,128)}, f32[8,10240]{1,0:T(8,128)}, bf16[576,10240]{1,0:T(8,128)(2,1)}) custom-call(bf16[16,2880,128]{2,1,0:T(8,128)(2,1)} %all-gather.7.cloned.1.call-done.z_ref, bf16[576,3072]{1,0:T(8,128)(2,1)} %reshape.42.w_ref.refs_1_, f32[8,10240]{1,0:T(8,128)} %maximum_maximum_fusion.tok_ref.refs_2_), custom_call_target="tpu_custom_call" | custom-call | flops 36238786560 | bytes 125829120 | tf_op jit(solution)/shard_map/head_pass1/pallas_call | solution.py:270
  251.7 22.5 %exchange_stats.2.refs_3_ = f32[8,10240]{1,0:T(8,128)} custom-call(f32[8,10240]{1,0:T(8,128)} %get-tuple-element.75.st_ref, f32[1,640]{1,0:T(1,128)} %slice.73.w_ref), custom_call_target="tpu_custom_call" | custom-call | flops 2000000000 | bytes 1048576 | tf_op jit(solution)/shard_map/exchange_stats/pallas_call | solution.py:222
  274.2 118.7 %head_pass2.2 = (f32[16,2880,128]{2,1,0:T(8,128)}, f32[576,3072]{1,0:T(8,128)}) custom-call(bf16[576,10240]{1,0:T(8,128)(2,1)} %get-tuple-element.74.refs_0_, bf16[576,3072]{1,0:T(8,128)(2,1)} %reshape.42.w_ref.refs_1_, f32[8,10240]{1,0:T(8,128)} %maximum_maximum_fusion.tok_ref.refs_2_, f32[8,10240]{1,0:T(8,128)} %exchange_stats.2.refs_3_, ...), custom_call_target="tpu_custom_call" | custom-call | flops 72477573120 | bytes 125829120 | tf_op jit(solution)/shard_map/head_pass2/pallas_call | solution.py:351
  394.7 46.9 %head_pass1.3 = (f32[6144,3072]{1,0:T(8,128)}, f32[6144,128]{1,0:T(8,128)}, f32[8,6144]{1,0:T(8,128)}, bf16[576,6144]{1,0:T(8,128)(2,1)}) custom-call(bf16[16,1728,128]{2,1,0:T(8,128)(2,1)} %all-gather.9.cloned.1.call-done.z_ref, bf16[576,3072]{1,0:T(8,128)(2,1)} %reshape.42.w_ref.refs_1_, f32[8,6144]{1,0:T(8,128)} %maximum_maximum_fusion.1.tok_ref.refs_2_), custom_call_target="tpu_custom_call" | custom-call | flops 21743271936 | bytes 75497472 | tf_op jit(solution)/shard_map/head_pass1/pallas_call | solution.py:270
  441.6 17.8 %exchange_stats.3.refs_3_ = f32[8,6144]{1,0:T(8,128)} custom-call(f32[8,6144]{1,0:T(8,128)} %get-tuple-element.85.st_ref, f32[1,384]{1,0:T(1,128)} %slice.74.w_ref), custom_call_target="tpu_custom_call" | custom-call | flops 2000000000 | bytes 1048576 | tf_op jit(solution)/shard_map/exchange_stats/pallas_call | solution.py:222
  459.4 87.1 %head_pass2.3 = (f32[16,1728,128]{2,1,0:T(8,128)}, f32[16,864,128]{2,1,0:T(8,128)}) custom-call(bf16[576,6144]{1,0:T(8,128)(2,1)} %get-tuple-element.84.refs_0_, bf16[576,3072]{1,0:T(8,128)(2,1)} %reshape.42.w_ref.refs_1_, f32[8,6144]{1,0:T(8,128)} %maximum_maximum_fusion.1.tok_ref.refs_2_, f32[8,6144]{1,0:T(8,128)} %exchange_stats.3.refs_3_, ...), custom_call_target="tpu_custom_call" | custom-call | flops 43486543872 | bytes 75497472 | tf_op jit(solution)/shard_map/head_pass2/pallas_call | solution.py:351
  546.5 57.9 %cube_reduce_scatter.2.refs_4_ = f32[1728,128]{1,0:T(8,128)} custom-call(f32[2,2,2,2,1728,128]{5,4,3,2,1,0:T(8,128)} %bitcast.56), custom_call_target="tpu_custom_call" | custom-call | flops 49999998976 | bytes 1048576 | tf_op jit(solution)/shard_map/cube_reduce_scatter/pallas_call | solution.py:593
  604.4 35.6 %block_backward.5 = (f32[1024,576]{1,0:T(8,128)}, f32[16,2592,128]{2,1,0:T(8,128)}, f32[16,864,128]{2,1,0:T(8,128)}) custom-call(bf16[1024,576]{1,0:T(8,128)(2,1)} %bitcast.45, bf16[16,1,1296,128]{3,2,1,0:T(8,128)(2,1)} %bitcast.54, bf16[1024,576]{1,0:T(8,128)(2,1)} %get-tuple-element.81.refs_2_, f32[2880,128]{1,0:T(8,128)} %bitcast.55, ...), custom_call_target="tpu_custom_call" | custom-call | flops 14495514624 | bytes 25165824 | tf_op jit(solution)/shard_map/block_backward/pallas_call | solution.py:480
  639.9 34.9 %block_backward.6 = (f32[1024,576]{1,0:T(8,128)}, f32[16,2592,128]{2,1,0:T(8,128)}, f32[16,864,128]{2,1,0:T(8,128)}) custom-call(bf16[1024,576]{1,0:T(8,128)(2,1)} %bitcast.42, bf16[16,4,1296,128]{3,2,1,0:T(8,128)(2,1)} %bitcast.35, f32[1024,576]{1,0:T(8,128)} %get-tuple-element.94.refs_2_, ...), custom_call_target="tpu_custom_call", output_to_operand_aliasing={{1}: (3, {}), {2}: (5, {})} | custom-call | flops 14495514624 | bytes 25165824 | tf_op jit(solution)/shard_map/block_backward/pallas_call | solution.py:480
  674.9 1.7 slice_reduce_fusion
  676.5 1.6 slice_reduce_fusion.2
  679.4 31.7 %block_backward.7 = (f32[1024,576]{1,0:T(8,128)}, f32[16,3888,128]{2,1,0:T(8,128)}, f32[16,864,128]{2,1,0:T(8,128)}) custom-call(bf16[1024,576]{1,0:T(8,128)(2,1)} %bitcast.46, bf16[16,4,1296,128]{3,2,1,0:T(8,128)(2,1)} %bitcast.36, f32[1024,576]{1,0:T(8,128)} %get-tuple-element.101.refs_2_, ...), custom_call_target="tpu_custom_call", output_to_operand_aliasing={{2}: (4, {})} | custom-call | flops 14495514624 | bytes 25165824 | tf_op jit(solution)/shard_map/block_backward/pallas_call | solution.py:480
  711.1 28.0 %block_backward.8 = (f32[1024,576]{1,0:T(8,128)}, f32[16,3888,128]{2,1,0:T(8,128)}, f32[16,864,128]{2,1,0:T(8,128)}) custom-call(bf16[1024,576]{1,0:T(8,128)(2,1)} %bitcast.41, bf16[16,4,1296,128]{3,2,1,0:T(8,128)(2,1)} %bitcast.37, f32[1024,576]{1,0:T(8,128)} %get-tuple-element.103.refs_2_, ...), custom_call_target="tpu_custom_call", output_to_operand_aliasing={{1}: (3, {}), {2}: (5, {})} | custom-call | flops 14495514624 | bytes 25165824 | tf_op jit(solution)/shard_map/block_backward/pallas_call | solution.py:480
  739.2 30.6 %block_backward.9 = (bf16[1024,576]{1,0:T(8,128)(2,1)}, f32[16,3888,128]{2,1,0:T(8,128)}, f32[16,864,128]{2,1,0:T(8,128)}) custom-call(bf16[1024,576]{1,0:T(8,128)(2,1)} %bitcast.40, bf16[16,4,1296,128]{3,2,1,0:T(8,128)(2,1)} %bitcast.38, f32[1024,576]{1,0:T(8,128)} %get-tuple-element.106.refs_2_, ...), custom_call_target="tpu_custom_call", output_to_operand_aliasing={{1}: (3, {}), {2}: (5, {})} | custom-call | flops 14495514624 | bytes 25165824 | tf_op jit(solution)/shard_map/block_backward/pallas_call | solution.py:480
  769.8 11.5 %unpack_head.1 = f32[36,49152]{1,0:T(8,128)} custom-call(f32[16,864,128]{2,1,0:T(8,128)} %get-tuple-element.110.p_ref), custom_call_target="tpu_custom_call" | custom-call | tf_op jit(solution)/shard_map/unpack_head/pallas_call | solution.py:500
  782.7 127.4 %cube_reduce_scatter.3.p_ref = f32[3888,128]{1,0:T(8,128)} custom-call(f32[2,2,2,2,3888,128]{5,4,3,2,1,0:T(8,128)} %bitcast.39), custom_call_target="tpu_custom_call" | custom-call | flops 49999998976 | bytes 1048576 | tf_op jit(solution)/shard_map/cube_reduce_scatter/pallas_call | solution.py:593
  910.2 2.2 unpack_grads.2
  912.4 3.7 unpack_grads.3
  (46 shorter events, 9.8 us)
Async XLA Ops:
  7.2 93.1 %all-gather.11.cloned.1.call-start = ((), (), s32[]{:S(2)}) async-start(), calls=%async_computation.6 | async-start | bytes 5640192 | tf_op jit(solution)/shard_map/all_gather | solution.py:692
  15.6 161.1 %all-gather.7.cloned.1.call-start = ((), (), s32[]{:S(2)}) async-start(), calls=%async_computation.2 | async-start | bytes 12533760 | tf_op jit(solution)/shard_map/all_gather | solution.py:703
  100.3 13.0 %copy-start = (bf16[5,1296,128]{2,1,0:T(8,128)(2,1)S(1)}, bf16[5,1296,128]{2,1,0:T(8,128)(2,1)}, u32[]{:S(2)}) copy-start(bf16[5,1296,128]{2,1,0:T(8,128)(2,1)} %pack_weights.1) | copy-start | bytes 4976644
  113.2 281.4 %all-gather.13.cloned.1.call-start = ((), (), s32[]{:S(2)}) async-start(), calls=%async_computation.7 | async-start | bytes 22560768 | tf_op jit(solution)/shard_map/all_gather | solution.py:704
  114.5 5.1 copy-start.2
  114.5 280.2 %all-gather.9.cloned.1.call-start = ((), (), s32[]{:S(2)}) async-start(), calls=%async_computation.3 | async-start | bytes 7520256 | tf_op jit(solution)/shard_map/all_gather | solution.py:703
  117.0 3.9 copy-start.1
  126.2 420.3 %reduce-scatter.3.cloned.1.call-start = ((), (), s32[]{:S(2)}) async-start(), calls=%async_computation.4 | async-start | bytes 25067520 | tf_op jit(solution)/shard_map/reduce_scatter | solution.py:724
  393.0 517.2 %reduce-scatter.5.cloned.1.call-start = ((), (), s32[]{:S(2)}) async-start(), calls=%async_computation.5 | async-start | bytes 22560768 | tf_op jit(solution)/shard_map/reduce_scatter | solution.py:737
  769.8 11.5 %copy-start.3 = (bf16[1024,576]{1,0:T(8,128)(2,1)S(1)}, bf16[1024,576]{1,0:T(8,128)(2,1)}, u32[]{:S(2)}) copy-start(bf16[1024,576]{1,0:T(8,128)(2,1)} %get-tuple-element.138) | copy-start | bytes 3538948
Sparse Core Ops, SparseCore 0:
  15.7 84.5 all-gather.10
  113.4 63.2 all-gather.6
  178.9 97.4 all-gather.12
  278.5 44.6 all-gather.8
  393.1 136.9 reduce-scatter.2
  675.0 161.5 reduce-scatter.4
